TPU v7x, 256 devices: a whole 4x4x8 slice. The times are simulated.
256 devices in a mesh: segment: 8 (over y, core), row: 32 (over z, x).
Axes of the slice: x: 4, y: 4, z: 8, core: 2. Of those that a mesh axis runs over, the one named last changes fastest.
Arguments:
- snapshots: float32 [8192, 1024], P('row', 'segment'), may hold values from -6 to 6
- basis: float32 [8192, 4096], P('row', 'segment'), may hold values from -0.0625 to 0.0625
Outputs:
- residual: float32 [8192, 1024], P('row', 'segment')
- coefficients: float32 [4096, 1024], P('segment')
- residual_rms: float32 [1024], P('segment')
All inputs are finite; a program needn't handle non-finite values.
Results may differ from a plain program's by a relative error of at most 0.0001.
Values sent between devices are 32-bit elements; how exact they have to be, the bound alone decides.
No kernel may reach another device: no remote copies, remote signals or barrier semaphores. Data moves between devices by JAX's collectives and lax.ppermute only.
A program may use at most 64 MiB of HBM per device.

v0:
```python
import jax
import jax.numpy as jnp
from jax import lax
from jax.sharding import PartitionSpec as P

TICKS = 2


def rows_for(lines, length):
    spare = -len(lines) % length
    return jnp.pad(lines, [(0, spare)] + [(0, 0)] * (lines.ndim - 1))


def copy_for_each(shard, axis):
    copies = jnp.broadcast_to(shard, (lax.axis_size(axis), *shard.shape))
    return lax.all_to_all(copies, axis, split_axis=0, concat_axis=0, tiled=True)


def in_order(parts, dim):
    shape = list(parts.shape[1:])
    shape[dim] *= parts.shape[0]
    return jnp.moveaxis(parts, 0, dim).reshape(shape)


def collect(shard, axis, dim):
    parts = copy_for_each(shard, axis)
    return in_order(parts, dim)


def in_blocks(shard, dim, length):
    before, after = (shard.shape[:dim], shard.shape[dim + 1 :])
    return jnp.moveaxis(shard.reshape(*before, length, -1, *after), dim, 0)


def sum_at_owner(shard, axis, dim):
    parts = in_blocks(shard, dim, lax.axis_size(axis))
    arrived = lax.all_to_all(parts, axis, split_axis=0, concat_axis=0, tiled=True)
    return arrived.sum(axis=0)


def nested_sum(shard, axes):
    lines = shard.reshape(-1, shard.shape[-1])
    padded = rows_for(lines, lax.axis_size(axes))
    whole = collect(sum_at_owner(padded, axes, 0), axes, 0)
    return lax.slice_in_dim(whole, 0, len(lines)).reshape(shard.shape)


def shifted(value, axis, steps):
    count = lax.axis_size(axis)
    pairs = [(source, (source + steps) % count) for source in range(count)]
    return lax.ppermute(value, axis, pairs)


def of_everyone(shard, axis):
    return copy_for_each(shard, axis).sum(axis=0)


def per_device(snapshots, basis):
    high = lax.Precision.HIGHEST
    sections = lax.axis_size("segment")
    position = lax.axis_index("segment")
    width = snapshots.shape[1]
    total_rows = basis.shape[0] * lax.axis_size("row")
    coeff = jnp.zeros((basis.shape[1], width * sections), jnp.float32)
    vec = snapshots
    for step in range(TICKS):
        visit_vec = vec
        visit_coeff = coeff
        owner = (position - step) % sections
        first = nested_sum(
            jnp.dot(basis.T, visit_vec, precision=high, preferred_element_type=jnp.float32), "row"
        )
        moved = visit_vec - jnp.dot(
            basis, first, precision=high, preferred_element_type=jnp.float32
        )
        second = nested_sum(
            jnp.dot(basis.T, moved, precision=high, preferred_element_type=jnp.float32), "row"
        )
        visit_vec = moved - jnp.dot(
            basis, second, precision=high, preferred_element_type=jnp.float32
        )
        visit_coeff = lax.dynamic_update_slice(
            visit_coeff, first + second, (jnp.int32(0), owner * width)
        )
        vec = visit_vec
        coeff = visit_coeff
        if step + 1 < TICKS:
            vec = shifted(vec, "segment", 1)
    vec = shifted(vec, "segment", 1 - TICKS)
    sums = of_everyone(jnp.sum(vec * vec, axis=0), "row")
    rms = jnp.sqrt(sums / total_rows)
    return (vec, coeff, rms)


def solution(mesh):
    placed = (P("row", "segment"), P("row", "segment"))
    return jax.shard_map(
        per_device,
        mesh=mesh,
        in_specs=placed,
        out_specs=(P("row", "segment"), P("segment", None), P("segment")),
        check_vma=False,
    )
```

profile of v0, /device:TPU:8, one launch (start us, length us, event | category | flops | bytes accessed | tf_op | source)
XLA Modules:
  0.0 164.2 jit_solution(8683577590723400725)
XLA Ops:
  0.6 0.0 copy-start
  0.6 0.0 copy-start.2
  0.7 1.0 copy-done
  1.7 1.9 %fusion.4 = f32[512,128]{1,0:T(8,128)S(1)} fusion(f32[256,512]{1,0:T(8,128)S(1)} %copy-done, f32[256,128]{1,0:T(8,128)} %param.2), kind=kOutput, calls=%fused_computation.15 | convolution fusion | flops 201326592 | bytes 917504 | tf_op jit(solution)/shard_map/dot_general | solution.py:71
  3.6 23.9 %all_to_all.46 = f32[32,16,128]{2,1,0:T(8,128)S(1)} all-to-all(f32[32,16,128]{2,1,0:T(8,128)S(1)} %bitcast.55), channel_id=1, replica_groups=mesh['segment'=8,'row'=32] {'row'}, dimensions={0} | all-to-all | bytes 524288 | tf_op jit(solution)/shard_map/all_to_all | solution.py:37
  27.5 0.7 broadcast_in_dim.18
  28.3 4.0 %all-to-all-start.1 = ((f32[32,16,128]{2,1,0:T(8,128)}), f32[32,16,128]{2,1,0:T(8,128)S(1)}, u32[]{:S(2)}, u32[]{:S(2)}) async-start(f32[32,16,128]{2,1,0:T(8,128)} %broadcast_in_dim.18), calls=%async_computation.1 | async-start | bytes 524288 | tf_op jit(solution)/shard_map/all_to_all | solution.py:16
  32.2 0.0 copy-done.2
  32.3 0.1 copy.17
  32.4 12.3 %all-to-all-done.1 = f32[32,16,128]{2,1,0:T(8,128)S(1)} async-done(((f32[32,16,128]{2,1,0:T(8,128)}), f32[32,16,128]{2,1,0:T(8,128)S(1)}, u32[]{:S(2)}, u32[]{:S(2)}) %all-to-all-start.1) | async-done | bytes 262176 | tf_op jit(solution)/shard_map/all_to_all | solution.py:16
  44.7 0.6 fusion.3
  45.3 0.4 convolution_bitcast_fusion.2
  45.7 0.1 copy.18
  45.8 15.3 %all_to_all.47 = f32[32,16,128]{2,1,0:T(8,128)S(1)} all-to-all(f32[32,16,128]{2,1,0:T(8,128)S(1)} %bitcast.56), channel_id=1, replica_groups=mesh['segment'=8,'row'=32] {'row'}, dimensions={0} | all-to-all | bytes 524288 | tf_op jit(solution)/shard_map/all_to_all | solution.py:37
  61.2 14.9 %all_to_all.48 = f32[32,16,128]{2,1,0:T(8,128)S(1)} all-to-all(f32[32,16,128]{2,1,0:T(8,128)S(1)} %broadcast_in_dim.19), channel_id=1, replica_groups=mesh['segment'=8,'row'=32] {'row'}, dimensions={0} | all-to-all | bytes 524288 | tf_op jit(solution)/shard_map/all_to_all | solution.py:16
  76.1 0.6 fusion.2
  76.7 0.0 collective-permute-start
  76.7 4.4 %collective-permute-done = f32[256,128]{0,1:T(8,128)S(1)} collective-permute-done((f32[256,128]{0,1:T(8,128)S(1)}, f32[256,128]{0,1:T(8,128)S(1)}, u32[]{:S(2)}, u32[]{:S(2)}) %collective-permute-start) | collective-permute-done | bytes 131104 | tf_op jit(solution)/shard_map/ppermute | solution.py:51
  81.1 0.4 convolution_bitcast_fusion.1
  81.6 0.1 copy.19
  81.7 16.0 %all_to_all.49 = f32[32,16,128]{2,1,0:T(8,128)S(1)} all-to-all(f32[32,16,128]{2,1,0:T(8,128)S(1)} %bitcast.57), channel_id=1, replica_groups=mesh['segment'=8,'row'=32] {'row'}, dimensions={0} | all-to-all | bytes 524288 | tf_op jit(solution)/shard_map/all_to_all | solution.py:37
  97.7 15.8 %all_to_all.50 = f32[32,16,128]{2,1,0:T(8,128)S(1)} all-to-all(f32[32,16,128]{2,1,0:T(8,128)S(1)} %broadcast_in_dim.20), channel_id=1, replica_groups=mesh['segment'=8,'row'=32] {'row'}, dimensions={0} | all-to-all | bytes 524288 | tf_op jit(solution)/shard_map/all_to_all | solution.py:16
  113.6 0.6 fusion.1
  114.2 0.4 convolution_bitcast_fusion
  114.6 0.1 copy.20
  114.7 15.2 %all_to_all.51 = f32[32,16,128]{2,1,0:T(8,128)S(1)} all-to-all(f32[32,16,128]{2,1,0:T(8,128)S(1)} %bitcast.58), channel_id=1, replica_groups=mesh['segment'=8,'row'=32] {'row'}, dimensions={0} | all-to-all | bytes 524288 | tf_op jit(solution)/shard_map/all_to_all | solution.py:37
  130.0 0.7 broadcast_in_dim.21
  130.7 3.9 %all-to-all-start.7 = ((f32[32,16,128]{2,1,0:T(8,128)}), f32[32,16,128]{2,1,0:T(8,128)S(1)}, u32[]{:S(2)}, u32[]{:S(2)}) async-start(f32[32,16,128]{2,1,0:T(8,128)} %broadcast_in_dim.21), calls=%async_computation.7 | async-start | bytes 524288 | tf_op jit(solution)/shard_map/all_to_all | solution.py:16
  134.6 11.7 %all-to-all-done.7 = f32[32,16,128]{2,1,0:T(8,128)S(1)} async-done(((f32[32,16,128]{2,1,0:T(8,128)}), f32[32,16,128]{2,1,0:T(8,128)S(1)}, u32[]{:S(2)}, u32[]{:S(2)}) %all-to-all-start.7) | async-done | bytes 262176 | tf_op jit(solution)/shard_map/all_to_all | solution.py:16
  146.3 0.6 fusion
  146.9 0.0 collective-permute-start.1
  146.9 0.2 broadcast_in_dim.22
  147.2 0.0 copy-start.1
  147.2 1.3 copy-done.1
  148.5 0.9 collective-permute-done.1
  149.4 0.1 multiply_reduce_fusion
  149.5 0.6 broadcast_in_dim.23
  150.1 3.9 %all-to-all-start.8 = ((f32[32,1,128]{2,1,0:T(1,128)}), f32[32,1,128]{2,1,0:T(1,128)S(1)}, u32[]{:S(2)}, u32[]{:S(2)}) async-start(f32[32,1,128]{2,1,0:T(1,128)} %broadcast_in_dim.23), calls=%async_computation.8 | async-start | bytes 32768 | tf_op jit(solution)/shard_map/all_to_all | solution.py:16
  154.0 0.7 add_dynamic-update-slice_fusion
  154.7 0.8 copy.22
  155.5 8.1 %all-to-all-done.8 = f32[32,1,128]{2,1,0:T(1,128)S(1)} async-done(((f32[32,1,128]{2,1,0:T(1,128)}), f32[32,1,128]{2,1,0:T(1,128)S(1)}, u32[]{:S(2)}, u32[]{:S(2)}) %all-to-all-start.8) | async-done | bytes 16416 | tf_op jit(solution)/shard_map/all_to_all | solution.py:16
  163.6 0.5 multiply_sqrt_fusion
  (8 shorter events, 0.2 us)
Async XLA Ops:
  0.6 1.0 copy-start
  0.6 31.6 %copy-start.2 = (f32[256,128]{1,0:T(8,128)S(1)}, f32[256,128]{1,0:T(8,128)}, u32[]{:S(2)}) copy-start(f32[256,128]{1,0:T(8,128)} %param.2) | copy-start | bytes 393220
  28.3 16.4 %all-to-all-start.1 = ((f32[32,16,128]{2,1,0:T(8,128)}), f32[32,16,128]{2,1,0:T(8,128)S(1)}, u32[]{:S(2)}, u32[]{:S(2)}) async-start(f32[32,16,128]{2,1,0:T(8,128)} %broadcast_in_dim.18), calls=%async_computation.1 | async-start | bytes 524288 | tf_op jit(solution)/shard_map/all_to_all | solution.py:16
  76.7 4.4 %collective-permute-start = (f32[256,128]{0,1:T(8,128)S(1)}, f32[256,128]{0,1:T(8,128)S(1)}, u32[]{:S(2)}, u32[]{:S(2)}) collective-permute-start(f32[256,128]{0,1:T(8,128)S(1)} %fusion.2), channel_id=1, source_target_pairs={{0,32},{32,64},{64,96},{96,128},{128,160},{160,192},{192,224},{224... | collective-permute-start | bytes 393224 | tf_op jit(solution)/shard_map/ppermute | solution.py:51
  130.7 15.6 %all-to-all-start.7 = ((f32[32,16,128]{2,1,0:T(8,128)}), f32[32,16,128]{2,1,0:T(8,128)S(1)}, u32[]{:S(2)}, u32[]{:S(2)}) async-start(f32[32,16,128]{2,1,0:T(8,128)} %broadcast_in_dim.21), calls=%async_computation.7 | async-start | bytes 524288 | tf_op jit(solution)/shard_map/all_to_all | solution.py:16
  146.9 2.5 %collective-permute-start.1 = (f32[256,128]{0,1:T(8,128)S(1)}, f32[256,128]{0,1:T(8,128)S(1)}, u32[]{:S(2)}, u32[]{:S(2)}) collective-permute-start(f32[256,128]{0,1:T(8,128)S(1)} %fusion), channel_id=1, source_target_pairs={{0,224},{32,0},{64,32},{96,64},{128,96},{160,128},{192,160},{224,1... | collective-permute-start | bytes 393224 | tf_op jit(solution)/shard_map/ppermute | solution.py:51
  147.2 1.3 copy-start.1
  150.1 13.5 %all-to-all-start.8 = ((f32[32,1,128]{2,1,0:T(1,128)}), f32[32,1,128]{2,1,0:T(1,128)S(1)}, u32[]{:S(2)}, u32[]{:S(2)}) async-start(f32[32,1,128]{2,1,0:T(1,128)} %broadcast_in_dim.23), calls=%async_computation.8 | async-start | bytes 32768 | tf_op jit(solution)/shard_map/all_to_all | solution.py:16
where the time goes:
time: 167 us; the launch traced here: 164 us
  blocking collectives  101 us (60%)
  waiting for transfers between devices  37.4 us (22%)
  starting transfers between devices  11.7 us (7%)
  local copies, waits for them, and re-layouts  5.9 us (4%)
  matrix products  5.52 us (3%)
    all_to_all x4, blocking collectives, sum_at_owner(): lax.all_to_all(parts, axis, split_axis=0, concat_axis=0, tiled=True)  70.4 us
    all_to_all x3, waiting for transfers between devices, copy_for_each(): return lax.all_to_all(copies, axis, split_axis=0, concat_axis=0, tiled=True)  32.1 us
    all_to_all x2, blocking collectives, copy_for_each(): return lax.all_to_all(copies, axis, split_axis=0, concat_axis=0, tiled=True)  30.8 us
    all_to_all x3, starting transfers between devices, copy_for_each(): return lax.all_to_all(copies, axis, split_axis=0, concat_axis=0, tiled=True)  11.7 us
    ppermute x2, waiting for transfers between devices, shifted(): return lax.ppermute(value, axis, pairs)  5.28 us
  transfers between devices with their start and end apart: 5, of which 5 were waited for; matrix products, arithmetic and copies ran while one was open for 1% of the time, Pallas kernels for 0%

commit v1 on v0

v1 whole, which is shorter than its diff:
```python
import jax
import jax.numpy as jnp
from jax import lax
from jax.sharding import PartitionSpec as P

TILE = 128


def exchange(blocks, axis):
    return lax.all_to_all(blocks, axis, split_axis=0, concat_axis=0, tiled=True)


def summed(blocks, axis):
    own = exchange(blocks, axis).sum(axis=0)
    return exchange(jnp.broadcast_to(own, blocks.shape), axis)


def shifted(value, axis, steps):
    count = lax.axis_size(axis)
    pairs = [(source, (source + steps) % count) for source in range(count)]
    return lax.ppermute(value, axis, pairs)


def dot(a, b, over):
    return lax.dot_general(
        a, b, ((over[0], over[1]), ((), ())), precision=lax.Precision.HIGH,
        preferred_element_type=jnp.float32,
    )


def upper(basis):
    tiles = basis.shape[1] // TILE
    rows = []
    for i in range(tiles):
        strip = dot(basis[:, i * TILE:(i + 1) * TILE], basis[:, i * TILE:], ((0,), (0,)))
        rows += [strip[:, j * TILE:(j + 1) * TILE] for j in range(tiles - i)]
    return jnp.concatenate(rows, 0)


def whole(packed, tiles):
    part, at = {}, 0
    for i in range(tiles):
        for j in range(i, tiles):
            tile = packed[at * TILE:(at + 1) * TILE]
            part[i, j] = tile
            if i != j:
                part[j, i] = tile.T
            at += 1
    return jnp.concatenate(
        [jnp.concatenate([part[i, j] for j in range(tiles)], 1) for i in range(tiles)], 0
    )


def both(first, gram):
    return 2.0 * first - dot(gram, first, ((1,), (0,)))


def per_device(snapshots, basis):
    sections = lax.axis_size("segment")
    lines = lax.axis_size("row")
    position = lax.axis_index("segment")
    width = snapshots.shape[1]
    size = basis.shape[1]
    tiles = size // TILE
    total_rows = basis.shape[0] * lines
    onward = shifted(basis, "segment", -1)

    first = dot(basis, snapshots, ((0,), (0,)))
    gram = upper(basis)
    share = len(gram) // lines
    sent = jnp.concatenate(
        [gram.reshape(lines, -1, TILE), first.reshape(lines, -1, TILE)], 1
    )
    got = summed(sent, "row")
    got_next = shifted(got, "segment", -1)
    first = got[:, share:].reshape(size, width)
    here = both(first, whole(got[:, :share].reshape(-1, TILE), tiles))
    vec = snapshots - dot(basis, here, ((1,), (0,)))

    first = dot(onward, vec, ((0,), (0,)))
    first = summed(first.reshape(lines, -1, width), "row").reshape(size, width)
    there = both(first, whole(got_next[:, :share].reshape(-1, TILE), tiles))
    vec = vec - dot(onward, there, ((1,), (0,)))

    arrived = shifted(there, "segment", 1)
    squares = jnp.sum(vec * vec, axis=0)
    sums = exchange(jnp.broadcast_to(squares, (lines, width)), "row").sum(axis=0)
    rms = jnp.sqrt(sums / total_rows)
    coeff = jnp.zeros((size, width * sections), jnp.float32)
    coeff = lax.dynamic_update_slice(coeff, here, (jnp.int32(0), position * width))
    before = (position - 1) % sections
    coeff = lax.dynamic_update_slice(coeff, arrived, (jnp.int32(0), before * width))
    return (vec, coeff, rms)


def solution(mesh):
    placed = (P("row", "segment"), P("row", "segment"))
    return jax.shard_map(
        per_device,
        mesh=mesh,
        in_specs=placed,
        out_specs=(P("row", "segment"), P("segment", None), P("segment")),
        check_vma=False,
    )
```

time: 167 us -> 140 us (0.84)
  blocking collectives: 101 us -> 55.6 us
  local copies, waits for them, and re-layouts: 5.9 us -> 13.6 us
  matrix products: 5.52 us -> 11.7 us
  waiting for transfers between devices: 37.4 us -> 41.4 us
  starting transfers between devices: 11.7 us -> 13.8 us
    all_to_all x6 -> x2, blocking collectives: 101 us -> 55.6 us  [exchange(): return lax.all_to_all(blocks, axis, split_axis=0, concat_axis=0, tiled=True)]
    all_to_all x3, waiting for transfers between devices: 32.1 us -> 41.4 us  [exchange(): return lax.all_to_all(blocks, axis, split_axis=0, concat_axis=0, tiled=True)]
    dot_general x8 -> x10, matrix products: 5.52 us -> 11.7 us  [dot(): lax.dot_general(a, b, ((over[0], over[1]), ((), ())), precision=lax.Preci...]
    ppermute x2 -> x3, waiting for transfers between devices: 5.28 us -> 0.01 us  [shifted(): return lax.ppermute(value, axis, pairs)]
    slice x0 -> x5, local copies, waits for them, and re-layouts: none -> 2.69 us  [the longest x2 1.49 us: whole(): tile = packed[at * TILE:(at + 1) * TILE]]
    transpose x0 -> x6, local copies, waits for them, and re-layouts: none -> 2.43 us  [whole(): part[j, i] = tile.T]
    all_to_all x3, starting transfers between devices: 11.7 us -> 13.7 us  [exchange(): return lax.all_to_all(blocks, axis, split_axis=0, concat_axis=0, tiled=True)]
    unnamed x8 -> x45, local copies, waits for them, and re-layouts: 3.2 us -> 4.82 us
  transfers between devices with their start and end apart: 5 -> 6, of which waited for: 5 -> 3; matrix products, arithmetic and copies ran while one was open for 1% -> 11% of each run, Pallas kernels for 0% -> 0%
where the time goes in v1:
time: 140 us; the launch traced here: 138 us
  blocking collectives  55.6 us (40%)
  waiting for transfers between devices  41.4 us (30%)
  starting transfers between devices  13.8 us (10%)
  local copies, waits for them, and re-layouts  13.6 us (10%)
  matrix products  11.7 us (8%)
    all_to_all x2, blocking collectives, exchange(): return lax.all_to_all(blocks, axis, split_axis=0, concat_axis=0, tiled=True)  55.6 us
    all_to_all x3, waiting for transfers between devices, exchange(): return lax.all_to_all(blocks, axis, split_axis=0, concat_axis=0, tiled=True)  41.4 us
    all_to_all x3, starting transfers between devices, exchange(): return lax.all_to_all(blocks, axis, split_axis=0, concat_axis=0, tiled=True)  13.7 us
    dot_general x10, matrix products, dot(): lax.dot_general(a, b, ((over[0], over[1]), ((), ())), precision=lax.Preci...  11.7 us
    unnamed x45, local copies, waits for them, and re-layouts  4.82 us
  transfers between devices with their start and end apart: 6, of which 3 were waited for; matrix products, arithmetic and copies ran while one was open for 11% of the time, Pallas kernels for 0%

profile of v1, /device:TPU:8, one launch (start us, length us, event | category | flops | bytes accessed | tf_op | source)
XLA Modules:
  0.0 137.9 jit_solution(12704134624860796696)
XLA Ops:
  0.7 1.5 %fusion.59 = f32[128,512]{1,0:T(8,128)S(1)} fusion(f32[256,512]{1,0:T(8,128)} %param.3), kind=kOutput, calls=%fused_computation.69 | convolution fusion | flops 100663296 | bytes 917504 | tf_op jit(solution)/shard_map/dot_general | solution.py:25
  2.1 1.4 %fusion.52 = f32[128,384]{1,0:T(8,128)S(1)} fusion(f32[256,512]{1,0:T(8,128)} %param.3), kind=kOutput, calls=%fused_computation.59 | convolution fusion | flops 75497472 | bytes 720896 | tf_op jit(solution)/shard_map/dot_general | solution.py:25
  3.6 1.3 fusion.54
  5.0 0.3 convolution_dynamic-update-slice_fusion
  5.3 0.6 fusion.65
  6.0 0.1 pad_maximum_fusion
  6.0 36.7 %all_to_all.26 = f32[32,56,128]{2,1,0:T(8,128)S(1)} all-to-all(f32[32,56,128]{2,1,0:T(8,128)S(1)} %pad_maximum_fusion), channel_id=1, replica_groups=mesh['segment'=8,'row'=32] {'row'}, dimensions={0} | all-to-all | bytes 1835008 | tf_op jit(solution)/shard_map/all_to_all | solution.py:10
  42.7 0.1 reduce_sum.36
  42.8 1.0 broadcast_in_dim.12
  43.7 5.3 %all-to-all-start.1 = ((f32[32,56,128]{2,1,0:T(8,128)}), f32[32,56,128]{2,1,0:T(8,128)S(1)}, u32[]{:S(2)}, u32[]{:S(2)}) async-start(f32[32,56,128]{2,1,0:T(8,128)} %broadcast_in_dim.12), calls=%async_computation.1 | async-start | bytes 1835008 | tf_op jit(solution)/shard_map/all_to_all | solution.py:10
  49.1 0.8 copy.62
  49.8 23.3 %all-to-all-done.1 = f32[32,56,128]{2,1,0:T(8,128)S(1)} async-done(((f32[32,56,128]{2,1,0:T(8,128)}), f32[32,56,128]{2,1,0:T(8,128)S(1)}, u32[]{:S(2)}, u32[]{:S(2)}) %all-to-all-start.1) | async-done | bytes 917536 | tf_op jit(solution)/shard_map/all_to_all | solution.py:10
  73.1 0.8 fusion.64
  73.9 0.1 copy.74
  74.0 0.1 copy.75
  74.1 0.1 copy.73
  74.2 0.8 copy.61
  75.1 0.7 copy.58
  75.8 0.7 copy.59
  76.5 0.7 copy.60
  77.3 0.2 broadcast_in_dim.14
  77.6 0.6 copy-done.6
  78.3 1.6 %constant_dynamic-update-slice_fusion.1 = (f32[512,1024]{1,0:T(8,128)S(1)}, f32[512,128]{1,0:T(8,128)S(1)}) fusion(f32[512,1024]{1,0:T(8,128)S(1)} %broadcast_in_dim.14, s32[]{:T(128)S(6)} %select_n.13, f32[512,128]{1,0:T(8,128)S(1)} %bitcast.54, f32[128,128]{1,0:T(8,128)} %get-tuple-element.38, f32[128,128]{1,0:T(8,128)S(1)} %copy-done.13, ...), kind=kOutput, calls=%fused_computation.82 | convolution fusion | flops 204603392 | bytes 2097156 | tf_op jit(solution)/shard_map/dot_general | solution.py:25
  80.0 0.4 fusion.1
  80.4 0.6 copy-done.2
  81.0 1.3 convolution_bitcast_fusion
  82.3 0.1 copy.63
  82.5 18.9 %all_to_all.27 = f32[32,16,128]{2,1,0:T(8,128)S(1)} all-to-all(f32[32,16,128]{2,1,0:T(8,128)S(1)} %bitcast.52), channel_id=1, replica_groups=mesh['segment'=8,'row'=32] {'row'}, dimensions={0} | all-to-all | bytes 524288 | tf_op jit(solution)/shard_map/all_to_all | solution.py:10
  101.4 0.7 broadcast_in_dim.13
  102.2 4.6 %all-to-all-start.3 = ((f32[32,16,128]{2,1,0:T(8,128)}), f32[32,16,128]{2,1,0:T(8,128)}, u32[]{:S(2)}, u32[]{:S(2)}) async-start(f32[32,16,128]{2,1,0:T(8,128)} %broadcast_in_dim.13), calls=%async_computation.3 | async-start | bytes 524288 | tf_op jit(solution)/shard_map/all_to_all | solution.py:10
  106.8 1.1 slice.174
  107.9 0.7 fusion.63
  108.6 0.1 copy.77
  108.7 0.1 copy.78
  108.8 0.1 copy.76
  108.9 0.1 copy.70
  109.1 0.1 copy.67
  109.2 0.1 copy.68
  109.3 0.1 copy.69
  109.4 9.3 %all-to-all-done.3 = f32[32,16,128]{2,1,0:T(8,128)} async-done(((f32[32,16,128]{2,1,0:T(8,128)}), f32[32,16,128]{2,1,0:T(8,128)}, u32[]{:S(2)}, u32[]{:S(2)}) %all-to-all-start.3) | async-done | bytes 262176 | tf_op jit(solution)/shard_map/all_to_all | solution.py:10
  118.6 1.7 %convolution_subtract_fusion = f32[512,128]{1,0:T(8,128)S(1)} fusion(f32[512,128]{1,0:T(8,128)} %bitcast.13, f32[128,128]{1,0:T(8,128)S(1)} %get-tuple-element.24, f32[128,128]{1,0:T(8,128)S(1)} %copy.69, f32[128,128]{1,0:T(8,128)S(1)} %bitcast.58, f32[128,128]{1,0:T(8,128)S(1)} %copy.68, f32[128,128]{1,0:T(8,128)S(1)} %get-tuple-element.23, ...), kind=kOutput, calls=%fused_computation.1 | convolution fusion | flops 204603392 | bytes 1572864 | tf_op jit(solution)/shard_map/dot_general | solution.py:25
  120.4 1.5 %multiply_reduce_fusion = (f32[128]{0:T(128)S(1)}, f32[256,128]{0,1:T(8,128)S(1)}) fusion(f32[256,128]{0,1:T(8,128)S(1)} %copy-done.3, f32[512,128]{1,0:T(8,128)S(1)} %convolution_subtract_fusion, f32[256,512]{1,0:T(8,128)} %collective-permute-done), kind=kOutput, calls=%fused_computation.65 | convolution fusion | flops 100761472 | bytes 1049088 | tf_op jit(solution)/shard_map/dot_general | solution.py:25
  121.9 0.6 broadcast_in_dim.15
  122.5 3.8 %all-to-all-start.4 = ((f32[32,1,128]{2,1,0:T(1,128)}), f32[32,1,128]{2,1,0:T(1,128)S(1)}, u32[]{:S(2)}, u32[]{:S(2)}) async-start(f32[32,1,128]{2,1,0:T(1,128)} %broadcast_in_dim.15), calls=%async_computation.4 | async-start | bytes 32768 | tf_op jit(solution)/shard_map/all_to_all | solution.py:10
  126.3 0.8 copy.72
  127.1 8.9 %all-to-all-done.4 = f32[32,1,128]{2,1,0:T(1,128)S(1)} async-done(((f32[32,1,128]{2,1,0:T(1,128)}), f32[32,1,128]{2,1,0:T(1,128)S(1)}, u32[]{:S(2)}, u32[]{:S(2)}) %all-to-all-start.4) | async-done | bytes 16416 | tf_op jit(solution)/shard_map/all_to_all | solution.py:10
  136.0 0.5 multiply_sqrt_fusion
  136.6 1.3 copy-done.1
  (47 shorter events, 0.5 us)
Async XLA Ops:
  0.6 4.4 %copy-start = (f32[256,512]{1,0:T(8,128)S(1)}, f32[256,512]{1,0:T(8,128)}, u32[]{:S(2)}) copy-start(f32[256,512]{1,0:T(8,128)} %param.3) | copy-start | bytes 1572868
  0.6 4.7 %copy-start.4 = (f32[256,128]{1,0:T(8,128)S(1)}, f32[256,128]{1,0:T(8,128)}, u32[]{:S(2)}) copy-start(f32[256,128]{1,0:T(8,128)} %param.2) | copy-start | bytes 393220
  43.7 29.3 %all-to-all-start.1 = ((f32[32,56,128]{2,1,0:T(8,128)}), f32[32,56,128]{2,1,0:T(8,128)S(1)}, u32[]{:S(2)}, u32[]{:S(2)}) async-start(f32[32,56,128]{2,1,0:T(8,128)} %broadcast_in_dim.12), calls=%async_computation.1 | async-start | bytes 1835008 | tf_op jit(solution)/shard_map/all_to_all | solution.py:10
  49.0 31.3 %collective-permute-start = (f32[256,512]{1,0:T(8,128)S(1)}, f32[256,512]{1,0:T(8,128)}, u32[]{:S(2)}, u32[]{:S(2)}) collective-permute-start(f32[256,512]{1,0:T(8,128)S(1)} %copy-done), channel_id=1, source_target_pairs={{0,224},{32,0},{64,32},{96,64},{128,96},{160,128},{192,160},{224,1... | collective-permute-start | bytes 1572872 | tf_op jit(solution)/shard_map/ppermute | solution.py:21
  74.0 3.3 %copy-start.7 = (f32[128,128]{0,1:T(8,128)}, f32[128,128]{0,1:T(8,128)S(1)}, u32[]{:S(2)}) copy-start(f32[128,128]{0,1:T(8,128)S(1)} %copy.74) | copy-start | bytes 196612
  74.1 3.2 %copy-start.9 = (f32[128,128]{0,1:T(8,128)}, f32[128,128]{0,1:T(8,128)S(1)}, u32[]{:S(2)}) copy-start(f32[128,128]{0,1:T(8,128)S(1)} %copy.75) | copy-start | bytes 196612
  77.2 0.9 copy-start.6
  77.2 1.0 copy-start.11
  77.2 1.0 copy-start.12
  77.2 1.0 copy-start.13
  77.3 29.5 %collective-permute-start.1 = (f32[32,56,128]{2,1,0:T(8,128)S(1)}, f32[32,56,128]{2,1,0:T(8,128)}, u32[]{:S(2)}, u32[]{:S(2)}) collective-permute-start(f32[32,56,128]{2,1,0:T(8,128)S(1)} %all-to-all-done.1), channel_id=1, source_target_pairs={{0,224},{32,0},{64,32},{96,64},{128,96},{160,128},{192,160},{224,1... | collective-permute-start | bytes 2752520 | tf_op jit(solution)/shard_map/ppermute | solution.py:21
  77.3 0.9 copy-start.8
  77.3 1.0 copy-start.10
  78.3 1.7 %copy-start.5 = (f32[256,128]{0,1:T(8,128)S(1)}, f32[256,128]{0,1:T(8,128)}, u32[]{:S(2)}) copy-start(f32[256,128]{0,1:T(8,128)} %copy.62) | copy-start | bytes 393220
  80.4 0.7 copy-start.2
  102.2 16.5 %all-to-all-start.3 = ((f32[32,16,128]{2,1,0:T(8,128)}), f32[32,16,128]{2,1,0:T(8,128)}, u32[]{:S(2)}, u32[]{:S(2)}) async-start(f32[32,16,128]{2,1,0:T(8,128)} %broadcast_in_dim.13), calls=%async_computation.3 | async-start | bytes 524288 | tf_op jit(solution)/shard_map/all_to_all | solution.py:10
  118.6 1.7 %copy-start.3 = (f32[256,128]{0,1:T(8,128)S(1)}, f32[256,128]{0,1:T(8,128)}, u32[]{:S(2)}) copy-start(f32[256,128]{0,1:T(8,128)} %copy-done.2) | copy-start | bytes 393220
  120.3 16.2 %collective-permute-start.2 = (f32[512,128]{1,0:T(8,128)S(1)}, f32[512,128]{1,0:T(8,128)S(1)}, u32[]{:S(2)}, u32[]{:S(2)}) collective-permute-start(f32[512,128]{1,0:T(8,128)S(1)} %convolution_subtract_fusion), channel_id=1, source_target_pairs={{0,32},{32,64},{64,96},{96,128},{128,160},{160,192},{192,224},{224... | collective-permute-start | bytes 786440 | tf_op jit(solution)/shard_map/ppermute | solution.py:21
  122.5 13.5 %all-to-all-start.4 = ((f32[32,1,128]{2,1,0:T(1,128)}), f32[32,1,128]{2,1,0:T(1,128)S(1)}, u32[]{:S(2)}, u32[]{:S(2)}) async-start(f32[32,1,128]{2,1,0:T(1,128)} %broadcast_in_dim.15), calls=%async_computation.4 | async-start | bytes 32768 | tf_op jit(solution)/shard_map/all_to_all | solution.py:10
  136.6 1.3 copy-start.1

commit v2 on v1

--- a/solution.py
+++ b/solution.py
@@ -6,8 +6,30 @@
 TILE = 128
 
 
-def exchange(blocks, axis):
-    return lax.all_to_all(blocks, axis, split_axis=0, concat_axis=0, tiled=True)
+NEAR = 4
+
+
+def exchange(blocks, axis, groups=None):
+    return lax.all_to_all(
+        blocks, axis, split_axis=0, concat_axis=0, axis_index_groups=groups, tiled=True
+    )
+
+
+def rings(axis):
+    count = lax.axis_size(axis)
+    near = [[a + b for b in range(NEAR)] for a in range(0, count, NEAR)]
+    far = [[a + b for a in range(0, count, NEAR)] for b in range(NEAR)]
+    return near, far
+
+
+def summed_in_turn(lines, axis):
+    near, far = rings(axis)
+    blocks = exchange(lines.reshape(len(near[0]), -1, TILE), axis, near)
+    blocks = exchange(blocks.sum(axis=0).reshape(len(far[0]), -1, TILE), axis, far)
+    own = blocks.sum(axis=0)
+    blocks = exchange(jnp.broadcast_to(own, blocks.shape), axis, far).reshape(-1, TILE)
+    blocks = exchange(jnp.broadcast_to(blocks, (len(near[0]), *blocks.shape)), axis, near)
+    return blocks.reshape(-1, TILE)
 
 
 def summed(blocks, axis):
@@ -67,19 +89,16 @@
 
     first = dot(basis, snapshots, ((0,), (0,)))
     gram = upper(basis)
-    share = len(gram) // lines
-    sent = jnp.concatenate(
-        [gram.reshape(lines, -1, TILE), first.reshape(lines, -1, TILE)], 1
-    )
-    got = summed(sent, "row")
-    got_next = shifted(got, "segment", -1)
-    first = got[:, share:].reshape(size, width)
-    here = both(first, whole(got[:, :share].reshape(-1, TILE), tiles))
+    share = len(gram)
+    got = summed_in_turn(jnp.concatenate([gram, first], 0), "row")
+    got_next = shifted(got[:share], "segment", -1)
+    first = got[share:]
+    here = both(first, whole(got[:share], tiles))
     vec = snapshots - dot(basis, here, ((1,), (0,)))
 
     first = dot(onward, vec, ((0,), (0,)))
     first = summed(first.reshape(lines, -1, width), "row").reshape(size, width)
-    there = both(first, whole(got_next[:, :share].reshape(-1, TILE), tiles))
+    there = both(first, whole(got_next, tiles))
     vec = vec - dot(onward, there, ((1,), (0,)))
 
     arrived = shifted(there, "segment", 1)

time: 140 us -> 134 us (0.957)
  waiting for transfers between devices: 41.4 us -> 28.2 us
  blocking collectives: 55.6 us -> 65.4 us
  starting transfers between devices: 13.8 us -> 11.3 us
    all_to_all x3, waiting for transfers between devices: 41.4 us -> 28.2 us  [exchange(): lax.all_to_all(blocks, axis, split_axis=0, concat_axis=0, axis_index_grou...]
    all_to_all x2 -> x4, blocking collectives: 55.6 us -> 65.4 us  [exchange(): lax.all_to_all(blocks, axis, split_axis=0, concat_axis=0, axis_index_grou...]
    all_to_all x3, starting transfers between devices: 13.7 us -> 11.2 us  [exchange(): lax.all_to_all(blocks, axis, split_axis=0, concat_axis=0, axis_index_grou...]
    unnamed x45 -> x41, local copies, waits for them, and re-layouts: 4.82 us -> 4.19 us
  transfers between devices with their start and end apart: 6 -> 6, of which waited for: 3 -> 3; matrix products, arithmetic and copies ran while one was open for 11% -> 12% of each run, Pallas kernels for 0% -> 0%
where the time goes in v2:
time: 134 us; the launch traced here: 132 us
  blocking collectives  65.4 us (49%)
  waiting for transfers between devices  28.2 us (21%)
  local copies, waits for them, and re-layouts  13.9 us (10%)
  matrix products  11.5 us (9%)
  starting transfers between devices  11.3 us (8%)
    all_to_all x4, blocking collectives, exchange(): lax.all_to_all(blocks, axis, split_axis=0, concat_axis=0, axis_index_grou...  65.4 us
    all_to_all x3, waiting for transfers between devices, exchange(): lax.all_to_all(blocks, axis, split_axis=0, concat_axis=0, axis_index_grou...  28.2 us
    dot_general x10, matrix products, dot(): lax.dot_general(a, b, ((over[0], over[1]), ((), ())), precision=lax.Preci...  11.5 us
    all_to_all x3, starting transfers between devices, exchange(): lax.all_to_all(blocks, axis, split_axis=0, concat_axis=0, axis_index_grou...  11.2 us
    unnamed x41, local copies, waits for them, and re-layouts  4.19 us
    slice x2, local copies, waits for them, and re-layouts, whole(): tile = packed[at * TILE:(at + 1) * TILE]  2.69 us
  transfers between devices with their start and end apart: 6, of which 3 were waited for; matrix products, arithmetic and copies ran while one was open for 12% of the time, Pallas kernels for 0%

profile of v2, /device:TPU:8, one launch (start us, length us, event | category | flops | bytes accessed | tf_op | source)
XLA Modules:
  0.0 132.1 jit_solution(1694050259710706890)
XLA Ops:
  0.7 1.5 %fusion.60 = f32[128,512]{1,0:T(8,128)S(1)} fusion(f32[256,512]{1,0:T(8,128)} %param.3), kind=kOutput, calls=%fused_computation.70 | convolution fusion | flops 100663296 | bytes 917504 | tf_op jit(solution)/shard_map/dot_general | solution.py:47
  2.1 1.4 %fusion.52 = f32[128,384]{1,0:T(8,128)S(1)} fusion(f32[256,512]{1,0:T(8,128)} %param.3), kind=kOutput, calls=%fused_computation.59 | convolution fusion | flops 75497472 | bytes 720896 | tf_op jit(solution)/shard_map/dot_general | solution.py:47
  3.6 1.3 %fusion.55 = f32[128,256]{1,0:T(8,128)S(1)} fusion(f32[256,512]{1,0:T(8,128)} %param.3), kind=kOutput, calls=%fused_computation.64 | convolution fusion | flops 50331648 | bytes 524288 | tf_op jit(solution)/shard_map/dot_general | solution.py:47
  5.0 0.3 convolution_dynamic-update-slice_fusion.1
  5.3 0.6 convolution_dynamic-update-slice_fusion
  6.0 17.8 %all_to_all.36 = f32[4,448,128]{2,1,0:T(8,128)S(1)} all-to-all(f32[4,448,128]{2,1,0:T(8,128)S(1)} %bitcast.50), channel_id=1, replica_groups={{0,1,2,3},{4,5,6,7},{8,9,10,11},{12,13,14,15},{16,17,18,19},{20,21,22,2..., dimensions={0} | all-to-all | bytes 1835008 | tf_op jit(solution)/shard_map/all_to_all | solution.py:13
  23.8 18.4 %all_to_all.37 = f32[8,56,128]{2,1,0:T(8,128)S(1)} all-to-all(f32[8,56,128]{2,1,0:T(8,128)S(1)} %bitcast.52), channel_id=1, replica_groups={{0,4,8,12,16,20,24,28},{1,5,9,13,17,21,25,29},{2,6,10,14,18,22,26,30},{..., dimensions={0} | all-to-all | bytes 458752 | tf_op jit(solution)/shard_map/all_to_all | solution.py:13
  42.2 12.5 %all_to_all.38 = f32[8,56,128]{2,1,0:T(8,128)S(1)} all-to-all(f32[8,56,128]{2,1,0:T(8,128)S(1)} %broadcast_in_dim.15), channel_id=1, replica_groups={{0,4,8,12,16,20,24,28},{1,5,9,13,17,21,25,29},{2,6,10,14,18,22,26,30},{..., dimensions={0} | all-to-all | bytes 458752 | tf_op jit(solution)/shard_map/all_to_all | solution.py:13
  54.8 1.0 broadcast_in_dim.16
  55.7 3.5 %all-to-all-start.3 = ((f32[4,448,128]{2,1,0:T(8,128)}), f32[4,448,128]{2,1,0:T(8,128)S(1)}, u32[]{:S(2)}, u32[]{:S(2)}) async-start(f32[4,448,128]{2,1,0:T(8,128)} %broadcast_in_dim.16), calls=%async_computation.3 | async-start | bytes 1835008 | tf_op jit(solution)/shard_map/all_to_all | solution.py:13
  59.3 0.8 copy.62
  60.1 9.6 %all-to-all-done.3 = f32[4,448,128]{2,1,0:T(8,128)S(1)} async-done(((f32[4,448,128]{2,1,0:T(8,128)}), f32[4,448,128]{2,1,0:T(8,128)S(1)}, u32[]{:S(2)}, u32[]{:S(2)}) %all-to-all-start.3) | async-done | bytes 917536 | tf_op jit(solution)/shard_map/all_to_all | solution.py:13
  69.6 0.8 fusion.64
  70.4 0.9 slice.180
  71.3 0.1 copy.74
  71.4 0.1 copy.75
  71.5 0.1 copy.73
  71.6 0.8 copy.61
  72.5 0.7 copy.58
  73.2 0.7 copy.59
  74.0 0.7 copy.60
  74.8 0.2 broadcast_in_dim.18
  75.0 0.6 copy-done.4
  75.7 0.0 copy-done.8
  75.7 1.6 %constant_dynamic-update-slice_fusion.1 = (f32[512,1024]{1,0:T(8,128)S(1)}, f32[512,128]{1,0:T(8,128)S(1)}) fusion(f32[512,1024]{1,0:T(8,128)S(1)} %broadcast_in_dim.18, s32[]{:T(128)S(6)} %select_n.13, f32[1792,128]{1,0:T(8,128)S(1)} %bitcast.49, f32[128,128]{1,0:T(8,128)} %get-tuple-element.24, f32[128,128]{1,0:T(8,128)S(1)} %copy-done.11, ...), kind=kOutput, calls=%fused_computation.83 | convolution fusion | flops 204603392 | bytes 2097156 | tf_op jit(solution)/shard_map/dot_general | solution.py:47
  77.4 0.4 fusion.1
  77.8 1.3 %convolution_bitcast_fusion = f32[512,128]{0,1:T(8,128)S(1)} fusion(f32[256,128]{0,1:T(8,128)S(1)} %fusion.1, f32[256,512]{1,0:T(8,128)} %collective-permute-done), kind=kOutput, calls=%fused_computation.1 | convolution fusion | flops 100663296 | bytes 917504 | tf_op jit(solution)/shard_map/dot_general | solution.py:47
  79.1 0.1 copy.63
  79.3 16.7 %all_to_all.39 = f32[32,16,128]{2,1,0:T(8,128)S(1)} all-to-all(f32[32,16,128]{2,1,0:T(8,128)S(1)} %bitcast.51), channel_id=1, replica_groups=mesh['segment'=8,'row'=32] {'row'}, dimensions={0} | all-to-all | bytes 524288 | tf_op jit(solution)/shard_map/all_to_all | solution.py:13
  96.0 0.7 broadcast_in_dim.17
  96.7 3.9 %all-to-all-start.5 = ((f32[32,16,128]{2,1,0:T(8,128)}), f32[32,16,128]{2,1,0:T(8,128)S(1)}, u32[]{:S(2)}, u32[]{:S(2)}) async-start(f32[32,16,128]{2,1,0:T(8,128)} %broadcast_in_dim.17), calls=%async_computation.5 | async-start | bytes 524288 | tf_op jit(solution)/shard_map/all_to_all | solution.py:13
  100.6 1.9 %fusion.65 = (f32[128,128]{1,0:T(8,128)S(1)}, f32[128,128]{0,1:T(8,128)S(1)}, f32[128,128]{0,1:T(8,128)S(1)}, f32[128,128]{0,1:T(8,128)S(1)}, f32[128,128]{0,1:T...) fusion(f32[1280,128]{1,0:T(8,128)} %collective-permute-done.1), kind=kLoop, calls=%fused_computation.95 | loop fusion | bytes 1572864 | tf_op jit(solution)/shard_map/slice | solution.py:66
  102.5 0.1 copy.77
  102.6 0.1 copy.78
  102.7 0.1 copy.76
  102.8 0.1 copy.70
  103.0 0.1 copy.67
  103.1 0.1 copy.68
  103.2 0.1 copy.69
  103.3 9.7 %all-to-all-done.5 = f32[32,16,128]{2,1,0:T(8,128)S(1)} async-done(((f32[32,16,128]{2,1,0:T(8,128)}), f32[32,16,128]{2,1,0:T(8,128)S(1)}, u32[]{:S(2)}, u32[]{:S(2)}) %all-to-all-start.5) | async-done | bytes 262176 | tf_op jit(solution)/shard_map/all_to_all | solution.py:13
  112.9 1.5 %convolution_subtract_fusion = f32[512,128]{1,0:T(8,128)S(1)} fusion(f32[512,128]{1,0:T(8,128)S(1)} %bitcast.54, f32[128,128]{1,0:T(8,128)} %get-tuple-element.38, f32[128,128]{1,0:T(8,128)S(1)} %copy.69, f32[128,128]{1,0:T(8,128)S(1)} %bitcast.58, f32[128,128]{1,0:T(8,128)S(1)} %copy.68, f32[128,128]{1,0:T(8,128)} %get-tuple-element.37, ...), kind=kOutput, calls=%fused_computation.2 | convolution fusion | flops 204603392 | bytes 1572864 | tf_op jit(solution)/shard_map/dot_general | solution.py:47
  114.5 1.5 %multiply_reduce_fusion = (f32[128]{0:T(128)S(1)}, f32[256,128]{0,1:T(8,128)S(1)}) fusion(f32[256,128]{0,1:T(8,128)S(1)} %fusion.1, f32[512,128]{1,0:T(8,128)S(1)} %convolution_subtract_fusion, f32[256,512]{1,0:T(8,128)} %collective-permute-done), kind=kOutput, calls=%fused_computation.66 | convolution fusion | flops 100761472 | bytes 1049088 | tf_op jit(solution)/shard_map/dot_general | solution.py:47
  116.0 0.6 broadcast_in_dim.19
  116.6 3.8 %all-to-all-start.6 = ((f32[32,1,128]{2,1,0:T(1,128)}), f32[32,1,128]{2,1,0:T(1,128)S(1)}, u32[]{:S(2)}, u32[]{:S(2)}) async-start(f32[32,1,128]{2,1,0:T(1,128)} %broadcast_in_dim.19), calls=%async_computation.6 | async-start | bytes 32768 | tf_op jit(solution)/shard_map/all_to_all | solution.py:13
  120.5 0.8 copy.72
  121.2 8.9 %all-to-all-done.6 = f32[32,1,128]{2,1,0:T(1,128)S(1)} async-done(((f32[32,1,128]{2,1,0:T(1,128)}), f32[32,1,128]{2,1,0:T(1,128)S(1)}, u32[]{:S(2)}, u32[]{:S(2)}) %all-to-all-start.6) | async-done | bytes 16416 | tf_op jit(solution)/shard_map/all_to_all | solution.py:13
  130.2 0.5 multiply_sqrt_fusion
  130.8 1.3 copy-done.1
  (44 shorter events, 0.4 us)
Async XLA Ops:
  0.6 4.4 %copy-start = (f32[256,512]{1,0:T(8,128)S(1)}, f32[256,512]{1,0:T(8,128)}, u32[]{:S(2)}) copy-start(f32[256,512]{1,0:T(8,128)} %param.3) | copy-start | bytes 1572868
  0.6 4.7 %copy-start.2 = (f32[256,128]{1,0:T(8,128)S(1)}, f32[256,128]{1,0:T(8,128)}, u32[]{:S(2)}) copy-start(f32[256,128]{1,0:T(8,128)} %param.2) | copy-start | bytes 393220
  55.7 13.9 %all-to-all-start.3 = ((f32[4,448,128]{2,1,0:T(8,128)}), f32[4,448,128]{2,1,0:T(8,128)S(1)}, u32[]{:S(2)}, u32[]{:S(2)}) async-start(f32[4,448,128]{2,1,0:T(8,128)} %broadcast_in_dim.16), calls=%async_computation.3 | async-start | bytes 1835008 | tf_op jit(solution)/shard_map/all_to_all | solution.py:13
  59.3 18.5 %collective-permute-start = (f32[256,512]{1,0:T(8,128)S(1)}, f32[256,512]{1,0:T(8,128)}, u32[]{:S(2)}, u32[]{:S(2)}) collective-permute-start(f32[256,512]{1,0:T(8,128)S(1)} %copy-done), channel_id=1, source_target_pairs={{0,224},{32,0},{64,32},{96,64},{128,96},{160,128},{192,160},{224,1... | collective-permute-start | bytes 1572872 | tf_op jit(solution)/shard_map/ppermute | solution.py:43
  71.4 3.3 %copy-start.5 = (f32[128,128]{0,1:T(8,128)}, f32[128,128]{0,1:T(8,128)S(1)}, u32[]{:S(2)}) copy-start(f32[128,128]{0,1:T(8,128)S(1)} %copy.74) | copy-start | bytes 196612
  71.5 3.2 %copy-start.7 = (f32[128,128]{0,1:T(8,128)}, f32[128,128]{0,1:T(8,128)S(1)}, u32[]{:S(2)}) copy-start(f32[128,128]{0,1:T(8,128)S(1)} %copy.75) | copy-start | bytes 196612
  74.7 0.9 copy-start.4
  74.7 1.0 copy-start.9
  74.7 1.0 copy-start.10
  74.7 1.0 copy-start.11
  74.7 25.9 %collective-permute-start.1 = (f32[1280,128]{1,0:T(8,128)}, f32[1280,128]{1,0:T(8,128)}, u32[]{:S(2)}, u32[]{:S(2)}) collective-permute-start(f32[1280,128]{1,0:T(8,128)} %slice.180), channel_id=1, source_target_pairs={{0,224},{32,0},{64,32},{96,64},{128,96},{160,128},{192,160},{224,1... | collective-permute-start | bytes 1966088 | tf_op jit(solution)/shard_map/ppermute | solution.py:43
  74.7 1.0 copy-start.6
  74.7 1.0 copy-start.8
  75.7 1.7 %copy-start.3 = (f32[256,128]{0,1:T(8,128)S(1)}, f32[256,128]{0,1:T(8,128)}, u32[]{:S(2)}) copy-start(f32[256,128]{0,1:T(8,128)} %copy.62) | copy-start | bytes 393220
  96.7 16.2 %all-to-all-start.5 = ((f32[32,16,128]{2,1,0:T(8,128)}), f32[32,16,128]{2,1,0:T(8,128)S(1)}, u32[]{:S(2)}, u32[]{:S(2)}) async-start(f32[32,16,128]{2,1,0:T(8,128)} %broadcast_in_dim.17), calls=%async_computation.5 | async-start | bytes 524288 | tf_op jit(solution)/shard_map/all_to_all | solution.py:13
  114.5 16.3 %collective-permute-start.2 = (f32[512,128]{1,0:T(8,128)S(1)}, f32[512,128]{1,0:T(8,128)S(1)}, u32[]{:S(2)}, u32[]{:S(2)}) collective-permute-start(f32[512,128]{1,0:T(8,128)S(1)} %convolution_subtract_fusion), channel_id=1, source_target_pairs={{0,32},{32,64},{64,96},{96,128},{128,160},{160,192},{192,224},{224... | collective-permute-start | bytes 786440 | tf_op jit(solution)/shard_map/ppermute | solution.py:43
  116.6 13.6 %all-to-all-start.6 = ((f32[32,1,128]{2,1,0:T(1,128)}), f32[32,1,128]{2,1,0:T(1,128)S(1)}, u32[]{:S(2)}, u32[]{:S(2)}) async-start(f32[32,1,128]{2,1,0:T(1,128)} %broadcast_in_dim.19), calls=%async_computation.6 | async-start | bytes 32768 | tf_op jit(solution)/shard_map/all_to_all | solution.py:13
  130.8 1.3 %copy-start.1 = (f32[512,1024]{1,0:T(8,128)}, f32[512,1024]{1,0:T(8,128)S(1)}, u32[]{:S(2)}) copy-start(f32[512,1024]{1,0:T(8,128)S(1)} %constant_dynamic-update-slice_fusion) | copy-start | bytes 6291460

commit v3 on v2

v3 whole, which is shorter than its diff:
```python
import jax
import jax.numpy as jnp
from jax import lax
from jax.experimental import pallas as pl
from jax.experimental.pallas import tpu as pltpu
from jax.sharding import PartitionSpec as P

TILE = 128
NEAR = 4


def exchange(blocks, axis, groups=None):
    return lax.all_to_all(
        blocks, axis, split_axis=0, concat_axis=0, axis_index_groups=groups, tiled=True
    )


def rings(axis):
    count = lax.axis_size(axis)
    near = [[a + b for b in range(NEAR)] for a in range(0, count, NEAR)]
    far = [[a + b for a in range(0, count, NEAR)] for b in range(NEAR)]
    return near, far


def summed_in_turn(lines, axis):
    near, far = rings(axis)
    blocks = exchange(lines.reshape(len(near[0]), -1, TILE), axis, near)
    blocks = exchange(blocks.sum(axis=0).reshape(len(far[0]), -1, TILE), axis, far)
    own = blocks.sum(axis=0)
    blocks = exchange(jnp.broadcast_to(own, blocks.shape), axis, far).reshape(-1, TILE)
    blocks = exchange(jnp.broadcast_to(blocks, (len(near[0]), *blocks.shape)), axis, near)
    return blocks.reshape(-1, TILE)


def summed(lines, axis):
    blocks = lines.reshape(lax.axis_size(axis), -1, TILE)
    own = exchange(blocks, axis).sum(axis=0)
    return exchange(jnp.broadcast_to(own, blocks.shape), axis).reshape(-1, TILE)


def shifted(value, axis, steps):
    count = lax.axis_size(axis)
    pairs = [(source, (source + steps) % count) for source in range(count)]
    return lax.ppermute(value, axis, pairs)


def halves(value):
    high = value.astype(jnp.bfloat16)
    return high, (value - high.astype(jnp.float32)).astype(jnp.bfloat16)


def product(a, b):
    def once(x, y):
        return jnp.dot(x, y, preferred_element_type=jnp.float32)

    return once(a[0], b[0]) + (once(a[0], b[1]) + once(a[1], b[0]))


def tiles_of(size):
    count = size // TILE
    return [(i, j) for i in range(count) for j in range(i, count)]


def start_kernel(basis_ref, vec_ref, out_ref):
    basis = basis_ref[...]
    size = basis.shape[1]
    count = size // TILE
    turned = halves(basis.T)
    right = halves(jnp.concatenate([basis, vec_ref[...]], axis=1))
    at = 0
    for i in range(count):
        left = tuple(part[i * TILE:(i + 1) * TILE] for part in turned)
        strip = product(left, tuple(part[:, i * TILE:] for part in right))
        for j in range(count - i):
            out_ref[at:at + TILE] = strip[:, j * TILE:(j + 1) * TILE]
            at += TILE
        base = (len(tiles_of(size)) + i) * TILE
        out_ref[base:base + TILE] = strip[:, (count - i) * TILE:]


def both(first, gram_ref, size):
    count = size // TILE
    part = {}
    for at, (i, j) in enumerate(tiles_of(size)):
        tile = gram_ref[at * TILE:(at + 1) * TILE]
        part[i, j] = tile
        if i != j:
            part[j, i] = tile.T
    right = halves(first)
    rows = []
    for i in range(count):
        row = jnp.concatenate([part[i, j] for j in range(count)], axis=1)
        rows.append(product(halves(row), right))
    return 2.0 * first - jnp.concatenate(rows, axis=0)


def turn_kernel(got_ref, basis_ref, vec_ref, next_ref, here_ref, vec_out, first_out):
    size = basis_ref.shape[1]
    here = both(got_ref[got_ref.shape[0] - size:], got_ref, size)
    here_ref[...] = here
    vec = vec_ref[...] - product(halves(basis_ref[...]), halves(here))
    vec_out[...] = vec
    first_out[...] = product(halves(next_ref[...].T), halves(vec))


def end_kernel(first_ref, gram_ref, basis_ref, vec_ref, there_ref, vec_out, squares_ref):
    there = both(first_ref[...], gram_ref, basis_ref.shape[1])
    there_ref[...] = there
    vec = vec_ref[...] - product(halves(basis_ref[...]), halves(there))
    vec_out[...] = vec
    squares_ref[...] = jnp.sum(vec * vec, axis=0, keepdims=True)


def local(kernel, ins, *shapes):
    outs = [jax.ShapeDtypeStruct(shape, jnp.float32) for shape in shapes]
    return pl.pallas_call(
        kernel,
        in_specs=[pl.BlockSpec(memory_space=pltpu.VMEM)] * ins,
        out_specs=[pl.BlockSpec(memory_space=pltpu.VMEM)] * len(outs),
        out_shape=outs,
        compiler_params=pltpu.CompilerParams(vmem_limit_bytes=16 * 2**20),
    )


def per_device(snapshots, basis):
    sections = lax.axis_size("segment")
    lines = lax.axis_size("row")
    position = lax.axis_index("segment")
    rows, width = snapshots.shape
    size = basis.shape[1]
    share = len(tiles_of(size)) * TILE
    total_rows = rows * lines
    onward = shifted(basis, "segment", -1)

    sent = local(start_kernel, 2, (share + size, TILE))(basis, snapshots)[0]
    got = summed_in_turn(sent, "row")
    gram_next = shifted(got[:share], "segment", -1)
    here, vec, first = local(turn_kernel, 4, (size, width), (rows, width), (size, width))(
        got, basis, snapshots, onward
    )
    first = summed(first, "row")
    there, vec, squares = local(end_kernel, 4, (size, width), (rows, width), (1, width))(
        first, gram_next, onward, vec
    )

    arrived = shifted(there, "segment", 1)
    sums = exchange(jnp.broadcast_to(squares, (lines, width)), "row").sum(axis=0)
    rms = jnp.sqrt(sums / total_rows)
    coeff = jnp.zeros((size, width * sections), jnp.float32)
    coeff = lax.dynamic_update_slice(coeff, here, (jnp.int32(0), position * width))
    before = (position - 1) % sections
    coeff = lax.dynamic_update_slice(coeff, arrived, (jnp.int32(0), before * width))
    return (vec, coeff, rms)


def solution(mesh):
    placed = (P("row", "segment"), P("row", "segment"))
    return jax.shard_map(
        per_device,
        mesh=mesh,
        in_specs=placed,
        out_specs=(P("row", "segment"), P("segment", None), P("segment")),
        check_vma=False,
    )
```

time: 134 us -> 120 us (0.90); the launches traced: 132 us -> 119 us
  blocking collectives: 65.4 us -> 48.8 us
  waiting for transfers between devices: 28.2 us -> 42.4 us
  matrix products: 11.5 us -> 0 us
  local copies, waits for them, and re-layouts: 13.9 us -> 7.34 us
  Pallas kernels: 0 us -> 4.2 us
  starting transfers between devices: 11.3 us -> 15.3 us
    all_to_all x4 -> x3, blocking collectives: 65.4 us -> 48.8 us  [exchange(): lax.all_to_all(blocks, axis, split_axis=0, concat_axis=0, axis_index_grou...]
    dot_general x10 -> x0, matrix products: 11.5 us -> none  [dot(): lax.dot_general(a, b, ((over[0], over[1]), ((), ())), precision=lax.Preci...]
    all_to_all x3 -> x4, waiting for transfers between devices: 28.2 us -> 35.7 us  [exchange(): lax.all_to_all(blocks, axis, split_axis=0, concat_axis=0, axis_index_grou...]
    ppermute x3, waiting for transfers between devices: 0.01 us -> 6.7 us  [shifted(): return lax.ppermute(value, axis, pairs)]
    pallas_call x0 -> x3, Pallas kernels: none -> 4.2 us  [the longest x1 2.03 us: per_device(): local(turn_kernel, 4, (size, width), (rows, width), (size, width))]
    all_to_all x3 -> x4, starting transfers between devices: 11.2 us -> 15.2 us  [exchange(): lax.all_to_all(blocks, axis, split_axis=0, concat_axis=0, axis_index_grou...]
    slice x3 -> x1, local copies, waits for them, and re-layouts: 3.57 us -> 0.04 us  [per_device(): gram_next = shifted(got[:share], 'segment', -1)]
    transpose x6 -> x0, local copies, waits for them, and re-layouts: 2.46 us -> none  [whole(): part[j, i] = tile.T]
  transfers between devices with their start and end apart: 6 -> 7, of which waited for: 3 -> 5; matrix products, arithmetic and copies ran while one was open for 12% -> 3% of each run, Pallas kernels for 0% -> 0%
where the time goes in v3:
time: 120 us; the launch traced here: 119 us
  blocking collectives  48.8 us (41%)
  waiting for transfers between devices  42.4 us (35%)
  starting transfers between devices  15.3 us (13%)
  local copies, waits for them, and re-layouts  7.34 us (6%)
  Pallas kernels  4.2 us (4%)
    all_to_all x3, blocking collectives, exchange(): lax.all_to_all(blocks, axis, split_axis=0, concat_axis=0, axis_index_grou...  48.8 us
    all_to_all x4, waiting for transfers between devices, exchange(): lax.all_to_all(blocks, axis, split_axis=0, concat_axis=0, axis_index_grou...  35.7 us
    all_to_all x4, starting transfers between devices, exchange(): lax.all_to_all(blocks, axis, split_axis=0, concat_axis=0, axis_index_grou...  15.2 us
    ppermute x3, waiting for transfers between devices, shifted(): return lax.ppermute(value, axis, pairs)  6.7 us
  transfers between devices with their start and end apart: 7, of which 5 were waited for; matrix products, arithmetic and copies ran while one was open for 3% of the time, Pallas kernels for 0%

profile of v3, /device:TPU:8, one launch (start us, length us, event | category | flops | bytes accessed | tf_op | source)
XLA Modules:
  0.0 119.5 jit_solution(7174332814486344791)
XLA Ops:
  0.6 0.0 copy-start
  0.6 1.0 copy-done
  1.7 0.0 copy-start.2
  1.7 0.9 copy-done.2
  2.6 0.6 shard_map.49
  3.2 17.8 %all_to_all.36 = f32[4,448,128]{2,1,0:T(8,128)S(1)} all-to-all(f32[4,448,128]{2,1,0:T(8,128)S(1)} %bitcast.10), channel_id=1, replica_groups={{0,1,2,3},{4,5,6,7},{8,9,10,11},{12,13,14,15},{16,17,18,19},{20,21,22,2..., dimensions={0} | all-to-all | bytes 1835008 | tf_op jit(solution)/shard_map/all_to_all | solution.py:13
  21.0 0.0 copy-start.1
  21.1 0.0 copy-start.3
  21.1 18.5 %all_to_all.37 = f32[8,56,128]{2,1,0:T(8,128)S(1)} all-to-all(f32[8,56,128]{2,1,0:T(8,128)S(1)} %bitcast.13), channel_id=1, replica_groups={{0,4,8,12,16,20,24,28},{1,5,9,13,17,21,25,29},{2,6,10,14,18,22,26,30},{..., dimensions={0} | all-to-all | bytes 458752 | tf_op jit(solution)/shard_map/all_to_all | solution.py:13
  39.6 12.5 %all_to_all.38 = f32[8,56,128]{2,1,0:T(8,128)S(1)} all-to-all(f32[8,56,128]{2,1,0:T(8,128)S(1)} %broadcast_in_dim.17), channel_id=1, replica_groups={{0,4,8,12,16,20,24,28},{1,5,9,13,17,21,25,29},{2,6,10,14,18,22,26,30},{..., dimensions={0} | all-to-all | bytes 458752 | tf_op jit(solution)/shard_map/all_to_all | solution.py:13
  52.2 1.0 broadcast_in_dim.18
  53.2 3.5 %all-to-all-start.3 = ((f32[4,448,128]{2,1,0:T(8,128)}), f32[4,448,128]{2,1,0:T(8,128)S(1)}, u32[]{:S(2)}, u32[]{:S(2)}) async-start(f32[4,448,128]{2,1,0:T(8,128)} %broadcast_in_dim.18), calls=%async_computation.3 | async-start | bytes 1835008 | tf_op jit(solution)/shard_map/all_to_all | solution.py:13
  56.7 0.0 copy-done.1
  56.7 0.0 collective-permute-start
  56.7 6.7 %collective-permute-done.next_ref.basis_ref = f32[256,512]{1,0:T(8,128)S(1)} collective-permute-done((f32[256,512]{1,0:T(8,128)S(1)}, f32[256,512]{1,0:T(8,128)S(1)}, u32[]{:S(2)}, u32[]{:S(2)}) %collective-permute-start) | collective-permute-done | bytes 524320 | tf_op jit(solution)/shard_map/ppermute | solution.py:44
  63.4 3.6 %all-to-all-done.3 = f32[4,448,128]{2,1,0:T(8,128)S(1)} async-done(((f32[4,448,128]{2,1,0:T(8,128)}), f32[4,448,128]{2,1,0:T(8,128)S(1)}, u32[]{:S(2)}, u32[]{:S(2)}) %all-to-all-start.3) | async-done | bytes 917536 | tf_op jit(solution)/shard_map/all_to_all | solution.py:13
  67.0 0.0 copy-done.3
  67.0 2.0 %shard_map.50 = (f32[512,128]{1,0:T(8,128)S(1)}, f32[256,128]{1,0:T(8,128)S(1)}, f32[512,128]{1,0:T(8,128)}) custom-call(f32[1792,128]{1,0:T(8,128)S(1)} %bitcast.8, f32[256,512]{1,0:T(8,128)S(1)} %copy-done.1, f32[256,128]{1,0:T(8,128)S(1)} %copy-done.3, f32[256,512]{1,0:T(8,128)S(1)} %collective-permute-done.next_ref.basis_ref), custom_call_target="tpu_custom_call" | custom-call | tf_op jit(solution)/shard_map/pallas_call | solution.py:138
  69.1 3.9 %all-to-all-start.4 = ((f32[32,16,128]{2,1,0:T(8,128)}), f32[32,16,128]{2,1,0:T(8,128)S(1)}, u32[]{:S(2)}, u32[]{:S(2)}) async-start(f32[32,16,128]{2,1,0:T(8,128)} %bitcast.4), calls=%async_computation.4 | async-start | bytes 524288 | tf_op jit(solution)/shard_map/all_to_all | solution.py:13
  73.0 0.0 collective-permute-start.1
  73.0 12.3 %all-to-all-done.4 = f32[32,16,128]{2,1,0:T(8,128)S(1)} async-done(((f32[32,16,128]{2,1,0:T(8,128)}), f32[32,16,128]{2,1,0:T(8,128)S(1)}, u32[]{:S(2)}, u32[]{:S(2)}) %all-to-all-start.4) | async-done | bytes 262176 | tf_op jit(solution)/shard_map/all_to_all | solution.py:13
  85.3 0.7 broadcast_in_dim.19
  86.1 4.1 %all-to-all-start.5 = ((f32[32,16,128]{2,1,0:T(8,128)}), f32[32,16,128]{2,1,0:T(8,128)S(1)}, u32[]{:S(2)}, u32[]{:S(2)}) async-start(f32[32,16,128]{2,1,0:T(8,128)} %broadcast_in_dim.19), calls=%async_computation.5 | async-start | bytes 524288 | tf_op jit(solution)/shard_map/all_to_all | solution.py:13
  90.2 0.0 collective-permute-done.1.gram_ref
  90.2 12.3 %all-to-all-done.5 = f32[32,16,128]{2,1,0:T(8,128)S(1)} async-done(((f32[32,16,128]{2,1,0:T(8,128)}), f32[32,16,128]{2,1,0:T(8,128)S(1)}, u32[]{:S(2)}, u32[]{:S(2)}) %all-to-all-start.5) | async-done | bytes 262176 | tf_op jit(solution)/shard_map/all_to_all | solution.py:13
  102.5 1.6 %shard_map.51 = (f32[512,128]{1,0:T(8,128)S(1)}, f32[256,128]{1,0:T(8,128)}, f32[1,128]{1,0:T(1,128)S(1)}) custom-call(f32[512,128]{1,0:T(8,128)S(1)} %bitcast.11, f32[1280,128]{1,0:T(8,128)S(1)} %collective-permute-done.1.gram_ref, f32[256,512]{1,0:T(8,128)S(1)} %collective-permute-done.next_ref.basis_ref, f32[256,128]{1,0:T(8,128)S(1)} %get-tuple-element.10.vec_ref), custom_call_target="tpu_custom_call" | custom-call | tf_op jit(solution)/shard_map/pallas_call | solution.py:142
  104.1 0.6 broadcast_in_dim.21
  104.7 3.8 %all-to-all-start.6 = ((f32[32,1,128]{2,1,0:T(1,128)}), f32[32,1,128]{2,1,0:T(1,128)S(1)}, u32[]{:S(2)}, u32[]{:S(2)}) async-start(f32[32,1,128]{2,1,0:T(1,128)} %broadcast_in_dim.21), calls=%async_computation.6 | async-start | bytes 32768 | tf_op jit(solution)/shard_map/all_to_all | solution.py:13
  108.5 0.0 collective-permute-start.2
  108.5 1.6 %broadcast_in_dim.20 = f32[512,1024]{1,0:T(8,128)} broadcast(f32[]{:T(128)} %constant.11.clone.1), dimensions={} | broadcast | bytes 2097156 | tf_op jit(solution)/shard_map/broadcast_in_dim | solution.py:149
  110.1 0.7 constant_dynamic-update-slice_fusion.1
  110.8 7.4 %all-to-all-done.6 = f32[32,1,128]{2,1,0:T(1,128)S(1)} async-done(((f32[32,1,128]{2,1,0:T(1,128)}), f32[32,1,128]{2,1,0:T(1,128)S(1)}, u32[]{:S(2)}, u32[]{:S(2)}) %all-to-all-start.6) | async-done | bytes 16416 | tf_op jit(solution)/shard_map/all_to_all | solution.py:13
  118.2 0.5 multiply_sqrt_fusion
  118.8 0.0 collective-permute-done.2
  118.8 0.7 constant_dynamic-update-slice_fusion
  (6 shorter events, 0.2 us)
Async XLA Ops:
  0.6 1.0 copy-start
  1.7 0.9 copy-start.2
  21.0 35.6 %copy-start.1 = (f32[256,512]{1,0:T(8,128)S(1)}, f32[256,512]{1,0:T(8,128)}, u32[]{:S(2)}) copy-start(f32[256,512]{1,0:T(8,128)} %basis_ref.3) | copy-start | bytes 1572868
  21.1 46.0 %copy-start.3 = (f32[256,128]{1,0:T(8,128)S(1)}, f32[256,128]{1,0:T(8,128)}, u32[]{:S(2)}) copy-start(f32[256,128]{1,0:T(8,128)} %vec_ref.3) | copy-start | bytes 393220
  53.2 13.9 %all-to-all-start.3 = ((f32[4,448,128]{2,1,0:T(8,128)}), f32[4,448,128]{2,1,0:T(8,128)S(1)}, u32[]{:S(2)}, u32[]{:S(2)}) async-start(f32[4,448,128]{2,1,0:T(8,128)} %broadcast_in_dim.18), calls=%async_computation.3 | async-start | bytes 1835008 | tf_op jit(solution)/shard_map/all_to_all | solution.py:13
  56.7 6.7 %collective-permute-start = (f32[256,512]{1,0:T(8,128)S(1)}, f32[256,512]{1,0:T(8,128)S(1)}, u32[]{:S(2)}, u32[]{:S(2)}) collective-permute-start(f32[256,512]{1,0:T(8,128)S(1)} %copy-done.1), channel_id=1, source_target_pairs={{0,224},{32,0},{64,32},{96,64},{128,96},{160,128},{192,160},{224,1... | collective-permute-start | bytes 1572872 | tf_op jit(solution)/shard_map/ppermute | solution.py:44
  69.1 16.2 %all-to-all-start.4 = ((f32[32,16,128]{2,1,0:T(8,128)}), f32[32,16,128]{2,1,0:T(8,128)S(1)}, u32[]{:S(2)}, u32[]{:S(2)}) async-start(f32[32,16,128]{2,1,0:T(8,128)} %bitcast.4), calls=%async_computation.4 | async-start | bytes 524288 | tf_op jit(solution)/shard_map/all_to_all | solution.py:13
  73.0 17.2 %collective-permute-start.1 = (f32[1280,128]{1,0:T(8,128)S(1)}, f32[1280,128]{1,0:T(8,128)S(1)}, u32[]{:S(2)}, u32[]{:S(2)}) collective-permute-start(f32[1280,128]{1,0:T(8,128)S(1)} %slice.4), channel_id=1, source_target_pairs={{0,224},{32,0},{64,32},{96,64},{128,96},{160,128},{192,160},{224,1... | collective-permute-start | bytes 1966088 | tf_op jit(solution)/shard_map/ppermute | solution.py:44
  86.1 16.5 %all-to-all-start.5 = ((f32[32,16,128]{2,1,0:T(8,128)}), f32[32,16,128]{2,1,0:T(8,128)S(1)}, u32[]{:S(2)}, u32[]{:S(2)}) async-start(f32[32,16,128]{2,1,0:T(8,128)} %broadcast_in_dim.19), calls=%async_computation.5 | async-start | bytes 524288 | tf_op jit(solution)/shard_map/all_to_all | solution.py:13
  104.7 13.5 %all-to-all-start.6 = ((f32[32,1,128]{2,1,0:T(1,128)}), f32[32,1,128]{2,1,0:T(1,128)S(1)}, u32[]{:S(2)}, u32[]{:S(2)}) async-start(f32[32,1,128]{2,1,0:T(1,128)} %broadcast_in_dim.21), calls=%async_computation.6 | async-start | bytes 32768 | tf_op jit(solution)/shard_map/all_to_all | solution.py:13
  108.5 10.3 %collective-permute-start.2 = (f32[512,128]{1,0:T(8,128)S(1)}, f32[512,128]{1,0:T(8,128)S(1)}, u32[]{:S(2)}, u32[]{:S(2)}) collective-permute-start(f32[512,128]{1,0:T(8,128)S(1)} %get-tuple-element.13), channel_id=1, source_target_pairs={{0,32},{32,64},{64,96},{96,128},{128,160},{160,192},{192,224},{224... | collective-permute-start | bytes 786440 | tf_op jit(solution)/shard_map/ppermute | solution.py:44

commit v4 on v3

--- a/solution.py
+++ b/solution.py
@@ -5,6 +5,7 @@
 from jax.experimental.pallas import tpu as pltpu
 from jax.sharding import PartitionSpec as P
 
+
 TILE = 128
 NEAR = 4
 
@@ -22,20 +23,12 @@
     return near, far
 
 
-def summed_in_turn(lines, axis):
-    near, far = rings(axis)
-    blocks = exchange(lines.reshape(len(near[0]), -1, TILE), axis, near)
-    blocks = exchange(blocks.sum(axis=0).reshape(len(far[0]), -1, TILE), axis, far)
+def gathered(mine, near, far):
+    blocks = exchange(mine.reshape(len(far[0]), -1, TILE), "row", far)
     own = blocks.sum(axis=0)
-    blocks = exchange(jnp.broadcast_to(own, blocks.shape), axis, far).reshape(-1, TILE)
-    blocks = exchange(jnp.broadcast_to(blocks, (len(near[0]), *blocks.shape)), axis, near)
+    blocks = exchange(jnp.broadcast_to(own, blocks.shape), "row", far).reshape(-1, TILE)
+    blocks = exchange(jnp.broadcast_to(blocks, (len(near[0]), *blocks.shape)), "row", near)
     return blocks.reshape(-1, TILE)
-
-
-def summed(lines, axis):
-    blocks = lines.reshape(lax.axis_size(axis), -1, TILE)
-    own = exchange(blocks, axis).sum(axis=0)
-    return exchange(jnp.broadcast_to(own, blocks.shape), axis).reshape(-1, TILE)
 
 
 def shifted(value, axis, steps):
@@ -61,7 +54,15 @@
     return [(i, j) for i in range(count) for j in range(i, count)]
 
 
-def start_kernel(basis_ref, vec_ref, out_ref):
+def start_kernel(basis_hbm, vec_hbm, out_ref, basis_ref, vec_ref, done):
+    copies = [
+        pltpu.make_async_copy(basis_hbm, basis_ref, done.at[0]),
+        pltpu.make_async_copy(vec_hbm, vec_ref, done.at[1]),
+    ]
+    for copy in copies:
+        copy.start()
+    for copy in copies:
+        copy.wait()
     basis = basis_ref[...]
     size = basis.shape[1]
     count = size // TILE
@@ -94,13 +95,34 @@
     return 2.0 * first - jnp.concatenate(rows, axis=0)
 
 
-def turn_kernel(got_ref, basis_ref, vec_ref, next_ref, here_ref, vec_out, first_out):
+def turn_kernel(
+    got_ref, basis_ref, vec_ref, next_ref, vec_out, first_out, coeff_hbm, here_ref, zero_ref, done
+):
     size = basis_ref.shape[1]
+    width = vec_ref.shape[1]
+    sections = coeff_hbm.shape[1] // width
+    zero_ref[...] = jnp.zeros_like(zero_ref)
+    fills = [
+        pltpu.make_async_copy(
+            zero_ref, coeff_hbm.at[:, b * width:(b + 1) * width], done.at[b]
+        )
+        for b in range(sections)
+    ]
+    for fill in fills:
+        fill.start()
     here = both(got_ref[got_ref.shape[0] - size:], got_ref, size)
     here_ref[...] = here
     vec = vec_ref[...] - product(halves(basis_ref[...]), halves(here))
     vec_out[...] = vec
+    for fill in fills:
+        fill.wait()
+    column = pl.multiple_of(lax.axis_index("segment") * width, width)
+    own = pltpu.make_async_copy(
+        here_ref, coeff_hbm.at[:, pl.ds(column, width)], done.at[sections]
+    )
+    own.start()
     first_out[...] = product(halves(next_ref[...].T), halves(vec))
+    own.wait()
 
 
 def end_kernel(first_ref, gram_ref, basis_ref, vec_ref, there_ref, vec_out, squares_ref):
@@ -111,13 +133,13 @@
     squares_ref[...] = jnp.sum(vec * vec, axis=0, keepdims=True)
 
 
-def local(kernel, ins, *shapes):
-    outs = [jax.ShapeDtypeStruct(shape, jnp.float32) for shape in shapes]
+def local(kernel, ins, outs, scratch=()):
     return pl.pallas_call(
         kernel,
-        in_specs=[pl.BlockSpec(memory_space=pltpu.VMEM)] * ins,
-        out_specs=[pl.BlockSpec(memory_space=pltpu.VMEM)] * len(outs),
-        out_shape=outs,
+        in_specs=[pl.BlockSpec(memory_space=space) for space in ins],
+        out_specs=[pl.BlockSpec(memory_space=space) for space, _ in outs],
+        out_shape=[jax.ShapeDtypeStruct(shape, jnp.float32) for _, shape in outs],
+        scratch_shapes=scratch,
         compiler_params=pltpu.CompilerParams(vmem_limit_bytes=16 * 2**20),
     )
 
@@ -130,26 +152,40 @@
     size = basis.shape[1]
     share = len(tiles_of(size)) * TILE
     total_rows = rows * lines
+    hbm = pltpu.HBM
+    near, far = rings("row")
+
     onward = shifted(basis, "segment", -1)
-
-    sent = local(start_kernel, 2, (share + size, TILE))(basis, snapshots)[0]
-    got = summed_in_turn(sent, "row")
-    gram_next = shifted(got[:share], "segment", -1)
-    here, vec, first = local(turn_kernel, 4, (size, width), (rows, width), (size, width))(
-        got, basis, snapshots, onward
-    )
-    first = summed(first, "row")
-    there, vec, squares = local(end_kernel, 4, (size, width), (rows, width), (1, width))(
-        first, gram_next, onward, vec
-    )
+    (sent,) = local(
+        start_kernel, (hbm, hbm), [(pltpu.VMEM, (share + size, TILE))],
+        (pltpu.VMEM(basis.shape, jnp.float32), pltpu.VMEM(snapshots.shape, jnp.float32),
+         pltpu.SemaphoreType.DMA((2,))),
+    )(*(pltpu.with_memory_space_constraint(array, hbm) for array in (basis, snapshots)))
+    blocks = exchange(sent.reshape(len(near[0]), -1, TILE), "row", near)
+    mine, onward = lax.optimization_barrier((blocks.sum(axis=0), onward))
+    got = gathered(mine, near, far)
+    gram_next = shifted(got, "segment", -1)
+    vec, first, coeff = local(
+        turn_kernel, (pltpu.VMEM,) * 4,
+        [(pltpu.VMEM, (rows, width)), (pltpu.VMEM, (size, width)),
+         (hbm, (size, width * sections))],
+        (pltpu.VMEM((size, width), jnp.float32), pltpu.VMEM((size, width), jnp.float32),
+         pltpu.SemaphoreType.DMA((sections + 1,))),
+    )(got, basis, snapshots, onward)
+    blocks = exchange(first.reshape(lines, -1, TILE), "row")
+    blocks, gram_next = lax.optimization_barrier((blocks, gram_next))
+    first = exchange(jnp.broadcast_to(blocks.sum(axis=0), blocks.shape), "row")
+    there, vec, squares = local(
+        end_kernel, (pltpu.VMEM,) * 4,
+        [(pltpu.VMEM, (size, width)), (pltpu.VMEM, (rows, width)), (pltpu.VMEM, (1, width))],
+    )(first.reshape(-1, TILE), gram_next, onward, vec)
 
     arrived = shifted(there, "segment", 1)
-    sums = exchange(jnp.broadcast_to(squares, (lines, width)), "row").sum(axis=0)
-    rms = jnp.sqrt(sums / total_rows)
-    coeff = jnp.zeros((size, width * sections), jnp.float32)
-    coeff = lax.dynamic_update_slice(coeff, here, (jnp.int32(0), position * width))
+    blocks = exchange(jnp.broadcast_to(squares, (lines, width)), "row")
     before = (position - 1) % sections
     coeff = lax.dynamic_update_slice(coeff, arrived, (jnp.int32(0), before * width))
+    blocks, coeff = lax.optimization_barrier((blocks, coeff))
+    rms = jnp.sqrt(blocks.sum(axis=0) / total_rows)
     return (vec, coeff, rms)
 
 

time: 120 us -> 120 us (level); the launches traced: 119 us -> 118 us
  blocking collectives: 48.8 us -> 76.7 us
  waiting for transfers between devices: 42.4 us -> 22.6 us
  starting transfers between devices: 15.3 us -> 8.35 us
  local copies, waits for them, and re-layouts: 7.34 us -> 1.43 us
  Pallas kernels: 4.2 us -> 7.36 us
    all_to_all x3 -> x5, blocking collectives: 48.8 us -> 76.7 us  [exchange(): lax.all_to_all(blocks, axis, split_axis=0, concat_axis=0, axis_index_grou...]
    all_to_all x4 -> x2, waiting for transfers between devices: 35.7 us -> 21.4 us  [exchange(): lax.all_to_all(blocks, axis, split_axis=0, concat_axis=0, axis_index_grou...]
    all_to_all x4 -> x2, starting transfers between devices: 15.2 us -> 8.34 us  [exchange(): lax.all_to_all(blocks, axis, split_axis=0, concat_axis=0, axis_index_grou...]
    ppermute x3, waiting for transfers between devices: 6.7 us -> 1.15 us  [shifted(): return lax.ppermute(value, axis, pairs)]
    broadcast_in_dim x5 -> x4, local copies, waits for them, and re-layouts: 3.9 us -> 0.7 us  [the longest x1 0.6 us: per_device(): blocks = exchange(jnp.broadcast_to(squares, (lines, width)), 'row')]
    pallas_call x3, Pallas kernels: 4.2 us -> 7.36 us  [the longest x1 3.11 us: per_device(): local(turn_kernel, (pltpu.VMEM,) * 4, [(pltpu.VMEM, (rows, width)), (pltp...]
    unnamed x8 -> x4, local copies, waits for them, and re-layouts: 1.95 us -> 0.01 us
  transfers between devices with their start and end apart: 7 -> 5, of which waited for: 5 -> 3; matrix products, arithmetic and copies ran while one was open for 3% -> 1% of each run, Pallas kernels for 0% -> 3%
where the time goes in v4:
time: 120 us; the launch traced here: 118 us
  blocking collectives  76.7 us (64%)
  waiting for transfers between devices  22.6 us (19%)
  starting transfers between devices  8.35 us (7%)
  Pallas kernels  7.36 us (6%)
  local copies, waits for them, and re-layouts  1.43 us (1%)
    all_to_all x5, blocking collectives, exchange(): lax.all_to_all(blocks, axis, split_axis=0, concat_axis=0, axis_index_grou...  76.7 us
    all_to_all x2, waiting for transfers between devices, exchange(): lax.all_to_all(blocks, axis, split_axis=0, concat_axis=0, axis_index_grou...  21.4 us
    all_to_all x2, starting transfers between devices, exchange(): lax.all_to_all(blocks, axis, split_axis=0, concat_axis=0, axis_index_grou...  8.34 us
    pallas_call x1, Pallas kernels, per_device(): local(turn_kernel, (pltpu.VMEM,) * 4, [(pltpu.VMEM, (rows, width)), (pltp...  3.11 us
    pallas_call x1, Pallas kernels, per_device(): local(start_kernel, (hbm, hbm), [(pltpu.VMEM, (share + size, TILE))], (pl...  2.69 us
  transfers between devices with their start and end apart: 5, of which 3 were waited for; matrix products, arithmetic and copies ran while one was open for 1% of the time, Pallas kernels for 3%

profile of v4, /device:TPU:8, one launch (start us, length us, event | category | flops | bytes accessed | tf_op | source)
XLA Modules:
  0.0 117.8 jit_solution(18147738823247752673)
XLA Ops:
  0.6 0.0 copy-start
  0.6 2.7 %shard_map.49 = f32[1792,128]{1,0:T(8,128)} custom-call(f32[256,512]{1,0:T(8,128)} %basis_ref.1, f32[256,128]{1,0:T(8,128)} %vec_ref.1), custom_call_target="tpu_custom_call" | custom-call | tf_op jit(solution)/shard_map/pallas_call | solution.py:159
  3.3 4.3 %all-to-all-start = ((f32[4,448,128]{2,1,0:T(8,128)}), f32[4,448,128]{2,1,0:T(8,128)S(1)}, u32[]{:S(2)}, u32[]{:S(2)}) async-start(f32[4,448,128]{2,1,0:T(8,128)} %bitcast), calls=%async_computation | async-start | bytes 1835008 | tf_op jit(solution)/shard_map/all_to_all | solution.py:14
  7.6 0.0 copy-done
  7.6 0.0 collective-permute-start
  7.6 13.7 %all-to-all-done = f32[4,448,128]{2,1,0:T(8,128)S(1)} async-done(((f32[4,448,128]{2,1,0:T(8,128)}), f32[4,448,128]{2,1,0:T(8,128)S(1)}, u32[]{:S(2)}, u32[]{:S(2)}) %all-to-all-start) | async-done | bytes 917536 | tf_op jit(solution)/shard_map/all_to_all | solution.py:14
  21.4 0.0 collective-permute-done.next_ref.basis_ref
  21.4 0.0 copy-start.1
  21.4 18.5 %all_to_all.39 = f32[8,56,128]{2,1,0:T(8,128)S(1)} all-to-all(f32[8,56,128]{2,1,0:T(8,128)S(1)} %bitcast.13), channel_id=1, replica_groups={{0,4,8,12,16,20,24,28},{1,5,9,13,17,21,25,29},{2,6,10,14,18,22,26,30},{..., dimensions={0} | all-to-all | bytes 458752 | tf_op jit(solution)/shard_map/all_to_all | solution.py:14
  40.0 12.5 %all_to_all.40 = f32[8,56,128]{2,1,0:T(8,128)S(1)} all-to-all(f32[8,56,128]{2,1,0:T(8,128)S(1)} %broadcast_in_dim.14), channel_id=1, replica_groups={{0,4,8,12,16,20,24,28},{1,5,9,13,17,21,25,29},{2,6,10,14,18,22,26,30},{..., dimensions={0} | all-to-all | bytes 458752 | tf_op jit(solution)/shard_map/all_to_all | solution.py:14
  52.5 0.1 broadcast_in_dim.15
  52.6 12.8 %all_to_all.41 = f32[4,448,128]{2,1,0:T(8,128)S(1)} all-to-all(f32[4,448,128]{2,1,0:T(8,128)S(1)} %broadcast_in_dim.15), channel_id=1, replica_groups={{0,1,2,3},{4,5,6,7},{8,9,10,11},{12,13,14,15},{16,17,18,19},{20,21,22,2..., dimensions={0} | all-to-all | bytes 1835008 | tf_op jit(solution)/shard_map/all_to_all | solution.py:14
  65.4 0.0 collective-permute-start.1
  65.4 0.0 copy-done.1
  65.4 3.1 %shard_map.50 = (f32[256,128]{1,0:T(8,128)S(1)}, f32[512,128]{1,0:T(8,128)S(1)}, f32[512,1024]{1,0:T(8,128)}) custom-call(f32[1792,128]{1,0:T(8,128)S(1)} %bitcast.9, f32[256,512]{1,0:T(8,128)S(1)} %copy-done, f32[256,128]{1,0:T(8,128)S(1)} %copy-done.1, f32[256,512]{1,0:T(8,128)S(1)} %collective-permute-done.next_ref.basis_ref), custom_call_target="tpu_custom_call" | custom-call | tf_op jit(solution)/shard_map/pallas_call | solution.py:168
  68.5 16.9 %all_to_all.42 = f32[32,16,128]{2,1,0:T(8,128)S(1)} all-to-all(f32[32,16,128]{2,1,0:T(8,128)S(1)} %bitcast.11), channel_id=1, replica_groups=mesh['segment'=8,'row'=32] {'row'}, dimensions={0} | all-to-all | bytes 524288 | tf_op jit(solution)/shard_map/all_to_all | solution.py:14
  85.3 0.0 collective-permute-done.1.gram_ref
  85.4 16.0 %all_to_all.43 = f32[32,16,128]{2,1,0:T(8,128)S(1)} all-to-all(f32[32,16,128]{2,1,0:T(8,128)S(1)} %broadcast_in_dim.16), channel_id=1, replica_groups=mesh['segment'=8,'row'=32] {'row'}, dimensions={0} | all-to-all | bytes 524288 | tf_op jit(solution)/shard_map/all_to_all | solution.py:14
  101.4 1.6 %shard_map.51 = (f32[512,128]{1,0:T(8,128)S(1)}, f32[256,128]{1,0:T(8,128)}, f32[1,128]{1,0:T(1,128)S(1)}) custom-call(f32[512,128]{1,0:T(8,128)S(1)} %bitcast.10, f32[1792,128]{1,0:T(8,128)S(1)} %collective-permute-done.1.gram_ref, f32[256,512]{1,0:T(8,128)S(1)} %collective-permute-done.next_ref.basis_ref, f32[256,128]{1,0:T(8,128)S(1)} %get-tuple-element.20.vec_ref), custom_call_target="tpu_custom_call" | custom-call | tf_op jit(solution)/shard_map/pallas_call | solution.py:178
  103.0 0.0 collective-permute-start.2
  103.0 0.6 broadcast_in_dim.17
  103.6 4.0 %all-to-all-start.6 = ((f32[32,1,128]{2,1,0:T(1,128)}), f32[32,1,128]{2,1,0:T(1,128)S(1)}, u32[]{:S(2)}, u32[]{:S(2)}) async-start(f32[32,1,128]{2,1,0:T(1,128)} %broadcast_in_dim.17), calls=%async_computation.6 | async-start | bytes 32768 | tf_op jit(solution)/shard_map/all_to_all | solution.py:14
  107.6 1.1 collective-permute-done.2
  108.8 0.7 constant_dynamic-update-slice_fusion
  109.5 7.7 %all-to-all-done.6 = f32[32,1,128]{2,1,0:T(1,128)S(1)} async-done(((f32[32,1,128]{2,1,0:T(1,128)}), f32[32,1,128]{2,1,0:T(1,128)S(1)}, u32[]{:S(2)}, u32[]{:S(2)}) %all-to-all-start.6) | async-done | bytes 16416 | tf_op jit(solution)/shard_map/all_to_all | solution.py:14
  117.2 0.5 multiply_sqrt_fusion
  (6 shorter events, 0.2 us)
Async XLA Ops:
  0.6 7.0 %copy-start = (f32[256,512]{1,0:T(8,128)S(1)}, f32[256,512]{1,0:T(8,128)}, u32[]{:S(2)}) copy-start(f32[256,512]{1,0:T(8,128)} %basis_ref.1) | copy-start | bytes 1572868
  3.3 18.0 %all-to-all-start = ((f32[4,448,128]{2,1,0:T(8,128)}), f32[4,448,128]{2,1,0:T(8,128)S(1)}, u32[]{:S(2)}, u32[]{:S(2)}) async-start(f32[4,448,128]{2,1,0:T(8,128)} %bitcast), calls=%async_computation | async-start | bytes 1835008 | tf_op jit(solution)/shard_map/all_to_all | solution.py:14
  7.6 13.7 %collective-permute-start = (f32[256,512]{1,0:T(8,128)S(1)}, f32[256,512]{1,0:T(8,128)S(1)}, u32[]{:S(2)}, u32[]{:S(2)}) collective-permute-start(f32[256,512]{1,0:T(8,128)S(1)} %copy-done), channel_id=1, source_target_pairs={{0,224},{32,0},{64,32},{96,64},{128,96},{160,128},{192,160},{224,1... | collective-permute-start | bytes 1572872 | tf_op jit(solution)/shard_map/ppermute | solution.py:37
  21.4 44.0 %copy-start.1 = (f32[256,128]{1,0:T(8,128)S(1)}, f32[256,128]{1,0:T(8,128)}, u32[]{:S(2)}) copy-start(f32[256,128]{1,0:T(8,128)} %vec_ref.1) | copy-start | bytes 393220
  65.4 20.0 %collective-permute-start.1 = (f32[1792,128]{1,0:T(8,128)S(1)}, f32[1792,128]{1,0:T(8,128)S(1)}, u32[]{:S(2)}, u32[]{:S(2)}) collective-permute-start(f32[1792,128]{1,0:T(8,128)S(1)} %bitcast.8), channel_id=1, source_target_pairs={{0,224},{32,0},{64,32},{96,64},{128,96},{160,128},{192,160},{224,1... | collective-permute-start | bytes 2752520 | tf_op jit(solution)/shard_map/ppermute | solution.py:37
  103.0 5.8 %collective-permute-start.2 = (f32[512,128]{1,0:T(8,128)S(1)}, f32[512,128]{1,0:T(8,128)S(1)}, u32[]{:S(2)}, u32[]{:S(2)}) collective-permute-start(f32[512,128]{1,0:T(8,128)S(1)} %get-tuple-element.24), channel_id=1, source_target_pairs={{0,32},{32,64},{64,96},{96,128},{128,160},{160,192},{192,224},{224... | collective-permute-start | bytes 786440 | tf_op jit(solution)/shard_map/ppermute | solution.py:37
  103.6 13.7 %all-to-all-start.6 = ((f32[32,1,128]{2,1,0:T(1,128)}), f32[32,1,128]{2,1,0:T(1,128)S(1)}, u32[]{:S(2)}, u32[]{:S(2)}) async-start(f32[32,1,128]{2,1,0:T(1,128)} %broadcast_in_dim.17), calls=%async_computation.6 | async-start | bytes 32768 | tf_op jit(solution)/shard_map/all_to_all | solution.py:14

commit v5 on v4

--- a/solution.py
+++ b/solution.py
@@ -96,17 +96,16 @@
 
 
 def turn_kernel(
-    got_ref, basis_ref, vec_ref, next_ref, vec_out, first_out, coeff_hbm, here_ref, zero_ref, done
+    got_ref, basis_ref, vec_ref, next_ref, here_ref, vec_out, first_out, coeff_hbm, zero_ref, done
 ):
     size = basis_ref.shape[1]
     width = vec_ref.shape[1]
-    sections = coeff_hbm.shape[1] // width
     zero_ref[...] = jnp.zeros_like(zero_ref)
     fills = [
         pltpu.make_async_copy(
             zero_ref, coeff_hbm.at[:, b * width:(b + 1) * width], done.at[b]
         )
-        for b in range(sections)
+        for b in range(coeff_hbm.shape[1] // width)
     ]
     for fill in fills:
         fill.start()
@@ -114,15 +113,9 @@
     here_ref[...] = here
     vec = vec_ref[...] - product(halves(basis_ref[...]), halves(here))
     vec_out[...] = vec
+    first_out[...] = product(halves(next_ref[...].T), halves(vec))
     for fill in fills:
         fill.wait()
-    column = pl.multiple_of(lax.axis_index("segment") * width, width)
-    own = pltpu.make_async_copy(
-        here_ref, coeff_hbm.at[:, pl.ds(column, width)], done.at[sections]
-    )
-    own.start()
-    first_out[...] = product(halves(next_ref[...].T), halves(vec))
-    own.wait()
 
 
 def end_kernel(first_ref, gram_ref, basis_ref, vec_ref, there_ref, vec_out, squares_ref):
@@ -164,17 +157,16 @@
     blocks = exchange(sent.reshape(len(near[0]), -1, TILE), "row", near)
     mine, onward = lax.optimization_barrier((blocks.sum(axis=0), onward))
     got = gathered(mine, near, far)
-    gram_next = shifted(got, "segment", -1)
-    vec, first, coeff = local(
+    gram_next = shifted(got[:share], "segment", -1)
+    here, vec, first, coeff = local(
         turn_kernel, (pltpu.VMEM,) * 4,
-        [(pltpu.VMEM, (rows, width)), (pltpu.VMEM, (size, width)),
-         (hbm, (size, width * sections))],
-        (pltpu.VMEM((size, width), jnp.float32), pltpu.VMEM((size, width), jnp.float32),
-         pltpu.SemaphoreType.DMA((sections + 1,))),
+        [(pltpu.VMEM, (size, width)), (pltpu.VMEM, (rows, width)),
+         (pltpu.VMEM, (size, width)), (hbm, (size, width * sections))],
+        (pltpu.VMEM((size, width), jnp.float32), pltpu.SemaphoreType.DMA((sections,))),
     )(got, basis, snapshots, onward)
     blocks = exchange(first.reshape(lines, -1, TILE), "row")
-    blocks, gram_next = lax.optimization_barrier((blocks, gram_next))
-    first = exchange(jnp.broadcast_to(blocks.sum(axis=0), blocks.shape), "row")
+    mine, gram_next = lax.optimization_barrier((blocks.sum(axis=0), gram_next))
+    first = exchange(jnp.broadcast_to(mine, blocks.shape), "row")
     there, vec, squares = local(
         end_kernel, (pltpu.VMEM,) * 4,
         [(pltpu.VMEM, (size, width)), (pltpu.VMEM, (rows, width)), (pltpu.VMEM, (1, width))],
@@ -182,6 +174,7 @@
 
     arrived = shifted(there, "segment", 1)
     blocks = exchange(jnp.broadcast_to(squares, (lines, width)), "row")
+    coeff = lax.dynamic_update_slice(coeff, here, (jnp.int32(0), position * width))
     before = (position - 1) % sections
     coeff = lax.dynamic_update_slice(coeff, arrived, (jnp.int32(0), before * width))
     blocks, coeff = lax.optimization_barrier((blocks, coeff))

time: 120 us -> 120 us (level)
  transfers between devices with their start and end apart: 5 -> 5, of which waited for: 3 -> 3; matrix products, arithmetic and copies ran while one was open for 1% -> 2% of each run, Pallas kernels for 3% -> 2%
where the time goes in v5:
time: 120 us; the launch traced here: 118 us
  blocking collectives  76.5 us (64%)
  waiting for transfers between devices  22.6 us (19%)
  starting transfers between devices  8.32 us (7%)
  Pallas kernels  6.92 us (6%)
  local copies, waits for them, and re-layouts  2.19 us (2%)
    all_to_all x5, blocking collectives, exchange(): lax.all_to_all(blocks, axis, split_axis=0, concat_axis=0, axis_index_grou...  76.5 us
    all_to_all x2, waiting for transfers between devices, exchange(): lax.all_to_all(blocks, axis, split_axis=0, concat_axis=0, axis_index_grou...  22.1 us
    all_to_all x2, starting transfers between devices, exchange(): lax.all_to_all(blocks, axis, split_axis=0, concat_axis=0, axis_index_grou...  8.3 us
    pallas_call x1, Pallas kernels, per_device(): local(start_kernel, (hbm, hbm), [(pltpu.VMEM, (share + size, TILE))], (pl...  2.69 us
    pallas_call x1, Pallas kernels, per_device(): local(turn_kernel, (pltpu.VMEM,) * 4, [(pltpu.VMEM, (size, width)), (pltp...  2.66 us
  transfers between devices with their start and end apart: 5, of which 3 were waited for; matrix products, arithmetic and copies ran while one was open for 2% of the time, Pallas kernels for 2%

profile of v5, /device:TPU:8, one launch (start us, length us, event | category | flops | bytes accessed | tf_op | source)
XLA Modules:
  0.0 117.9 jit_solution(5085825248951123665)
XLA Ops:
  0.6 0.0 copy-start
  0.6 2.7 %shard_map.49 = f32[1792,128]{1,0:T(8,128)} custom-call(f32[256,512]{1,0:T(8,128)} %basis_ref.1, f32[256,128]{1,0:T(8,128)} %vec_ref.1), custom_call_target="tpu_custom_call" | custom-call | tf_op jit(solution)/shard_map/pallas_call | solution.py:152
  3.3 4.3 %all-to-all-start = ((f32[4,448,128]{2,1,0:T(8,128)}), f32[4,448,128]{2,1,0:T(8,128)S(1)}, u32[]{:S(2)}, u32[]{:S(2)}) async-start(f32[4,448,128]{2,1,0:T(8,128)} %bitcast), calls=%async_computation | async-start | bytes 1835008 | tf_op jit(solution)/shard_map/all_to_all | solution.py:14
  7.6 0.0 copy-done
  7.6 0.0 collective-permute-start
  7.6 13.7 %all-to-all-done = f32[4,448,128]{2,1,0:T(8,128)S(1)} async-done(((f32[4,448,128]{2,1,0:T(8,128)}), f32[4,448,128]{2,1,0:T(8,128)S(1)}, u32[]{:S(2)}, u32[]{:S(2)}) %all-to-all-start) | async-done | bytes 917536 | tf_op jit(solution)/shard_map/all_to_all | solution.py:14
  21.3 0.1 reduce_sum.36
  21.4 0.0 collective-permute-done.next_ref.basis_ref
  21.4 18.4 %all_to_all.39 = f32[8,56,128]{2,1,0:T(8,128)S(1)} all-to-all(f32[8,56,128]{2,1,0:T(8,128)S(1)} %bitcast.13), channel_id=1, replica_groups={{0,4,8,12,16,20,24,28},{1,5,9,13,17,21,25,29},{2,6,10,14,18,22,26,30},{..., dimensions={0} | all-to-all | bytes 458752 | tf_op jit(solution)/shard_map/all_to_all | solution.py:14
  39.8 12.5 %all_to_all.40 = f32[8,56,128]{2,1,0:T(8,128)S(1)} all-to-all(f32[8,56,128]{2,1,0:T(8,128)S(1)} %broadcast_in_dim.14), channel_id=1, replica_groups={{0,4,8,12,16,20,24,28},{1,5,9,13,17,21,25,29},{2,6,10,14,18,22,26,30},{..., dimensions={0} | all-to-all | bytes 458752 | tf_op jit(solution)/shard_map/all_to_all | solution.py:14
  52.4 0.0 copy-start.1
  52.4 0.1 broadcast_in_dim.15
  52.4 12.8 %all_to_all.41 = f32[4,448,128]{2,1,0:T(8,128)S(1)} all-to-all(f32[4,448,128]{2,1,0:T(8,128)S(1)} %broadcast_in_dim.15), channel_id=1, replica_groups={{0,1,2,3},{4,5,6,7},{8,9,10,11},{12,13,14,15},{16,17,18,19},{20,21,22,2..., dimensions={0} | all-to-all | bytes 1835008 | tf_op jit(solution)/shard_map/all_to_all | solution.py:14
  65.3 0.0 collective-permute-start.1
  65.3 0.0 copy-done.1
  65.3 2.7 %shard_map.50 = (f32[512,128]{1,0:T(8,128)S(1)}, f32[256,128]{1,0:T(8,128)S(1)}, f32[512,128]{1,0:T(8,128)S(1)}, f32[512,1024]{1,0:T(8,128)}) custom-call(f32[1792,128]{1,0:T(8,128)S(1)} %bitcast.9, f32[256,512]{1,0:T(8,128)S(1)} %copy-done, f32[256,128]{1,0:T(8,128)S(1)} %copy-done.1, f32[256,512]{1,0:T(8,128)S(1)} %collective-permute-done.next_ref.basis_ref), custom_call_target="tpu_custom_call" | custom-call | tf_op jit(solution)/shard_map/pallas_call | solution.py:161
  68.0 16.8 %all_to_all.42 = f32[32,16,128]{2,1,0:T(8,128)S(1)} all-to-all(f32[32,16,128]{2,1,0:T(8,128)S(1)} %bitcast.11), channel_id=1, replica_groups=mesh['segment'=8,'row'=32] {'row'}, dimensions={0} | all-to-all | bytes 524288 | tf_op jit(solution)/shard_map/all_to_all | solution.py:14
  84.9 0.0 collective-permute-done.1.gram_ref
  84.9 16.0 %all_to_all.43 = f32[32,16,128]{2,1,0:T(8,128)S(1)} all-to-all(f32[32,16,128]{2,1,0:T(8,128)S(1)} %broadcast_in_dim.16), channel_id=1, replica_groups=mesh['segment'=8,'row'=32] {'row'}, dimensions={0} | all-to-all | bytes 524288 | tf_op jit(solution)/shard_map/all_to_all | solution.py:14
  100.9 1.6 %shard_map.51 = (f32[512,128]{1,0:T(8,128)S(1)}, f32[256,128]{1,0:T(8,128)}, f32[1,128]{1,0:T(1,128)S(1)}) custom-call(f32[512,128]{1,0:T(8,128)S(1)} %bitcast.10, f32[1280,128]{1,0:T(8,128)S(1)} %collective-permute-done.1.gram_ref, f32[256,512]{1,0:T(8,128)S(1)} %collective-permute-done.next_ref.basis_ref, f32[256,128]{1,0:T(8,128)S(1)} %get-tuple-element.21.vec_ref), custom_call_target="tpu_custom_call" | custom-call | tf_op jit(solution)/shard_map/pallas_call | solution.py:170
  102.4 0.0 collective-permute-start.2
  102.4 0.7 constant_dynamic-update-slice_fusion.1
  103.1 0.6 broadcast_in_dim.17
  103.8 4.0 %all-to-all-start.6 = ((f32[32,1,128]{2,1,0:T(1,128)}), f32[32,1,128]{2,1,0:T(1,128)S(1)}, u32[]{:S(2)}, u32[]{:S(2)}) async-start(f32[32,1,128]{2,1,0:T(1,128)} %broadcast_in_dim.17), calls=%async_computation.6 | async-start | bytes 32768 | tf_op jit(solution)/shard_map/all_to_all | solution.py:14
  107.8 0.5 collective-permute-done.2
  108.2 0.7 constant_dynamic-update-slice_fusion
  108.9 8.4 %all-to-all-done.6 = f32[32,1,128]{2,1,0:T(1,128)S(1)} async-done(((f32[32,1,128]{2,1,0:T(1,128)}), f32[32,1,128]{2,1,0:T(1,128)S(1)}, u32[]{:S(2)}, u32[]{:S(2)}) %all-to-all-start.6) | async-done | bytes 16416 | tf_op jit(solution)/shard_map/all_to_all | solution.py:14
  117.4 0.5 multiply_sqrt_fusion
  (6 shorter events, 0.2 us)
Async XLA Ops:
  0.6 7.0 %copy-start = (f32[256,512]{1,0:T(8,128)S(1)}, f32[256,512]{1,0:T(8,128)}, u32[]{:S(2)}) copy-start(f32[256,512]{1,0:T(8,128)} %basis_ref.1) | copy-start | bytes 1572868
  3.3 18.0 %all-to-all-start = ((f32[4,448,128]{2,1,0:T(8,128)}), f32[4,448,128]{2,1,0:T(8,128)S(1)}, u32[]{:S(2)}, u32[]{:S(2)}) async-start(f32[4,448,128]{2,1,0:T(8,128)} %bitcast), calls=%async_computation | async-start | bytes 1835008 | tf_op jit(solution)/shard_map/all_to_all | solution.py:14
  7.6 13.7 %collective-permute-start = (f32[256,512]{1,0:T(8,128)S(1)}, f32[256,512]{1,0:T(8,128)S(1)}, u32[]{:S(2)}, u32[]{:S(2)}) collective-permute-start(f32[256,512]{1,0:T(8,128)S(1)} %copy-done), channel_id=1, source_target_pairs={{0,224},{32,0},{64,32},{96,64},{128,96},{160,128},{192,160},{224,1... | collective-permute-start | bytes 1572872 | tf_op jit(solution)/shard_map/ppermute | solution.py:37
  52.4 12.9 %copy-start.1 = (f32[256,128]{1,0:T(8,128)S(1)}, f32[256,128]{1,0:T(8,128)}, u32[]{:S(2)}) copy-start(f32[256,128]{1,0:T(8,128)} %vec_ref.1) | copy-start | bytes 393220
  65.3 19.6 %collective-permute-start.1 = (f32[1280,128]{1,0:T(8,128)S(1)}, f32[1280,128]{1,0:T(8,128)S(1)}, u32[]{:S(2)}, u32[]{:S(2)}) collective-permute-start(f32[1280,128]{1,0:T(8,128)S(1)} %slice.4), channel_id=1, source_target_pairs={{0,224},{32,0},{64,32},{96,64},{128,96},{160,128},{192,160},{224,1... | collective-permute-start | bytes 1966088 | tf_op jit(solution)/shard_map/ppermute | solution.py:37
  102.4 5.8 %collective-permute-start.2 = (f32[512,128]{1,0:T(8,128)S(1)}, f32[512,128]{1,0:T(8,128)S(1)}, u32[]{:S(2)}, u32[]{:S(2)}) collective-permute-start(f32[512,128]{1,0:T(8,128)S(1)} %get-tuple-element.26), channel_id=1, source_target_pairs={{0,32},{32,64},{64,96},{96,128},{128,160},{160,192},{192,224},{224... | collective-permute-start | bytes 786440 | tf_op jit(solution)/shard_map/ppermute | solution.py:37
  103.8 13.6 %all-to-all-start.6 = ((f32[32,1,128]{2,1,0:T(1,128)}), f32[32,1,128]{2,1,0:T(1,128)S(1)}, u32[]{:S(2)}, u32[]{:S(2)}) async-start(f32[32,1,128]{2,1,0:T(1,128)} %broadcast_in_dim.17), calls=%async_computation.6 | async-start | bytes 32768 | tf_op jit(solution)/shard_map/all_to_all | solution.py:14

commit v6 on v5

--- a/solution.py
+++ b/solution.py
@@ -95,27 +95,13 @@
     return 2.0 * first - jnp.concatenate(rows, axis=0)
 
 
-def turn_kernel(
-    got_ref, basis_ref, vec_ref, next_ref, here_ref, vec_out, first_out, coeff_hbm, zero_ref, done
-):
+def turn_kernel(got_ref, basis_ref, vec_ref, next_ref, here_ref, vec_out, first_out):
     size = basis_ref.shape[1]
-    width = vec_ref.shape[1]
-    zero_ref[...] = jnp.zeros_like(zero_ref)
-    fills = [
-        pltpu.make_async_copy(
-            zero_ref, coeff_hbm.at[:, b * width:(b + 1) * width], done.at[b]
-        )
-        for b in range(coeff_hbm.shape[1] // width)
-    ]
-    for fill in fills:
-        fill.start()
     here = both(got_ref[got_ref.shape[0] - size:], got_ref, size)
     here_ref[...] = here
     vec = vec_ref[...] - product(halves(basis_ref[...]), halves(here))
     vec_out[...] = vec
     first_out[...] = product(halves(next_ref[...].T), halves(vec))
-    for fill in fills:
-        fill.wait()
 
 
 def end_kernel(first_ref, gram_ref, basis_ref, vec_ref, there_ref, vec_out, squares_ref):
@@ -158,15 +144,16 @@
     mine, onward = lax.optimization_barrier((blocks.sum(axis=0), onward))
     got = gathered(mine, near, far)
     gram_next = shifted(got[:share], "segment", -1)
-    here, vec, first, coeff = local(
+    here, vec, first = local(
         turn_kernel, (pltpu.VMEM,) * 4,
-        [(pltpu.VMEM, (size, width)), (pltpu.VMEM, (rows, width)),
-         (pltpu.VMEM, (size, width)), (hbm, (size, width * sections))],
-        (pltpu.VMEM((size, width), jnp.float32), pltpu.SemaphoreType.DMA((sections,))),
+        [(pltpu.VMEM, (size, width)), (pltpu.VMEM, (rows, width)), (pltpu.VMEM, (size, width))],
     )(got, basis, snapshots, onward)
+    coeff = jnp.zeros((size, width * sections), jnp.float32)
+    coeff = lax.dynamic_update_slice(coeff, here, (jnp.int32(0), position * width))
     blocks = exchange(first.reshape(lines, -1, TILE), "row")
-    mine, gram_next = lax.optimization_barrier((blocks.sum(axis=0), gram_next))
+    mine, coeff = lax.optimization_barrier((blocks.sum(axis=0), coeff))
     first = exchange(jnp.broadcast_to(mine, blocks.shape), "row")
+    first, gram_next = lax.optimization_barrier((first, gram_next))
     there, vec, squares = local(
         end_kernel, (pltpu.VMEM,) * 4,
         [(pltpu.VMEM, (size, width)), (pltpu.VMEM, (rows, width)), (pltpu.VMEM, (1, width))],
@@ -174,7 +161,6 @@
 
     arrived = shifted(there, "segment", 1)
     blocks = exchange(jnp.broadcast_to(squares, (lines, width)), "row")
-    coeff = lax.dynamic_update_slice(coeff, here, (jnp.int32(0), position * width))
     before = (position - 1) % sections
     coeff = lax.dynamic_update_slice(coeff, arrived, (jnp.int32(0), before * width))
     blocks, coeff = lax.optimization_barrier((blocks, coeff))

time: 120 us -> 118 us (0.983)
  blocking collectives: 76.5 us -> 43.9 us
  waiting for transfers between devices: 22.6 us -> 43.6 us
  starting transfers between devices: 8.32 us -> 15.9 us
  local copies, waits for them, and re-layouts: 2.19 us -> 4.46 us
    all_to_all x5 -> x3, blocking collectives: 76.5 us -> 43.9 us  [exchange(): lax.all_to_all(blocks, axis, split_axis=0, concat_axis=0, axis_index_grou...]
    all_to_all x2 -> x4, waiting for transfers between devices: 22.1 us -> 42.2 us  [exchange(): lax.all_to_all(blocks, axis, split_axis=0, concat_axis=0, axis_index_grou...]
    all_to_all x2 -> x4, starting transfers between devices: 8.3 us -> 15.8 us  [exchange(): lax.all_to_all(blocks, axis, split_axis=0, concat_axis=0, axis_index_grou...]
    broadcast_in_dim x0 -> x1, local copies, waits for them, and re-layouts: none -> 1.58 us  [per_device(): coeff = jnp.zeros((size, width * sections), jnp.float32)]
  transfers between devices with their start and end apart: 5 -> 7, of which waited for: 3 -> 5; matrix products, arithmetic and copies ran while one was open for 2% -> 4% of each run, Pallas kernels for 2% -> 0%
where the time goes in v6:
time: 118 us; the launch traced here: 115 us
  blocking collectives  43.9 us (37%)
  waiting for transfers between devices  43.6 us (37%)
  starting transfers between devices  15.9 us (13%)
  Pallas kernels  6.26 us (5%)
  local copies, waits for them, and re-layouts  4.46 us (4%)
    all_to_all x3, blocking collectives, exchange(): lax.all_to_all(blocks, axis, split_axis=0, concat_axis=0, axis_index_grou...  43.9 us
    all_to_all x4, waiting for transfers between devices, exchange(): lax.all_to_all(blocks, axis, split_axis=0, concat_axis=0, axis_index_grou...  42.2 us
    all_to_all x4, starting transfers between devices, exchange(): lax.all_to_all(blocks, axis, split_axis=0, concat_axis=0, axis_index_grou...  15.8 us
    pallas_call x1, Pallas kernels, per_device(): local(start_kernel, (hbm, hbm), [(pltpu.VMEM, (share + size, TILE))], (pl...  2.69 us
  transfers between devices with their start and end apart: 7, of which 5 were waited for; matrix products, arithmetic and copies ran while one was open for 4% of the time, Pallas kernels for 0%

profile of v6, /device:TPU:8, one launch (start us, length us, event | category | flops | bytes accessed | tf_op | source)
XLA Modules:
  0.0 115.5 jit_solution(3127386152340615693)
XLA Ops:
  0.6 0.0 copy-start
  0.6 2.7 %shard_map.49 = f32[1792,128]{1,0:T(8,128)} custom-call(f32[256,512]{1,0:T(8,128)} %basis_ref.1, f32[256,128]{1,0:T(8,128)} %vec_ref.1), custom_call_target="tpu_custom_call" | custom-call | tf_op jit(solution)/shard_map/pallas_call | solution.py:138
  3.3 4.3 %all-to-all-start = ((f32[4,448,128]{2,1,0:T(8,128)}), f32[4,448,128]{2,1,0:T(8,128)S(1)}, u32[]{:S(2)}, u32[]{:S(2)}) async-start(f32[4,448,128]{2,1,0:T(8,128)} %bitcast), calls=%async_computation | async-start | bytes 1835008 | tf_op jit(solution)/shard_map/all_to_all | solution.py:14
  7.6 0.0 copy-done
  7.6 0.0 collective-permute-start
  7.6 13.7 %all-to-all-done = f32[4,448,128]{2,1,0:T(8,128)S(1)} async-done(((f32[4,448,128]{2,1,0:T(8,128)}), f32[4,448,128]{2,1,0:T(8,128)S(1)}, u32[]{:S(2)}, u32[]{:S(2)}) %all-to-all-start) | async-done | bytes 917536 | tf_op jit(solution)/shard_map/all_to_all | solution.py:14
  21.4 0.0 collective-permute-done.next_ref.basis_ref
  21.4 0.0 copy-start.1
  21.4 18.5 %all_to_all.39 = f32[8,56,128]{2,1,0:T(8,128)S(1)} all-to-all(f32[8,56,128]{2,1,0:T(8,128)S(1)} %bitcast.12), channel_id=1, replica_groups={{0,4,8,12,16,20,24,28},{1,5,9,13,17,21,25,29},{2,6,10,14,18,22,26,30},{..., dimensions={0} | all-to-all | bytes 458752 | tf_op jit(solution)/shard_map/all_to_all | solution.py:14
  40.0 12.5 %all_to_all.40 = f32[8,56,128]{2,1,0:T(8,128)S(1)} all-to-all(f32[8,56,128]{2,1,0:T(8,128)S(1)} %broadcast_in_dim.17), channel_id=1, replica_groups={{0,4,8,12,16,20,24,28},{1,5,9,13,17,21,25,29},{2,6,10,14,18,22,26,30},{..., dimensions={0} | all-to-all | bytes 458752 | tf_op jit(solution)/shard_map/all_to_all | solution.py:14
  52.5 0.1 broadcast_in_dim.18
  52.6 12.8 %all_to_all.41 = f32[4,448,128]{2,1,0:T(8,128)S(1)} all-to-all(f32[4,448,128]{2,1,0:T(8,128)S(1)} %broadcast_in_dim.18), channel_id=1, replica_groups={{0,1,2,3},{4,5,6,7},{8,9,10,11},{12,13,14,15},{16,17,18,19},{20,21,22,2..., dimensions={0} | all-to-all | bytes 1835008 | tf_op jit(solution)/shard_map/all_to_all | solution.py:14
  65.4 0.0 copy-done.1
  65.4 2.0 %shard_map.50 = (f32[512,128]{1,0:T(8,128)S(1)}, f32[256,128]{1,0:T(8,128)S(1)}, f32[512,128]{1,0:T(8,128)}) custom-call(f32[1792,128]{1,0:T(8,128)S(1)} %bitcast.8, f32[256,512]{1,0:T(8,128)S(1)} %copy-done, f32[256,128]{1,0:T(8,128)S(1)} %copy-done.1, f32[256,512]{1,0:T(8,128)S(1)} %collective-permute-done.next_ref.basis_ref), custom_call_target="tpu_custom_call" | custom-call | tf_op jit(solution)/shard_map/pallas_call | solution.py:147
  67.4 3.9 %all-to-all-start.4 = ((f32[32,16,128]{2,1,0:T(8,128)}), f32[32,16,128]{2,1,0:T(8,128)S(1)}, u32[]{:S(2)}, u32[]{:S(2)}) async-start(f32[32,16,128]{2,1,0:T(8,128)} %bitcast.4), calls=%async_computation.4 | async-start | bytes 524288 | tf_op jit(solution)/shard_map/all_to_all | solution.py:14
  71.3 0.0 collective-permute-start.1
  71.4 1.6 %broadcast_in_dim.19 = f32[512,1024]{1,0:T(8,128)} broadcast(f32[]{:T(128)} %constant.11.clone.1), dimensions={} | broadcast | bytes 2097156 | tf_op jit(solution)/shard_map/broadcast_in_dim | solution.py:151
  72.9 0.7 constant_dynamic-update-slice_fusion.1
  73.7 9.3 %all-to-all-done.4 = f32[32,16,128]{2,1,0:T(8,128)S(1)} async-done(((f32[32,16,128]{2,1,0:T(8,128)}), f32[32,16,128]{2,1,0:T(8,128)S(1)}, u32[]{:S(2)}, u32[]{:S(2)}) %all-to-all-start.4) | async-done | bytes 262176 | tf_op jit(solution)/shard_map/all_to_all | solution.py:14
  83.0 0.7 broadcast_in_dim.20
  83.7 3.9 %all-to-all-start.5 = ((f32[32,16,128]{2,1,0:T(8,128)}), f32[32,16,128]{2,1,0:T(8,128)S(1)}, u32[]{:S(2)}, u32[]{:S(2)}) async-start(f32[32,16,128]{2,1,0:T(8,128)} %broadcast_in_dim.20), calls=%async_computation.5 | async-start | bytes 524288 | tf_op jit(solution)/shard_map/all_to_all | solution.py:14
  87.6 0.0 collective-permute-done.1.gram_ref
  87.6 11.7 %all-to-all-done.5 = f32[32,16,128]{2,1,0:T(8,128)S(1)} async-done(((f32[32,16,128]{2,1,0:T(8,128)}), f32[32,16,128]{2,1,0:T(8,128)S(1)}, u32[]{:S(2)}, u32[]{:S(2)}) %all-to-all-start.5) | async-done | bytes 262176 | tf_op jit(solution)/shard_map/all_to_all | solution.py:14
  99.3 1.6 %shard_map.51 = (f32[512,128]{1,0:T(8,128)S(1)}, f32[256,128]{1,0:T(8,128)}, f32[1,128]{1,0:T(1,128)S(1)}) custom-call(f32[512,128]{1,0:T(8,128)S(1)} %bitcast.10, f32[1280,128]{1,0:T(8,128)S(1)} %collective-permute-done.1.gram_ref, f32[256,512]{1,0:T(8,128)S(1)} %collective-permute-done.next_ref.basis_ref, f32[256,128]{1,0:T(8,128)S(1)} %get-tuple-element.24.vec_ref), custom_call_target="tpu_custom_call" | custom-call | tf_op jit(solution)/shard_map/pallas_call | solution.py:157
  100.9 0.0 collective-permute-start.2
  100.9 0.6 broadcast_in_dim.21
  101.5 3.8 %all-to-all-start.6 = ((f32[32,1,128]{2,1,0:T(1,128)}), f32[32,1,128]{2,1,0:T(1,128)S(1)}, u32[]{:S(2)}, u32[]{:S(2)}) async-start(f32[32,1,128]{2,1,0:T(1,128)} %broadcast_in_dim.21), calls=%async_computation.6 | async-start | bytes 32768 | tf_op jit(solution)/shard_map/all_to_all | solution.py:14
  105.3 1.4 %collective-permute-done.2 = f32[512,128]{1,0:T(8,128)S(1)} collective-permute-done((f32[512,128]{1,0:T(8,128)S(1)}, f32[512,128]{1,0:T(8,128)S(1)}, u32[]{:S(2)}, u32[]{:S(2)}) %collective-permute-start.2) | collective-permute-done | bytes 262176 | tf_op jit(solution)/shard_map/ppermute | solution.py:37
  106.7 0.7 constant_dynamic-update-slice_fusion
  107.4 7.5 %all-to-all-done.6 = f32[32,1,128]{2,1,0:T(1,128)S(1)} async-done(((f32[32,1,128]{2,1,0:T(1,128)}), f32[32,1,128]{2,1,0:T(1,128)S(1)}, u32[]{:S(2)}, u32[]{:S(2)}) %all-to-all-start.6) | async-done | bytes 16416 | tf_op jit(solution)/shard_map/all_to_all | solution.py:14
  114.9 0.5 multiply_sqrt_fusion
  (6 shorter events, 0.2 us)
Async XLA Ops:
  0.6 7.0 %copy-start = (f32[256,512]{1,0:T(8,128)S(1)}, f32[256,512]{1,0:T(8,128)}, u32[]{:S(2)}) copy-start(f32[256,512]{1,0:T(8,128)} %basis_ref.1) | copy-start | bytes 1572868
  3.3 18.0 %all-to-all-start = ((f32[4,448,128]{2,1,0:T(8,128)}), f32[4,448,128]{2,1,0:T(8,128)S(1)}, u32[]{:S(2)}, u32[]{:S(2)}) async-start(f32[4,448,128]{2,1,0:T(8,128)} %bitcast), calls=%async_computation | async-start | bytes 1835008 | tf_op jit(solution)/shard_map/all_to_all | solution.py:14
  7.6 13.7 %collective-permute-start = (f32[256,512]{1,0:T(8,128)S(1)}, f32[256,512]{1,0:T(8,128)S(1)}, u32[]{:S(2)}, u32[]{:S(2)}) collective-permute-start(f32[256,512]{1,0:T(8,128)S(1)} %copy-done), channel_id=1, source_target_pairs={{0,224},{32,0},{64,32},{96,64},{128,96},{160,128},{192,160},{224,1... | collective-permute-start | bytes 1572872 | tf_op jit(solution)/shard_map/ppermute | solution.py:37
  21.4 44.0 %copy-start.1 = (f32[256,128]{1,0:T(8,128)S(1)}, f32[256,128]{1,0:T(8,128)}, u32[]{:S(2)}) copy-start(f32[256,128]{1,0:T(8,128)} %vec_ref.1) | copy-start | bytes 393220
  67.4 15.6 %all-to-all-start.4 = ((f32[32,16,128]{2,1,0:T(8,128)}), f32[32,16,128]{2,1,0:T(8,128)S(1)}, u32[]{:S(2)}, u32[]{:S(2)}) async-start(f32[32,16,128]{2,1,0:T(8,128)} %bitcast.4), calls=%async_computation.4 | async-start | bytes 524288 | tf_op jit(solution)/shard_map/all_to_all | solution.py:14
  71.3 16.3 %collective-permute-start.1 = (f32[1280,128]{1,0:T(8,128)S(1)}, f32[1280,128]{1,0:T(8,128)S(1)}, u32[]{:S(2)}, u32[]{:S(2)}) collective-permute-start(f32[1280,128]{1,0:T(8,128)S(1)} %slice.4), channel_id=1, source_target_pairs={{0,224},{32,0},{64,32},{96,64},{128,96},{160,128},{192,160},{224,1... | collective-permute-start | bytes 1966088 | tf_op jit(solution)/shard_map/ppermute | solution.py:37
  83.7 15.6 %all-to-all-start.5 = ((f32[32,16,128]{2,1,0:T(8,128)}), f32[32,16,128]{2,1,0:T(8,128)S(1)}, u32[]{:S(2)}, u32[]{:S(2)}) async-start(f32[32,16,128]{2,1,0:T(8,128)} %broadcast_in_dim.20), calls=%async_computation.5 | async-start | bytes 524288 | tf_op jit(solution)/shard_map/all_to_all | solution.py:14
  100.9 5.8 %collective-permute-start.2 = (f32[512,128]{1,0:T(8,128)S(1)}, f32[512,128]{1,0:T(8,128)S(1)}, u32[]{:S(2)}, u32[]{:S(2)}) collective-permute-start(f32[512,128]{1,0:T(8,128)S(1)} %get-tuple-element.28), channel_id=1, source_target_pairs={{0,32},{32,64},{64,96},{96,128},{128,160},{160,192},{192,224},{224... | collective-permute-start | bytes 786440 | tf_op jit(solution)/shard_map/ppermute | solution.py:37
  101.5 13.4 %all-to-all-start.6 = ((f32[32,1,128]{2,1,0:T(1,128)}), f32[32,1,128]{2,1,0:T(1,128)S(1)}, u32[]{:S(2)}, u32[]{:S(2)}) async-start(f32[32,1,128]{2,1,0:T(1,128)} %broadcast_in_dim.21), calls=%async_computation.6 | async-start | bytes 32768 | tf_op jit(solution)/shard_map/all_to_all | solution.py:14

commit v7 on v6

--- a/solution.py
+++ b/solution.py
@@ -109,7 +109,8 @@
     there_ref[...] = there
     vec = vec_ref[...] - product(halves(basis_ref[...]), halves(there))
     vec_out[...] = vec
-    squares_ref[...] = jnp.sum(vec * vec, axis=0, keepdims=True)
+    squares = jnp.sum(vec * vec, axis=0, keepdims=True)
+    squares_ref[...] = jnp.broadcast_to(squares[None], squares_ref.shape)
 
 
 def local(kernel, ins, outs, scratch=()):
@@ -153,18 +154,19 @@
     blocks = exchange(first.reshape(lines, -1, TILE), "row")
     mine, coeff = lax.optimization_barrier((blocks.sum(axis=0), coeff))
     first = exchange(jnp.broadcast_to(mine, blocks.shape), "row")
+    first = lax.optimization_barrier(first)
     first, gram_next = lax.optimization_barrier((first, gram_next))
     there, vec, squares = local(
         end_kernel, (pltpu.VMEM,) * 4,
-        [(pltpu.VMEM, (size, width)), (pltpu.VMEM, (rows, width)), (pltpu.VMEM, (1, width))],
+        [(pltpu.VMEM, (size, width)), (pltpu.VMEM, (rows, width)),
+         (pltpu.VMEM, (lines, 1, width))],
     )(first.reshape(-1, TILE), gram_next, onward, vec)
 
     arrived = shifted(there, "segment", 1)
-    blocks = exchange(jnp.broadcast_to(squares, (lines, width)), "row")
+    blocks = exchange(squares, "row")
     before = (position - 1) % sections
     coeff = lax.dynamic_update_slice(coeff, arrived, (jnp.int32(0), before * width))
-    blocks, coeff = lax.optimization_barrier((blocks, coeff))
-    rms = jnp.sqrt(blocks.sum(axis=0) / total_rows)
+    rms = jnp.sqrt(blocks.sum(axis=(0, 1)) / total_rows)
     return (vec, coeff, rms)
 
 

time: 118 us -> 117 us (level)
  blocking collectives: 43.9 us -> 59.1 us
  waiting for transfers between devices: 43.6 us -> 32.8 us
  starting transfers between devices: 15.9 us -> 12 us
  local copies, waits for them, and re-layouts: 4.46 us -> 3.17 us
    all_to_all x3 -> x4, blocking collectives: 43.9 us -> 59.1 us  [exchange(): lax.all_to_all(blocks, axis, split_axis=0, concat_axis=0, axis_index_grou...]
    all_to_all x4 -> x3, waiting for transfers between devices: 42.2 us -> 32.8 us  [exchange(): lax.all_to_all(blocks, axis, split_axis=0, concat_axis=0, axis_index_grou...]
    all_to_all x4 -> x3, starting transfers between devices: 15.8 us -> 12 us  [exchange(): lax.all_to_all(blocks, axis, split_axis=0, concat_axis=0, axis_index_grou...]
    ppermute x3, waiting for transfers between devices: 1.38 us -> 0.01 us  [shifted(): return lax.ppermute(value, axis, pairs)]
  transfers between devices with their start and end apart: 7 -> 6, of which waited for: 5 -> 3; matrix products, arithmetic and copies ran while one was open for 4% -> 3% of each run, Pallas kernels for 0% -> 0%
where the time goes in v7:
time: 117 us; the launch traced here: 115 us
  blocking collectives  59.1 us (51%)
  waiting for transfers between devices  32.8 us (28%)
  starting transfers between devices  12 us (10%)
  Pallas kernels  6.26 us (5%)
  local copies, waits for them, and re-layouts  3.17 us (3%)
    all_to_all x4, blocking collectives, exchange(): lax.all_to_all(blocks, axis, split_axis=0, concat_axis=0, axis_index_grou...  59.1 us
    all_to_all x3, waiting for transfers between devices, exchange(): lax.all_to_all(blocks, axis, split_axis=0, concat_axis=0, axis_index_grou...  32.8 us
    all_to_all x3, starting transfers between devices, exchange(): lax.all_to_all(blocks, axis, split_axis=0, concat_axis=0, axis_index_grou...  12 us
    pallas_call x1, Pallas kernels, per_device(): local(start_kernel, (hbm, hbm), [(pltpu.VMEM, (share + size, TILE))], (pl...  2.69 us
  transfers between devices with their start and end apart: 6, of which 3 were waited for; matrix products, arithmetic and copies ran while one was open for 3% of the time, Pallas kernels for 0%

profile of v7, /device:TPU:8, one launch (start us, length us, event | category | flops | bytes accessed | tf_op | source)
XLA Modules:
  0.0 114.7 jit_solution(2955909622596994699)
XLA Ops:
  0.6 0.0 copy-start
  0.6 2.7 %shard_map.49 = f32[1792,128]{1,0:T(8,128)} custom-call(f32[256,512]{1,0:T(8,128)} %basis_ref.1, f32[256,128]{1,0:T(8,128)} %vec_ref.1), custom_call_target="tpu_custom_call" | custom-call | tf_op jit(solution)/shard_map/pallas_call | solution.py:139
  3.3 4.3 %all-to-all-start = ((f32[4,448,128]{2,1,0:T(8,128)}), f32[4,448,128]{2,1,0:T(8,128)S(1)}, u32[]{:S(2)}, u32[]{:S(2)}) async-start(f32[4,448,128]{2,1,0:T(8,128)} %bitcast), calls=%async_computation | async-start | bytes 1835008 | tf_op jit(solution)/shard_map/all_to_all | solution.py:14
  7.6 0.0 copy-done
  7.6 0.0 collective-permute-start
  7.6 13.7 %all-to-all-done = f32[4,448,128]{2,1,0:T(8,128)S(1)} async-done(((f32[4,448,128]{2,1,0:T(8,128)}), f32[4,448,128]{2,1,0:T(8,128)S(1)}, u32[]{:S(2)}, u32[]{:S(2)}) %all-to-all-start) | async-done | bytes 917536 | tf_op jit(solution)/shard_map/all_to_all | solution.py:14
  21.4 0.0 collective-permute-done.next_ref.basis_ref
  21.4 0.0 copy-start.1
  21.4 18.5 %all_to_all.35 = f32[8,56,128]{2,1,0:T(8,128)S(1)} all-to-all(f32[8,56,128]{2,1,0:T(8,128)S(1)} %bitcast.9), channel_id=1, replica_groups={{0,4,8,12,16,20,24,28},{1,5,9,13,17,21,25,29},{2,6,10,14,18,22,26,30},{..., dimensions={0} | all-to-all | bytes 458752 | tf_op jit(solution)/shard_map/all_to_all | solution.py:14
  40.0 12.5 %all_to_all.36 = f32[8,56,128]{2,1,0:T(8,128)S(1)} all-to-all(f32[8,56,128]{2,1,0:T(8,128)S(1)} %broadcast_in_dim.12), channel_id=1, replica_groups={{0,4,8,12,16,20,24,28},{1,5,9,13,17,21,25,29},{2,6,10,14,18,22,26,30},{..., dimensions={0} | all-to-all | bytes 458752 | tf_op jit(solution)/shard_map/all_to_all | solution.py:14
  52.5 0.1 broadcast_in_dim.13
  52.6 12.8 %all_to_all.37 = f32[4,448,128]{2,1,0:T(8,128)S(1)} all-to-all(f32[4,448,128]{2,1,0:T(8,128)S(1)} %broadcast_in_dim.13), channel_id=1, replica_groups={{0,1,2,3},{4,5,6,7},{8,9,10,11},{12,13,14,15},{16,17,18,19},{20,21,22,2..., dimensions={0} | all-to-all | bytes 1835008 | tf_op jit(solution)/shard_map/all_to_all | solution.py:14
  65.4 0.0 copy-done.1
  65.4 2.0 %shard_map.50 = (f32[512,128]{1,0:T(8,128)S(1)}, f32[256,128]{1,0:T(8,128)S(1)}, f32[512,128]{1,0:T(8,128)}) custom-call(f32[1792,128]{1,0:T(8,128)S(1)} %bitcast.6, f32[256,512]{1,0:T(8,128)S(1)} %copy-done, f32[256,128]{1,0:T(8,128)S(1)} %copy-done.1, f32[256,512]{1,0:T(8,128)S(1)} %collective-permute-done.next_ref.basis_ref), custom_call_target="tpu_custom_call" | custom-call | tf_op jit(solution)/shard_map/pallas_call | solution.py:148
  67.4 3.9 %all-to-all-start.4 = ((f32[32,16,128]{2,1,0:T(8,128)}), f32[32,16,128]{2,1,0:T(8,128)S(1)}, u32[]{:S(2)}, u32[]{:S(2)}) async-start(f32[32,16,128]{2,1,0:T(8,128)} %bitcast.4), calls=%async_computation.4 | async-start | bytes 524288 | tf_op jit(solution)/shard_map/all_to_all | solution.py:14
  71.3 0.0 collective-permute-start.1
  71.4 1.6 %broadcast_in_dim.14 = f32[512,1024]{1,0:T(8,128)} broadcast(f32[]{:T(128)} %constant.11.clone.1), dimensions={} | broadcast | bytes 2097156 | tf_op jit(solution)/shard_map/broadcast_in_dim | solution.py:152
  72.9 0.7 constant_dynamic-update-slice_fusion.1
  73.6 9.3 %all-to-all-done.4 = f32[32,16,128]{2,1,0:T(8,128)S(1)} async-done(((f32[32,16,128]{2,1,0:T(8,128)}), f32[32,16,128]{2,1,0:T(8,128)S(1)}, u32[]{:S(2)}, u32[]{:S(2)}) %all-to-all-start.4) | async-done | bytes 262176 | tf_op jit(solution)/shard_map/all_to_all | solution.py:14
  83.1 15.3 %all_to_all.38 = f32[32,16,128]{2,1,0:T(8,128)S(1)} all-to-all(f32[32,16,128]{2,1,0:T(8,128)S(1)} %broadcast_in_dim.15), channel_id=1, replica_groups=mesh['segment'=8,'row'=32] {'row'}, dimensions={0} | all-to-all | bytes 524288 | tf_op jit(solution)/shard_map/all_to_all | solution.py:14
  98.3 0.0 collective-permute-done.1.gram_ref
  98.3 1.6 %shard_map.51 = (f32[512,128]{1,0:T(8,128)S(1)}, f32[256,128]{1,0:T(8,128)}, f32[32,1,128]{2,1,0:T(1,128)}) custom-call(f32[512,128]{1,0:T(8,128)S(1)} %bitcast.8, f32[1280,128]{1,0:T(8,128)S(1)} %collective-permute-done.1.gram_ref, f32[256,512]{1,0:T(8,128)S(1)} %collective-permute-done.next_ref.basis_ref, f32[256,128]{1,0:T(8,128)S(1)} %get-tuple-element.22.vec_ref), custom_call_target="tpu_custom_call" | custom-call | tf_op jit(solution)/shard_map/pallas_call | solution.py:159
  99.9 0.0 collective-permute-start.2
  99.9 3.8 %all-to-all-start.6 = ((f32[32,1,128]{2,1,0:T(1,128)}), f32[32,1,128]{2,1,0:T(1,128)S(1)}, u32[]{:S(2)}, u32[]{:S(2)}) async-start(f32[32,1,128]{2,1,0:T(1,128)} %get-tuple-element.26), calls=%async_computation.6 | async-start | bytes 32768 | tf_op jit(solution)/shard_map/all_to_all | solution.py:14
  103.7 9.7 %all-to-all-done.6 = f32[32,1,128]{2,1,0:T(1,128)S(1)} async-done(((f32[32,1,128]{2,1,0:T(1,128)}), f32[32,1,128]{2,1,0:T(1,128)S(1)}, u32[]{:S(2)}, u32[]{:S(2)}) %all-to-all-start.6) | async-done | bytes 16416 | tf_op jit(solution)/shard_map/all_to_all | solution.py:14
  113.4 0.1 reduce_sum.39
  113.5 0.5 multiply_sqrt_fusion
  114.0 0.0 collective-permute-done.2
  114.0 0.7 constant_dynamic-update-slice_fusion
  (6 shorter events, 0.2 us)
Async XLA Ops:
  0.6 7.0 %copy-start = (f32[256,512]{1,0:T(8,128)S(1)}, f32[256,512]{1,0:T(8,128)}, u32[]{:S(2)}) copy-start(f32[256,512]{1,0:T(8,128)} %basis_ref.1) | copy-start | bytes 1572868
  3.3 18.0 %all-to-all-start = ((f32[4,448,128]{2,1,0:T(8,128)}), f32[4,448,128]{2,1,0:T(8,128)S(1)}, u32[]{:S(2)}, u32[]{:S(2)}) async-start(f32[4,448,128]{2,1,0:T(8,128)} %bitcast), calls=%async_computation | async-start | bytes 1835008 | tf_op jit(solution)/shard_map/all_to_all | solution.py:14
  7.6 13.7 %collective-permute-start = (f32[256,512]{1,0:T(8,128)S(1)}, f32[256,512]{1,0:T(8,128)S(1)}, u32[]{:S(2)}, u32[]{:S(2)}) collective-permute-start(f32[256,512]{1,0:T(8,128)S(1)} %copy-done), channel_id=1, source_target_pairs={{0,224},{32,0},{64,32},{96,64},{128,96},{160,128},{192,160},{224,1... | collective-permute-start | bytes 1572872 | tf_op jit(solution)/shard_map/ppermute | solution.py:37
  21.4 44.0 %copy-start.1 = (f32[256,128]{1,0:T(8,128)S(1)}, f32[256,128]{1,0:T(8,128)}, u32[]{:S(2)}) copy-start(f32[256,128]{1,0:T(8,128)} %vec_ref.1) | copy-start | bytes 393220
  67.4 15.6 %all-to-all-start.4 = ((f32[32,16,128]{2,1,0:T(8,128)}), f32[32,16,128]{2,1,0:T(8,128)S(1)}, u32[]{:S(2)}, u32[]{:S(2)}) async-start(f32[32,16,128]{2,1,0:T(8,128)} %bitcast.4), calls=%async_computation.4 | async-start | bytes 524288 | tf_op jit(solution)/shard_map/all_to_all | solution.py:14
  71.3 27.0 %collective-permute-start.1 = (f32[1280,128]{1,0:T(8,128)S(1)}, f32[1280,128]{1,0:T(8,128)S(1)}, u32[]{:S(2)}, u32[]{:S(2)}) collective-permute-start(f32[1280,128]{1,0:T(8,128)S(1)} %slice.4), channel_id=1, source_target_pairs={{0,224},{32,0},{64,32},{96,64},{128,96},{160,128},{192,160},{224,1... | collective-permute-start | bytes 1966088 | tf_op jit(solution)/shard_map/ppermute | solution.py:37
  99.9 14.2 %collective-permute-start.2 = (f32[512,128]{1,0:T(8,128)S(1)}, f32[512,128]{1,0:T(8,128)S(1)}, u32[]{:S(2)}, u32[]{:S(2)}) collective-permute-start(f32[512,128]{1,0:T(8,128)S(1)} %get-tuple-element.25), channel_id=1, source_target_pairs={{0,32},{32,64},{64,96},{96,128},{128,160},{160,192},{192,224},{224... | collective-permute-start | bytes 786440 | tf_op jit(solution)/shard_map/ppermute | solution.py:37
  99.9 13.6 %all-to-all-start.6 = ((f32[32,1,128]{2,1,0:T(1,128)}), f32[32,1,128]{2,1,0:T(1,128)S(1)}, u32[]{:S(2)}, u32[]{:S(2)}) async-start(f32[32,1,128]{2,1,0:T(1,128)} %get-tuple-element.26), calls=%async_computation.6 | async-start | bytes 32768 | tf_op jit(solution)/shard_map/all_to_all | solution.py:14

commit v8 on v7

--- a/solution.py
+++ b/solution.py
@@ -7,7 +7,7 @@
 
 
 TILE = 128
-NEAR = 4
+NEAR = 8
 
 
 def exchange(blocks, axis, groups=None):
@@ -47,6 +47,13 @@
         return jnp.dot(x, y, preferred_element_type=jnp.float32)
 
     return once(a[0], b[0]) + (once(a[0], b[1]) + once(a[1], b[0]))
+
+
+def narrow_product(a, b):
+    width = b[0].shape[1]
+    wide = jnp.dot(a[0], jnp.concatenate(b, axis=1), preferred_element_type=jnp.float32)
+    low = jnp.dot(a[1], b[0], preferred_element_type=jnp.float32)
+    return wide[:, :width] + (wide[:, width:] + low)
 
 
 def tiles_of(size):
@@ -91,7 +98,7 @@
     rows = []
     for i in range(count):
         row = jnp.concatenate([part[i, j] for j in range(count)], axis=1)
-        rows.append(product(halves(row), right))
+        rows.append(narrow_product(halves(row), right))
     return 2.0 * first - jnp.concatenate(rows, axis=0)
 
 
@@ -99,15 +106,15 @@
     size = basis_ref.shape[1]
     here = both(got_ref[got_ref.shape[0] - size:], got_ref, size)
     here_ref[...] = here
-    vec = vec_ref[...] - product(halves(basis_ref[...]), halves(here))
+    vec = vec_ref[...] - narrow_product(halves(basis_ref[...]), halves(here))
     vec_out[...] = vec
-    first_out[...] = product(halves(next_ref[...].T), halves(vec))
+    first_out[...] = narrow_product(halves(next_ref[...].T), halves(vec))
 
 
 def end_kernel(first_ref, gram_ref, basis_ref, vec_ref, there_ref, vec_out, squares_ref):
     there = both(first_ref[...], gram_ref, basis_ref.shape[1])
     there_ref[...] = there
-    vec = vec_ref[...] - product(halves(basis_ref[...]), halves(there))
+    vec = vec_ref[...] - narrow_product(halves(basis_ref[...]), halves(there))
     vec_out[...] = vec
     squares = jnp.sum(vec * vec, axis=0, keepdims=True)
     squares_ref[...] = jnp.broadcast_to(squares[None], squares_ref.shape)

time: 117 us -> 115 us (0.983)
  blocking collectives: 59.1 us -> 57.1 us
  starting transfers between devices: 12 us -> 13.5 us
    all_to_all x4, blocking collectives: 59.1 us -> 57.1 us  [exchange(): lax.all_to_all(blocks, axis, split_axis=0, concat_axis=0, axis_index_grou...]
    all_to_all x3, starting transfers between devices: 12 us -> 13.4 us  [exchange(): lax.all_to_all(blocks, axis, split_axis=0, concat_axis=0, axis_index_grou...]
where the time goes in v8:
time: 115 us; the launch traced here: 113 us
  blocking collectives  57.1 us (50%)
  waiting for transfers between devices  32.2 us (28%)
  starting transfers between devices  13.5 us (12%)
  Pallas kernels  5.65 us (5%)
  local copies, waits for them, and re-layouts  3.16 us (3%)
    all_to_all x4, blocking collectives, exchange(): lax.all_to_all(blocks, axis, split_axis=0, concat_axis=0, axis_index_grou...  57.1 us
    all_to_all x3, waiting for transfers between devices, exchange(): lax.all_to_all(blocks, axis, split_axis=0, concat_axis=0, axis_index_grou...  32.2 us
    all_to_all x3, starting transfers between devices, exchange(): lax.all_to_all(blocks, axis, split_axis=0, concat_axis=0, axis_index_grou...  13.4 us
    pallas_call x1, Pallas kernels, per_device(): local(start_kernel, (hbm, hbm), [(pltpu.VMEM, (share + size, TILE))], (pl...  2.69 us
  transfers between devices with their start and end apart: 6, of which 3 were waited for; matrix products, arithmetic and copies ran while one was open for 3% of the time, Pallas kernels for 0%

profile of v8, /device:TPU:8, one launch (start us, length us, event | category | flops | bytes accessed | tf_op | source)
XLA Modules:
  0.0 113.1 jit_solution(3877869295185854276)
XLA Ops:
  0.6 0.0 copy-start
  0.6 2.7 %shard_map.49 = f32[1792,128]{1,0:T(8,128)} custom-call(f32[256,512]{1,0:T(8,128)} %basis_ref.1, f32[256,128]{1,0:T(8,128)} %vec_ref.1), custom_call_target="tpu_custom_call" | custom-call | tf_op jit(solution)/shard_map/pallas_call | solution.py:146
  3.3 5.7 %all-to-all-start = ((f32[8,224,128]{2,1,0:T(8,128)}), f32[8,224,128]{2,1,0:T(8,128)S(1)}, u32[]{:S(2)}, u32[]{:S(2)}) async-start(f32[8,224,128]{2,1,0:T(8,128)} %bitcast), calls=%async_computation | async-start | bytes 1835008 | tf_op jit(solution)/shard_map/all_to_all | solution.py:14
  9.0 0.0 copy-done
  9.0 0.0 copy-start.1
  9.0 0.0 collective-permute-start
  9.0 13.4 %all-to-all-done = f32[8,224,128]{2,1,0:T(8,128)S(1)} async-done(((f32[8,224,128]{2,1,0:T(8,128)}), f32[8,224,128]{2,1,0:T(8,128)S(1)}, u32[]{:S(2)}, u32[]{:S(2)}) %all-to-all-start) | async-done | bytes 917536 | tf_op jit(solution)/shard_map/all_to_all | solution.py:14
  22.4 0.0 collective-permute-done.next_ref.basis_ref
  22.5 16.3 %all_to_all.35 = f32[4,56,128]{2,1,0:T(8,128)S(1)} all-to-all(f32[4,56,128]{2,1,0:T(8,128)S(1)} %bitcast.9), channel_id=1, replica_groups={{0,8,16,24},{1,9,17,25},{2,10,18,26},{3,11,19,27},{4,12,20,28},{5,13,21..., dimensions={0} | all-to-all | bytes 229376 | tf_op jit(solution)/shard_map/all_to_all | solution.py:14
  38.8 10.8 %all_to_all.36 = f32[4,56,128]{2,1,0:T(8,128)S(1)} all-to-all(f32[4,56,128]{2,1,0:T(8,128)S(1)} %broadcast_in_dim.12), channel_id=1, replica_groups={{0,8,16,24},{1,9,17,25},{2,10,18,26},{3,11,19,27},{4,12,20,28},{5,13,21..., dimensions={0} | all-to-all | bytes 229376 | tf_op jit(solution)/shard_map/all_to_all | solution.py:14
  49.6 0.1 broadcast_in_dim.13
  49.7 14.9 %all_to_all.37 = f32[8,224,128]{2,1,0:T(8,128)S(1)} all-to-all(f32[8,224,128]{2,1,0:T(8,128)S(1)} %broadcast_in_dim.13), channel_id=1, replica_groups={{0,1,2,3,4,5,6,7},{8,9,10,11,12,13,14,15},{16,17,18,19,20,21,22,23},{24..., dimensions={0} | all-to-all | bytes 1835008 | tf_op jit(solution)/shard_map/all_to_all | solution.py:14
  64.6 0.0 copy-done.1
  64.6 1.6 %shard_map.50 = (f32[512,128]{1,0:T(8,128)S(1)}, f32[256,128]{1,0:T(8,128)S(1)}, f32[512,128]{1,0:T(8,128)}) custom-call(f32[1792,128]{1,0:T(8,128)S(1)} %bitcast.6, f32[256,512]{1,0:T(8,128)S(1)} %copy-done, f32[256,128]{1,0:T(8,128)S(1)} %copy-done.1, f32[256,512]{1,0:T(8,128)S(1)} %collective-permute-done.next_ref.basis_ref), custom_call_target="tpu_custom_call" | custom-call | tf_op jit(solution)/shard_map/pallas_call | solution.py:155
  66.2 3.9 %all-to-all-start.4 = ((f32[32,16,128]{2,1,0:T(8,128)}), f32[32,16,128]{2,1,0:T(8,128)S(1)}, u32[]{:S(2)}, u32[]{:S(2)}) async-start(f32[32,16,128]{2,1,0:T(8,128)} %bitcast.4), calls=%async_computation.4 | async-start | bytes 524288 | tf_op jit(solution)/shard_map/all_to_all | solution.py:14
  70.1 0.0 collective-permute-start.1
  70.2 1.6 %broadcast_in_dim.14 = f32[512,1024]{1,0:T(8,128)} broadcast(f32[]{:T(128)} %constant.11.clone.1), dimensions={} | broadcast | bytes 2097156 | tf_op jit(solution)/shard_map/broadcast_in_dim | solution.py:159
  71.8 0.7 constant_dynamic-update-slice_fusion.1
  72.5 9.1 %all-to-all-done.4 = f32[32,16,128]{2,1,0:T(8,128)S(1)} async-done(((f32[32,16,128]{2,1,0:T(8,128)}), f32[32,16,128]{2,1,0:T(8,128)S(1)}, u32[]{:S(2)}, u32[]{:S(2)}) %all-to-all-start.4) | async-done | bytes 262176 | tf_op jit(solution)/shard_map/all_to_all | solution.py:14
  81.7 15.1 %all_to_all.38 = f32[32,16,128]{2,1,0:T(8,128)S(1)} all-to-all(f32[32,16,128]{2,1,0:T(8,128)S(1)} %broadcast_in_dim.15), channel_id=1, replica_groups=mesh['segment'=8,'row'=32] {'row'}, dimensions={0} | all-to-all | bytes 524288 | tf_op jit(solution)/shard_map/all_to_all | solution.py:14
  96.8 0.0 collective-permute-done.1.gram_ref
  96.8 1.3 %shard_map.51 = (f32[512,128]{1,0:T(8,128)S(1)}, f32[256,128]{1,0:T(8,128)}, f32[32,1,128]{2,1,0:T(1,128)}) custom-call(f32[512,128]{1,0:T(8,128)S(1)} %bitcast.8, f32[1280,128]{1,0:T(8,128)S(1)} %collective-permute-done.1.gram_ref, f32[256,512]{1,0:T(8,128)S(1)} %collective-permute-done.next_ref.basis_ref, f32[256,128]{1,0:T(8,128)S(1)} %get-tuple-element.22.vec_ref), custom_call_target="tpu_custom_call" | custom-call | tf_op jit(solution)/shard_map/pallas_call | solution.py:166
  98.1 0.0 collective-permute-start.2
  98.1 3.9 %all-to-all-start.6 = ((f32[32,1,128]{2,1,0:T(1,128)}), f32[32,1,128]{2,1,0:T(1,128)S(1)}, u32[]{:S(2)}, u32[]{:S(2)}) async-start(f32[32,1,128]{2,1,0:T(1,128)} %get-tuple-element.26), calls=%async_computation.6 | async-start | bytes 32768 | tf_op jit(solution)/shard_map/all_to_all | solution.py:14
  102.1 9.8 %all-to-all-done.6 = f32[32,1,128]{2,1,0:T(1,128)S(1)} async-done(((f32[32,1,128]{2,1,0:T(1,128)}), f32[32,1,128]{2,1,0:T(1,128)S(1)}, u32[]{:S(2)}, u32[]{:S(2)}) %all-to-all-start.6) | async-done | bytes 16416 | tf_op jit(solution)/shard_map/all_to_all | solution.py:14
  111.8 0.1 reduce_sum.39
  111.9 0.5 multiply_sqrt_fusion
  112.4 0.0 collective-permute-done.2
  112.4 0.7 constant_dynamic-update-slice_fusion
  (6 shorter events, 0.2 us)
Async XLA Ops:
  0.6 8.4 %copy-start = (f32[256,512]{1,0:T(8,128)S(1)}, f32[256,512]{1,0:T(8,128)}, u32[]{:S(2)}) copy-start(f32[256,512]{1,0:T(8,128)} %basis_ref.1) | copy-start | bytes 1572868
  3.3 19.1 %all-to-all-start = ((f32[8,224,128]{2,1,0:T(8,128)}), f32[8,224,128]{2,1,0:T(8,128)S(1)}, u32[]{:S(2)}, u32[]{:S(2)}) async-start(f32[8,224,128]{2,1,0:T(8,128)} %bitcast), calls=%async_computation | async-start | bytes 1835008 | tf_op jit(solution)/shard_map/all_to_all | solution.py:14
  9.0 55.6 %copy-start.1 = (f32[256,128]{1,0:T(8,128)S(1)}, f32[256,128]{1,0:T(8,128)}, u32[]{:S(2)}) copy-start(f32[256,128]{1,0:T(8,128)} %vec_ref.1) | copy-start | bytes 393220
  9.0 13.4 %collective-permute-start = (f32[256,512]{1,0:T(8,128)S(1)}, f32[256,512]{1,0:T(8,128)S(1)}, u32[]{:S(2)}, u32[]{:S(2)}) collective-permute-start(f32[256,512]{1,0:T(8,128)S(1)} %copy-done), channel_id=1, source_target_pairs={{0,224},{32,0},{64,32},{96,64},{128,96},{160,128},{192,160},{224,1... | collective-permute-start | bytes 1572872 | tf_op jit(solution)/shard_map/ppermute | solution.py:37
  66.2 15.4 %all-to-all-start.4 = ((f32[32,16,128]{2,1,0:T(8,128)}), f32[32,16,128]{2,1,0:T(8,128)S(1)}, u32[]{:S(2)}, u32[]{:S(2)}) async-start(f32[32,16,128]{2,1,0:T(8,128)} %bitcast.4), calls=%async_computation.4 | async-start | bytes 524288 | tf_op jit(solution)/shard_map/all_to_all | solution.py:14
  70.1 26.6 %collective-permute-start.1 = (f32[1280,128]{1,0:T(8,128)S(1)}, f32[1280,128]{1,0:T(8,128)S(1)}, u32[]{:S(2)}, u32[]{:S(2)}) collective-permute-start(f32[1280,128]{1,0:T(8,128)S(1)} %slice.4), channel_id=1, source_target_pairs={{0,224},{32,0},{64,32},{96,64},{128,96},{160,128},{192,160},{224,1... | collective-permute-start | bytes 1966088 | tf_op jit(solution)/shard_map/ppermute | solution.py:37
  98.1 14.3 %collective-permute-start.2 = (f32[512,128]{1,0:T(8,128)S(1)}, f32[512,128]{1,0:T(8,128)S(1)}, u32[]{:S(2)}, u32[]{:S(2)}) collective-permute-start(f32[512,128]{1,0:T(8,128)S(1)} %get-tuple-element.25), channel_id=1, source_target_pairs={{0,32},{32,64},{64,96},{96,128},{128,160},{160,192},{192,224},{224... | collective-permute-start | bytes 786440 | tf_op jit(solution)/shard_map/ppermute | solution.py:37
  98.1 13.7 %all-to-all-start.6 = ((f32[32,1,128]{2,1,0:T(1,128)}), f32[32,1,128]{2,1,0:T(1,128)S(1)}, u32[]{:S(2)}, u32[]{:S(2)}) async-start(f32[32,1,128]{2,1,0:T(1,128)} %get-tuple-element.26), calls=%async_computation.6 | async-start | bytes 32768 | tf_op jit(solution)/shard_map/all_to_all | solution.py:14

commit v9 on v8

--- a/solution.py
+++ b/solution.py
@@ -7,7 +7,7 @@
 
 
 TILE = 128
-NEAR = 8
+NEAR = 16
 
 
 def exchange(blocks, axis, groups=None):
@@ -24,10 +24,9 @@
 
 
 def gathered(mine, near, far):
-    blocks = exchange(mine.reshape(len(far[0]), -1, TILE), "row", far)
+    blocks = exchange(jnp.broadcast_to(mine, (len(far[0]), *mine.shape)), "row", far)
     own = blocks.sum(axis=0)
-    blocks = exchange(jnp.broadcast_to(own, blocks.shape), "row", far).reshape(-1, TILE)
-    blocks = exchange(jnp.broadcast_to(blocks, (len(near[0]), *blocks.shape)), "row", near)
+    blocks = exchange(jnp.broadcast_to(own, (len(near[0]), *own.shape)), "row", near)
     return blocks.reshape(-1, TILE)
 
 

time: 115 us -> 127 us (1.10)
  waiting for transfers between devices: 32.2 us -> 41.6 us
  starting transfers between devices: 13.5 us -> 16.9 us
    all_to_all x3, waiting for transfers between devices: 32.2 us -> 41.6 us  [exchange(): lax.all_to_all(blocks, axis, split_axis=0, concat_axis=0, axis_index_grou...]
    all_to_all x3, starting transfers between devices: 13.4 us -> 16.9 us  [exchange(): lax.all_to_all(blocks, axis, split_axis=0, concat_axis=0, axis_index_grou...]
    all_to_all x4 -> x3, blocking collectives: 57.1 us -> 56.5 us  [exchange(): lax.all_to_all(blocks, axis, split_axis=0, concat_axis=0, axis_index_grou...]
  transfers between devices with their start and end apart: 6 -> 6, of which waited for: 3 -> 3; matrix products, arithmetic and copies ran while one was open for 3% -> 2% of each run, Pallas kernels for 0% -> 0%
where the time goes in v9:
time: 127 us; the launch traced here: 125 us
  blocking collectives  56.5 us (44%)
  waiting for transfers between devices  41.6 us (33%)
  starting transfers between devices  16.9 us (13%)
  Pallas kernels  5.65 us (4%)
  local copies, waits for them, and re-layouts  3.16 us (2%)
    all_to_all x3, blocking collectives, exchange(): lax.all_to_all(blocks, axis, split_axis=0, concat_axis=0, axis_index_grou...  56.5 us
    all_to_all x3, waiting for transfers between devices, exchange(): lax.all_to_all(blocks, axis, split_axis=0, concat_axis=0, axis_index_grou...  41.6 us
    all_to_all x3, starting transfers between devices, exchange(): lax.all_to_all(blocks, axis, split_axis=0, concat_axis=0, axis_index_grou...  16.9 us
    pallas_call x1, Pallas kernels, per_device(): local(start_kernel, (hbm, hbm), [(pltpu.VMEM, (share + size, TILE))], (pl...  2.69 us
  transfers between devices with their start and end apart: 6, of which 3 were waited for; matrix products, arithmetic and copies ran while one was open for 2% of the time, Pallas kernels for 0%

profile of v9, /device:TPU:8, one launch (start us, length us, event | category | flops | bytes accessed | tf_op | source)
XLA Modules:
  0.0 125.2 jit_solution(5307502554617957458)
XLA Ops:
  0.6 0.0 copy-start
  0.6 2.7 %shard_map.49 = f32[1792,128]{1,0:T(8,128)} custom-call(f32[256,512]{1,0:T(8,128)} %basis_ref.1, f32[256,128]{1,0:T(8,128)} %vec_ref.1), custom_call_target="tpu_custom_call" | custom-call | tf_op jit(solution)/shard_map/pallas_call | solution.py:145
  3.3 8.5 %all-to-all-start = ((f32[16,112,128]{2,1,0:T(8,128)}), f32[16,112,128]{2,1,0:T(8,128)S(1)}, u32[]{:S(2)}, u32[]{:S(2)}) async-start(f32[16,112,128]{2,1,0:T(8,128)} %bitcast), calls=%async_computation | async-start | bytes 1835008 | tf_op jit(solution)/shard_map/all_to_all | solution.py:14
  11.8 0.0 copy-done
  11.8 0.0 copy-start.1
  11.8 0.0 collective-permute-start
  11.9 22.2 %all-to-all-done = f32[16,112,128]{2,1,0:T(8,128)S(1)} async-done(((f32[16,112,128]{2,1,0:T(8,128)}), f32[16,112,128]{2,1,0:T(8,128)S(1)}, u32[]{:S(2)}, u32[]{:S(2)}) %all-to-all-start) | async-done | bytes 917536 | tf_op jit(solution)/shard_map/all_to_all | solution.py:14
  34.1 0.1 reduce_sum.36
  34.2 0.0 collective-permute-done.next_ref.basis_ref
  34.2 13.9 %all_to_all.30 = f32[2,112,128]{2,1,0:T(8,128)S(1)} all-to-all(f32[2,112,128]{2,1,0:T(8,128)S(1)} %broadcast_in_dim.12), channel_id=1, replica_groups={{0,16},{1,17},{2,18},{3,19},{4,20},{5,21},{6,22},{7,23},{8,24},{9,25},{..., dimensions={0} | all-to-all | bytes 229376 | tf_op jit(solution)/shard_map/all_to_all | solution.py:14
  48.1 0.1 broadcast_in_dim.13
  48.1 27.7 %all_to_all.31 = f32[16,112,128]{2,1,0:T(8,128)S(1)} all-to-all(f32[16,112,128]{2,1,0:T(8,128)S(1)} %broadcast_in_dim.13), channel_id=1, replica_groups={{0,1,2,3,4,5,6,7,8,9,10,11,12,13,14,15},{16,17,18,19,20,21,22,23,24,25,..., dimensions={0} | all-to-all | bytes 1835008 | tf_op jit(solution)/shard_map/all_to_all | solution.py:14
  75.8 0.0 copy-done.1
  75.8 1.6 %shard_map.50 = (f32[512,128]{1,0:T(8,128)S(1)}, f32[256,128]{1,0:T(8,128)S(1)}, f32[512,128]{1,0:T(8,128)}) custom-call(f32[1792,128]{1,0:T(8,128)S(1)} %bitcast.4, f32[256,512]{1,0:T(8,128)S(1)} %copy-done, f32[256,128]{1,0:T(8,128)S(1)} %copy-done.1, f32[256,512]{1,0:T(8,128)S(1)} %collective-permute-done.next_ref.basis_ref), custom_call_target="tpu_custom_call" | custom-call | tf_op jit(solution)/shard_map/pallas_call | solution.py:154
  77.4 4.5 %all-to-all-start.3 = ((f32[32,16,128]{2,1,0:T(8,128)}), f32[32,16,128]{2,1,0:T(8,128)S(1)}, u32[]{:S(2)}, u32[]{:S(2)}) async-start(f32[32,16,128]{2,1,0:T(8,128)} %bitcast.2), calls=%async_computation.3 | async-start | bytes 524288 | tf_op jit(solution)/shard_map/all_to_all | solution.py:14
  82.0 0.0 collective-permute-start.1
  82.1 1.6 %broadcast_in_dim.14 = f32[512,1024]{1,0:T(8,128)} broadcast(f32[]{:T(128)} %constant.11.clone.1), dimensions={} | broadcast | bytes 2097156 | tf_op jit(solution)/shard_map/broadcast_in_dim | solution.py:158
  83.7 0.7 constant_dynamic-update-slice_fusion.1
  84.4 9.6 %all-to-all-done.3 = f32[32,16,128]{2,1,0:T(8,128)S(1)} async-done(((f32[32,16,128]{2,1,0:T(8,128)}), f32[32,16,128]{2,1,0:T(8,128)S(1)}, u32[]{:S(2)}, u32[]{:S(2)}) %all-to-all-start.3) | async-done | bytes 262176 | tf_op jit(solution)/shard_map/all_to_all | solution.py:14
  94.1 14.9 %all_to_all.32 = f32[32,16,128]{2,1,0:T(8,128)S(1)} all-to-all(f32[32,16,128]{2,1,0:T(8,128)S(1)} %broadcast_in_dim.15), channel_id=1, replica_groups=mesh['segment'=8,'row'=32] {'row'}, dimensions={0} | all-to-all | bytes 524288 | tf_op jit(solution)/shard_map/all_to_all | solution.py:14
  109.0 0.0 collective-permute-done.1.gram_ref
  109.0 1.3 %shard_map.51 = (f32[512,128]{1,0:T(8,128)S(1)}, f32[256,128]{1,0:T(8,128)}, f32[32,1,128]{2,1,0:T(1,128)}) custom-call(f32[512,128]{1,0:T(8,128)S(1)} %bitcast.6, f32[1280,128]{1,0:T(8,128)S(1)} %collective-permute-done.1.gram_ref, f32[256,512]{1,0:T(8,128)S(1)} %collective-permute-done.next_ref.basis_ref, f32[256,128]{1,0:T(8,128)S(1)} %get-tuple-element.22.vec_ref), custom_call_target="tpu_custom_call" | custom-call | tf_op jit(solution)/shard_map/pallas_call | solution.py:165
  110.3 0.0 collective-permute-start.2
  110.3 3.8 %all-to-all-start.5 = ((f32[32,1,128]{2,1,0:T(1,128)}), f32[32,1,128]{2,1,0:T(1,128)S(1)}, u32[]{:S(2)}, u32[]{:S(2)}) async-start(f32[32,1,128]{2,1,0:T(1,128)} %get-tuple-element.26), calls=%async_computation.5 | async-start | bytes 32768 | tf_op jit(solution)/shard_map/all_to_all | solution.py:14
  114.2 9.8 %all-to-all-done.5 = f32[32,1,128]{2,1,0:T(1,128)S(1)} async-done(((f32[32,1,128]{2,1,0:T(1,128)}), f32[32,1,128]{2,1,0:T(1,128)S(1)}, u32[]{:S(2)}, u32[]{:S(2)}) %all-to-all-start.5) | async-done | bytes 16416 | tf_op jit(solution)/shard_map/all_to_all | solution.py:14
  123.9 0.1 reduce_sum.39
  124.0 0.5 multiply_sqrt_fusion
  124.5 0.0 collective-permute-done.2
  124.5 0.7 constant_dynamic-update-slice_fusion
  (5 shorter events, 0.1 us)
Async XLA Ops:
  0.6 11.2 %copy-start = (f32[256,512]{1,0:T(8,128)S(1)}, f32[256,512]{1,0:T(8,128)}, u32[]{:S(2)}) copy-start(f32[256,512]{1,0:T(8,128)} %basis_ref.1) | copy-start | bytes 1572868
  3.3 30.8 %all-to-all-start = ((f32[16,112,128]{2,1,0:T(8,128)}), f32[16,112,128]{2,1,0:T(8,128)S(1)}, u32[]{:S(2)}, u32[]{:S(2)}) async-start(f32[16,112,128]{2,1,0:T(8,128)} %bitcast), calls=%async_computation | async-start | bytes 1835008 | tf_op jit(solution)/shard_map/all_to_all | solution.py:14
  11.8 64.0 %copy-start.1 = (f32[256,128]{1,0:T(8,128)S(1)}, f32[256,128]{1,0:T(8,128)}, u32[]{:S(2)}) copy-start(f32[256,128]{1,0:T(8,128)} %vec_ref.1) | copy-start | bytes 393220
  11.8 22.3 %collective-permute-start = (f32[256,512]{1,0:T(8,128)S(1)}, f32[256,512]{1,0:T(8,128)S(1)}, u32[]{:S(2)}, u32[]{:S(2)}) collective-permute-start(f32[256,512]{1,0:T(8,128)S(1)} %copy-done), channel_id=1, source_target_pairs={{0,224},{32,0},{64,32},{96,64},{128,96},{160,128},{192,160},{224,1... | collective-permute-start | bytes 1572872 | tf_op jit(solution)/shard_map/ppermute | solution.py:36
  77.4 16.6 %all-to-all-start.3 = ((f32[32,16,128]{2,1,0:T(8,128)}), f32[32,16,128]{2,1,0:T(8,128)S(1)}, u32[]{:S(2)}, u32[]{:S(2)}) async-start(f32[32,16,128]{2,1,0:T(8,128)} %bitcast.2), calls=%async_computation.3 | async-start | bytes 524288 | tf_op jit(solution)/shard_map/all_to_all | solution.py:14
  82.0 26.9 %collective-permute-start.1 = (f32[1280,128]{1,0:T(8,128)S(1)}, f32[1280,128]{1,0:T(8,128)S(1)}, u32[]{:S(2)}, u32[]{:S(2)}) collective-permute-start(f32[1280,128]{1,0:T(8,128)S(1)} %slice.4), channel_id=1, source_target_pairs={{0,224},{32,0},{64,32},{96,64},{128,96},{160,128},{192,160},{224,1... | collective-permute-start | bytes 1966088 | tf_op jit(solution)/shard_map/ppermute | solution.py:36
  110.3 14.2 %collective-permute-start.2 = (f32[512,128]{1,0:T(8,128)S(1)}, f32[512,128]{1,0:T(8,128)S(1)}, u32[]{:S(2)}, u32[]{:S(2)}) collective-permute-start(f32[512,128]{1,0:T(8,128)S(1)} %get-tuple-element.25), channel_id=1, source_target_pairs={{0,32},{32,64},{64,96},{96,128},{128,160},{160,192},{192,224},{224... | collective-permute-start | bytes 786440 | tf_op jit(solution)/shard_map/ppermute | solution.py:36
  110.3 13.6 %all-to-all-start.5 = ((f32[32,1,128]{2,1,0:T(1,128)}), f32[32,1,128]{2,1,0:T(1,128)S(1)}, u32[]{:S(2)}, u32[]{:S(2)}) async-start(f32[32,1,128]{2,1,0:T(1,128)} %get-tuple-element.26), calls=%async_computation.5 | async-start | bytes 32768 | tf_op jit(solution)/shard_map/all_to_all | solution.py:14

commit v10 on v9

--- a/solution.py
+++ b/solution.py
@@ -7,7 +7,7 @@
 
 
 TILE = 128
-NEAR = 16
+NEAR = 8
 
 
 def exchange(blocks, axis, groups=None):
@@ -157,9 +157,8 @@
     )(got, basis, snapshots, onward)
     coeff = jnp.zeros((size, width * sections), jnp.float32)
     coeff = lax.dynamic_update_slice(coeff, here, (jnp.int32(0), position * width))
-    blocks = exchange(first.reshape(lines, -1, TILE), "row")
-    mine, coeff = lax.optimization_barrier((blocks.sum(axis=0), coeff))
-    first = exchange(jnp.broadcast_to(mine, blocks.shape), "row")
+    blocks = exchange(first.reshape(len(near[0]), -1, TILE), "row", near)
+    first = gathered(blocks.sum(axis=0), near, far)
     first = lax.optimization_barrier(first)
     first, gram_next = lax.optimization_barrier((first, gram_next))
     there, vec, squares = local(

time: 127 us -> 113 us (0.89); the launches traced: 125 us -> 113 us
  blocking collectives: 56.5 us -> 49.4 us
  waiting for transfers between devices: 41.6 us -> 36.2 us
  local copies, waits for them, and re-layouts: 3.16 us -> 4.55 us
    all_to_all x3, blocking collectives: 56.5 us -> 49.4 us  [exchange(): lax.all_to_all(blocks, axis, split_axis=0, concat_axis=0, axis_index_grou...]
    all_to_all x3 -> x4, waiting for transfers between devices: 41.6 us -> 36.2 us  [exchange(): lax.all_to_all(blocks, axis, split_axis=0, concat_axis=0, axis_index_grou...]
    all_to_all x3 -> x4, starting transfers between devices: 16.9 us -> 16.2 us  [exchange(): lax.all_to_all(blocks, axis, split_axis=0, concat_axis=0, axis_index_grou...]
  transfers between devices with their start and end apart: 6 -> 7, of which waited for: 3 -> 4; matrix products, arithmetic and copies ran while one was open for 2% -> 3% of each run, Pallas kernels for 0% -> 0%
where the time goes in v10:
time: 113 us
  blocking collectives  49.4 us (44%)
  waiting for transfers between devices  36.2 us (32%)
  starting transfers between devices  16.2 us (14%)
  Pallas kernels  4.96 us (4%)
  local copies, waits for them, and re-layouts  4.55 us (4%)
    all_to_all x3, blocking collectives, exchange(): lax.all_to_all(blocks, axis, split_axis=0, concat_axis=0, axis_index_grou...  49.4 us
    all_to_all x4, waiting for transfers between devices, exchange(): lax.all_to_all(blocks, axis, split_axis=0, concat_axis=0, axis_index_grou...  36.2 us
    all_to_all x4, starting transfers between devices, exchange(): lax.all_to_all(blocks, axis, split_axis=0, concat_axis=0, axis_index_grou...  16.2 us
    pallas_call x1, Pallas kernels, per_device(): local(start_kernel, (hbm, hbm), [(pltpu.VMEM, (share + size, TILE))], (pl...  2.69 us
  transfers between devices with their start and end apart: 7, of which 4 were waited for; matrix products, arithmetic and copies ran while one was open for 3% of the time, Pallas kernels for 0%

profile of v10, /device:TPU:8, one launch (start us, length us, event | category | flops | bytes accessed | tf_op | source)
XLA Modules:
  0.0 112.8 jit_solution(7463568020487028853)
XLA Ops:
  0.6 0.0 copy-start
  0.6 2.7 %shard_map.49 = f32[1792,128]{1,0:T(8,128)} custom-call(f32[256,512]{1,0:T(8,128)} %basis_ref.1, f32[256,128]{1,0:T(8,128)} %vec_ref.1), custom_call_target="tpu_custom_call" | custom-call | tf_op jit(solution)/shard_map/pallas_call | solution.py:145
  3.3 5.7 %all-to-all-start = ((f32[8,224,128]{2,1,0:T(8,128)}), f32[8,224,128]{2,1,0:T(8,128)S(1)}, u32[]{:S(2)}, u32[]{:S(2)}) async-start(f32[8,224,128]{2,1,0:T(8,128)} %bitcast), calls=%async_computation | async-start | bytes 1835008 | tf_op jit(solution)/shard_map/all_to_all | solution.py:14
  9.0 0.0 copy-done
  9.0 0.0 collective-permute-start
  9.0 13.4 %all-to-all-done = f32[8,224,128]{2,1,0:T(8,128)S(1)} async-done(((f32[8,224,128]{2,1,0:T(8,128)}), f32[8,224,128]{2,1,0:T(8,128)S(1)}, u32[]{:S(2)}, u32[]{:S(2)}) %all-to-all-start) | async-done | bytes 917536 | tf_op jit(solution)/shard_map/all_to_all | solution.py:14
  22.4 0.0 collective-permute-done.next_ref.basis_ref
  22.5 0.0 copy-start.1
  22.5 23.0 %all_to_all.35 = f32[4,224,128]{2,1,0:T(8,128)S(1)} all-to-all(f32[4,224,128]{2,1,0:T(8,128)S(1)} %broadcast_in_dim.15), channel_id=1, replica_groups={{0,8,16,24},{1,9,17,25},{2,10,18,26},{3,11,19,27},{4,12,20,28},{5,13,21..., dimensions={0} | all-to-all | bytes 917504 | tf_op jit(solution)/shard_map/all_to_all | solution.py:14
  45.6 0.1 broadcast_in_dim.16
  45.6 16.7 %all_to_all.36 = f32[8,224,128]{2,1,0:T(8,128)S(1)} all-to-all(f32[8,224,128]{2,1,0:T(8,128)S(1)} %broadcast_in_dim.16), channel_id=1, replica_groups={{0,1,2,3,4,5,6,7},{8,9,10,11,12,13,14,15},{16,17,18,19,20,21,22,23},{24..., dimensions={0} | all-to-all | bytes 1835008 | tf_op jit(solution)/shard_map/all_to_all | solution.py:14
  62.3 0.0 copy-done.1
  62.3 0.9 shard_map.50
  63.3 9.7 %all_to_all.37 = f32[8,64,128]{2,1,0:T(8,128)S(1)} all-to-all(f32[8,64,128]{2,1,0:T(8,128)S(1)} %bitcast.7), channel_id=1, replica_groups={{0,1,2,3,4,5,6,7},{8,9,10,11,12,13,14,15},{16,17,18,19,20,21,22,23},{24..., dimensions={0} | all-to-all | bytes 524288 | tf_op jit(solution)/shard_map/all_to_all | solution.py:14
  73.0 0.7 broadcast_in_dim.17
  73.7 3.3 %all-to-all-start.4 = ((f32[4,64,128]{2,1,0:T(8,128)}), f32[4,64,128]{2,1,0:T(8,128)S(1)}, u32[]{:S(2)}, u32[]{:S(2)}) async-start(f32[4,64,128]{2,1,0:T(8,128)} %broadcast_in_dim.17), calls=%async_computation.4 | async-start | bytes 262144 | tf_op jit(solution)/shard_map/all_to_all | solution.py:14
  77.0 0.0 collective-permute-start.1
  77.1 8.3 %all-to-all-done.4 = f32[4,64,128]{2,1,0:T(8,128)S(1)} async-done(((f32[4,64,128]{2,1,0:T(8,128)}), f32[4,64,128]{2,1,0:T(8,128)S(1)}, u32[]{:S(2)}, u32[]{:S(2)}) %all-to-all-start.4) | async-done | bytes 131104 | tf_op jit(solution)/shard_map/all_to_all | solution.py:14
  85.4 0.7 broadcast_in_dim.18
  86.1 3.4 %all-to-all-start.5 = ((f32[8,64,128]{2,1,0:T(8,128)}), f32[8,64,128]{2,1,0:T(8,128)S(1)}, u32[]{:S(2)}, u32[]{:S(2)}) async-start(f32[8,64,128]{2,1,0:T(8,128)} %broadcast_in_dim.18), calls=%async_computation.5 | async-start | bytes 524288 | tf_op jit(solution)/shard_map/all_to_all | solution.py:14
  89.5 7.1 %all-to-all-done.5 = f32[8,64,128]{2,1,0:T(8,128)S(1)} async-done(((f32[8,64,128]{2,1,0:T(8,128)}), f32[8,64,128]{2,1,0:T(8,128)S(1)}, u32[]{:S(2)}, u32[]{:S(2)}) %all-to-all-start.5) | async-done | bytes 262176 | tf_op jit(solution)/shard_map/all_to_all | solution.py:14
  96.7 0.0 collective-permute-done.1.gram_ref
  96.7 1.3 %shard_map.51 = (f32[512,128]{1,0:T(8,128)S(1)}, f32[256,128]{1,0:T(8,128)}, f32[32,1,128]{2,1,0:T(1,128)}) custom-call(f32[512,128]{1,0:T(8,128)S(1)} %bitcast.6, f32[1280,128]{1,0:T(8,128)S(1)} %collective-permute-done.1.gram_ref, f32[256,512]{1,0:T(8,128)S(1)} %collective-permute-done.next_ref.basis_ref, f32[256,128]{1,0:T(8,128)S(1)} %get-tuple-element.18.vec_ref), custom_call_target="tpu_custom_call" | custom-call | tf_op jit(solution)/shard_map/pallas_call | solution.py:164
  98.0 3.8 %all-to-all-start.6 = ((f32[32,1,128]{2,1,0:T(1,128)}), f32[32,1,128]{2,1,0:T(1,128)S(1)}, u32[]{:S(2)}, u32[]{:S(2)}) async-start(f32[32,1,128]{2,1,0:T(1,128)} %get-tuple-element.22), calls=%async_computation.6 | async-start | bytes 32768 | tf_op jit(solution)/shard_map/all_to_all | solution.py:14
  101.8 0.0 collective-permute-start.2
  101.8 1.6 %broadcast_in_dim.19 = f32[512,1024]{1,0:T(8,128)} broadcast(f32[]{:T(128)} %constant.11.clone.1), dimensions={} | broadcast | bytes 2097156 | tf_op jit(solution)/shard_map/broadcast_in_dim | solution.py:158
  103.4 0.7 constant_dynamic-update-slice_fusion.1
  104.1 7.4 %all-to-all-done.6 = f32[32,1,128]{2,1,0:T(1,128)S(1)} async-done(((f32[32,1,128]{2,1,0:T(1,128)}), f32[32,1,128]{2,1,0:T(1,128)S(1)}, u32[]{:S(2)}, u32[]{:S(2)}) %all-to-all-start.6) | async-done | bytes 16416 | tf_op jit(solution)/shard_map/all_to_all | solution.py:14
  111.5 0.1 reduce_sum.49
  111.6 0.5 multiply_sqrt_fusion
  112.1 0.0 collective-permute-done.2
  112.1 0.7 constant_dynamic-update-slice_fusion
  (6 shorter events, 0.2 us)
Async XLA Ops:
  0.6 8.4 %copy-start = (f32[256,512]{1,0:T(8,128)S(1)}, f32[256,512]{1,0:T(8,128)}, u32[]{:S(2)}) copy-start(f32[256,512]{1,0:T(8,128)} %basis_ref.1) | copy-start | bytes 1572868
  3.3 19.1 %all-to-all-start = ((f32[8,224,128]{2,1,0:T(8,128)}), f32[8,224,128]{2,1,0:T(8,128)S(1)}, u32[]{:S(2)}, u32[]{:S(2)}) async-start(f32[8,224,128]{2,1,0:T(8,128)} %bitcast), calls=%async_computation | async-start | bytes 1835008 | tf_op jit(solution)/shard_map/all_to_all | solution.py:14
  9.0 13.4 %collective-permute-start = (f32[256,512]{1,0:T(8,128)S(1)}, f32[256,512]{1,0:T(8,128)S(1)}, u32[]{:S(2)}, u32[]{:S(2)}) collective-permute-start(f32[256,512]{1,0:T(8,128)S(1)} %copy-done), channel_id=1, source_target_pairs={{0,224},{32,0},{64,32},{96,64},{128,96},{160,128},{192,160},{224,1... | collective-permute-start | bytes 1572872 | tf_op jit(solution)/shard_map/ppermute | solution.py:36
  22.5 39.8 %copy-start.1 = (f32[256,128]{1,0:T(8,128)S(1)}, f32[256,128]{1,0:T(8,128)}, u32[]{:S(2)}) copy-start(f32[256,128]{1,0:T(8,128)} %vec_ref.1) | copy-start | bytes 393220
  73.7 11.7 %all-to-all-start.4 = ((f32[4,64,128]{2,1,0:T(8,128)}), f32[4,64,128]{2,1,0:T(8,128)S(1)}, u32[]{:S(2)}, u32[]{:S(2)}) async-start(f32[4,64,128]{2,1,0:T(8,128)} %broadcast_in_dim.17), calls=%async_computation.4 | async-start | bytes 262144 | tf_op jit(solution)/shard_map/all_to_all | solution.py:14
  77.0 19.6 %collective-permute-start.1 = (f32[1280,128]{1,0:T(8,128)S(1)}, f32[1280,128]{1,0:T(8,128)S(1)}, u32[]{:S(2)}, u32[]{:S(2)}) collective-permute-start(f32[1280,128]{1,0:T(8,128)S(1)} %slice.4), channel_id=1, source_target_pairs={{0,224},{32,0},{64,32},{96,64},{128,96},{160,128},{192,160},{224,1... | collective-permute-start | bytes 1966088 | tf_op jit(solution)/shard_map/ppermute | solution.py:36
  86.1 10.6 %all-to-all-start.5 = ((f32[8,64,128]{2,1,0:T(8,128)}), f32[8,64,128]{2,1,0:T(8,128)S(1)}, u32[]{:S(2)}, u32[]{:S(2)}) async-start(f32[8,64,128]{2,1,0:T(8,128)} %broadcast_in_dim.18), calls=%async_computation.5 | async-start | bytes 524288 | tf_op jit(solution)/shard_map/all_to_all | solution.py:14
  98.0 13.5 %all-to-all-start.6 = ((f32[32,1,128]{2,1,0:T(1,128)}), f32[32,1,128]{2,1,0:T(1,128)S(1)}, u32[]{:S(2)}, u32[]{:S(2)}) async-start(f32[32,1,128]{2,1,0:T(1,128)} %get-tuple-element.22), calls=%async_computation.6 | async-start | bytes 32768 | tf_op jit(solution)/shard_map/all_to_all | solution.py:14
  101.8 10.3 %collective-permute-start.2 = (f32[512,128]{1,0:T(8,128)S(1)}, f32[512,128]{1,0:T(8,128)S(1)}, u32[]{:S(2)}, u32[]{:S(2)}) collective-permute-start(f32[512,128]{1,0:T(8,128)S(1)} %get-tuple-element.21), channel_id=1, source_target_pairs={{0,32},{32,64},{64,96},{96,128},{128,160},{160,192},{192,224},{224... | collective-permute-start | bytes 786440 | tf_op jit(solution)/shard_map/ppermute | solution.py:36

commit v11 on v10

--- a/solution.py
+++ b/solution.py
@@ -155,10 +155,14 @@
         turn_kernel, (pltpu.VMEM,) * 4,
         [(pltpu.VMEM, (size, width)), (pltpu.VMEM, (rows, width)), (pltpu.VMEM, (size, width))],
     )(got, basis, snapshots, onward)
-    coeff = jnp.zeros((size, width * sections), jnp.float32)
-    coeff = lax.dynamic_update_slice(coeff, here, (jnp.int32(0), position * width))
     blocks = exchange(first.reshape(len(near[0]), -1, TILE), "row", near)
-    first = gathered(blocks.sum(axis=0), near, far)
+    mine = blocks.sum(axis=0)
+    blocks = exchange(jnp.broadcast_to(mine, (len(far[0]), *mine.shape)), "row", far)
+    before = (position - 1) % sections
+    own, at, behind = lax.optimization_barrier(
+        (blocks.sum(axis=0), position * width, before * width)
+    )
+    first = exchange(jnp.broadcast_to(own, (len(near[0]), *own.shape)), "row", near)
     first = lax.optimization_barrier(first)
     first, gram_next = lax.optimization_barrier((first, gram_next))
     there, vec, squares = local(
@@ -169,8 +173,9 @@
 
     arrived = shifted(there, "segment", 1)
     blocks = exchange(squares, "row")
-    before = (position - 1) % sections
-    coeff = lax.dynamic_update_slice(coeff, arrived, (jnp.int32(0), before * width))
+    coeff = jnp.zeros((size, width * sections), jnp.float32)
+    coeff = lax.dynamic_update_slice(coeff, here, (jnp.int32(0), at))
+    coeff = lax.dynamic_update_slice(coeff, arrived, (jnp.int32(0), behind))
     rms = jnp.sqrt(blocks.sum(axis=(0, 1)) / total_rows)
     return (vec, coeff, rms)
 

time: 113 us -> 115 us (1.018); the launches traced: 113 us -> 113 us
  blocking collectives: 49.4 us -> 59.6 us
  waiting for transfers between devices: 36.2 us -> 27.9 us
  starting transfers between devices: 16.2 us -> 12.9 us
  local copies, waits for them, and re-layouts: 4.55 us -> 5.96 us
    all_to_all x3 -> x4, blocking collectives: 49.4 us -> 59.6 us  [exchange(): lax.all_to_all(blocks, axis, split_axis=0, concat_axis=0, axis_index_grou...]
    all_to_all x4 -> x3, waiting for transfers between devices: 36.2 us -> 27.9 us  [exchange(): lax.all_to_all(blocks, axis, split_axis=0, concat_axis=0, axis_index_grou...]
    all_to_all x4 -> x3, starting transfers between devices: 16.2 us -> 12.8 us  [exchange(): lax.all_to_all(blocks, axis, split_axis=0, concat_axis=0, axis_index_grou...]
    dynamic_update_slice x2, local copies, waits for them, and re-layouts: 1.44 us -> 3.55 us  [the longest x1 1.78 us: per_device(): coeff = lax.dynamic_update_slice(coeff, arrived, (jnp.int32(0), behind))]
  transfers between devices with their start and end apart: 7 -> 6, of which waited for: 4 -> 3; matrix products, arithmetic and copies ran while one was open for 3% -> 4% of each run, Pallas kernels for 0% -> 0%
where the time goes in v11:
time: 115 us; the launch traced here: 113 us
  blocking collectives  59.6 us (52%)
  waiting for transfers between devices  27.9 us (24%)
  starting transfers between devices  12.9 us (11%)
  local copies, waits for them, and re-layouts  5.96 us (5%)
  Pallas kernels  4.96 us (4%)
    all_to_all x4, blocking collectives, exchange(): lax.all_to_all(blocks, axis, split_axis=0, concat_axis=0, axis_index_grou...  59.6 us
    all_to_all x3, waiting for transfers between devices, exchange(): lax.all_to_all(blocks, axis, split_axis=0, concat_axis=0, axis_index_grou...  27.9 us
    all_to_all x3, starting transfers between devices, exchange(): lax.all_to_all(blocks, axis, split_axis=0, concat_axis=0, axis_index_grou...  12.8 us
    pallas_call x1, Pallas kernels, per_device(): local(start_kernel, (hbm, hbm), [(pltpu.VMEM, (share + size, TILE))], (pl...  2.69 us
  transfers between devices with their start and end apart: 6, of which 3 were waited for; matrix products, arithmetic and copies ran while one was open for 4% of the time, Pallas kernels for 0%

profile of v11, /device:TPU:8, one launch (start us, length us, event | category | flops | bytes accessed | tf_op | source)
XLA Modules:
  0.0 112.7 jit_solution(9071780899804198821)
XLA Ops:
  0.6 0.0 copy-start
  0.6 2.7 %shard_map.49 = f32[1792,128]{1,0:T(8,128)} custom-call(f32[256,512]{1,0:T(8,128)} %basis_ref.1, f32[256,128]{1,0:T(8,128)} %vec_ref.1), custom_call_target="tpu_custom_call" | custom-call | tf_op jit(solution)/shard_map/pallas_call | solution.py:145
  3.3 5.7 %all-to-all-start = ((f32[8,224,128]{2,1,0:T(8,128)}), f32[8,224,128]{2,1,0:T(8,128)S(1)}, u32[]{:S(2)}, u32[]{:S(2)}) async-start(f32[8,224,128]{2,1,0:T(8,128)} %bitcast), calls=%async_computation | async-start | bytes 1835008 | tf_op jit(solution)/shard_map/all_to_all | solution.py:14
  9.0 0.0 copy-done
  9.0 0.0 collective-permute-start
  9.0 13.4 %all-to-all-done = f32[8,224,128]{2,1,0:T(8,128)S(1)} async-done(((f32[8,224,128]{2,1,0:T(8,128)}), f32[8,224,128]{2,1,0:T(8,128)S(1)}, u32[]{:S(2)}, u32[]{:S(2)}) %all-to-all-start) | async-done | bytes 917536 | tf_op jit(solution)/shard_map/all_to_all | solution.py:14
  22.4 0.0 collective-permute-done.next_ref.basis_ref
  22.5 0.0 copy-start.1
  22.5 23.0 %all_to_all.35 = f32[4,224,128]{2,1,0:T(8,128)S(1)} all-to-all(f32[4,224,128]{2,1,0:T(8,128)S(1)} %broadcast_in_dim.15), channel_id=1, replica_groups={{0,8,16,24},{1,9,17,25},{2,10,18,26},{3,11,19,27},{4,12,20,28},{5,13,21..., dimensions={0} | all-to-all | bytes 917504 | tf_op jit(solution)/shard_map/all_to_all | solution.py:14
  45.6 0.1 broadcast_in_dim.16
  45.6 16.7 %all_to_all.36 = f32[8,224,128]{2,1,0:T(8,128)S(1)} all-to-all(f32[8,224,128]{2,1,0:T(8,128)S(1)} %broadcast_in_dim.16), channel_id=1, replica_groups={{0,1,2,3,4,5,6,7},{8,9,10,11,12,13,14,15},{16,17,18,19,20,21,22,23},{24..., dimensions={0} | all-to-all | bytes 1835008 | tf_op jit(solution)/shard_map/all_to_all | solution.py:14
  62.3 0.0 copy-done.1
  62.3 0.9 shard_map.50
  63.3 9.7 %all_to_all.37 = f32[8,64,128]{2,1,0:T(8,128)S(1)} all-to-all(f32[8,64,128]{2,1,0:T(8,128)S(1)} %bitcast.7), channel_id=1, replica_groups={{0,1,2,3,4,5,6,7},{8,9,10,11,12,13,14,15},{16,17,18,19,20,21,22,23},{24..., dimensions={0} | all-to-all | bytes 524288 | tf_op jit(solution)/shard_map/all_to_all | solution.py:14
  73.0 0.7 broadcast_in_dim.17
  73.7 3.3 %all-to-all-start.4 = ((f32[4,64,128]{2,1,0:T(8,128)}), f32[4,64,128]{2,1,0:T(8,128)S(1)}, u32[]{:S(2)}, u32[]{:S(2)}) async-start(f32[4,64,128]{2,1,0:T(8,128)} %broadcast_in_dim.17), calls=%async_computation.4 | async-start | bytes 262144 | tf_op jit(solution)/shard_map/all_to_all | solution.py:14
  77.0 0.0 collective-permute-start.1
  77.1 8.3 %all-to-all-done.4 = f32[4,64,128]{2,1,0:T(8,128)S(1)} async-done(((f32[4,64,128]{2,1,0:T(8,128)}), f32[4,64,128]{2,1,0:T(8,128)S(1)}, u32[]{:S(2)}, u32[]{:S(2)}) %all-to-all-start.4) | async-done | bytes 131104 | tf_op jit(solution)/shard_map/all_to_all | solution.py:14
  85.4 10.2 %all_to_all.38 = f32[8,64,128]{2,1,0:T(8,128)S(1)} all-to-all(f32[8,64,128]{2,1,0:T(8,128)S(1)} %broadcast_in_dim.18), channel_id=1, replica_groups={{0,1,2,3,4,5,6,7},{8,9,10,11,12,13,14,15},{16,17,18,19,20,21,22,23},{24..., dimensions={0} | all-to-all | bytes 524288 | tf_op jit(solution)/shard_map/all_to_all | solution.py:14
  95.5 0.0 collective-permute-done.1.gram_ref
  95.5 1.3 %shard_map.51 = (f32[512,128]{1,0:T(8,128)S(1)}, f32[256,128]{1,0:T(8,128)}, f32[32,1,128]{2,1,0:T(1,128)}) custom-call(f32[512,128]{1,0:T(8,128)S(1)} %bitcast.6, f32[1280,128]{1,0:T(8,128)S(1)} %collective-permute-done.1.gram_ref, f32[256,512]{1,0:T(8,128)S(1)} %collective-permute-done.next_ref.basis_ref, f32[256,128]{1,0:T(8,128)S(1)} %get-tuple-element.22.vec_ref), custom_call_target="tpu_custom_call" | custom-call | tf_op jit(solution)/shard_map/pallas_call | solution.py:168
  96.9 0.0 collective-permute-start.2
  96.9 3.9 %all-to-all-start.6 = ((f32[32,1,128]{2,1,0:T(1,128)}), f32[32,1,128]{2,1,0:T(1,128)S(1)}, u32[]{:S(2)}, u32[]{:S(2)}) async-start(f32[32,1,128]{2,1,0:T(1,128)} %get-tuple-element.28), calls=%async_computation.6 | async-start | bytes 32768 | tf_op jit(solution)/shard_map/all_to_all | solution.py:14
  100.8 1.6 %broadcast_in_dim.19 = f32[512,1024]{1,0:T(8,128)} broadcast(f32[]{:T(128)} %constant.11.clone.1), dimensions={} | broadcast | bytes 2097156 | tf_op jit(solution)/shard_map/broadcast_in_dim | solution.py:176
  102.3 1.8 %dynamic_update_slice.6 = f32[512,1024]{1,0:T(8,128)} dynamic-update-slice(f32[512,1024]{1,0:T(8,128)} %broadcast_in_dim.19, f32[512,128]{1,0:T(8,128)S(1)} %get-tuple-element.24, s32[]{:T(128)} %constant.28.clone.1, s32[]{:T(128)S(6)} %select_n.14) | dynamic-update-slice | bytes 524292 | tf_op jit(solution)/shard_map/dynamic_update_slice | solution.py:177
  104.1 6.3 %all-to-all-done.6 = f32[32,1,128]{2,1,0:T(1,128)S(1)} async-done(((f32[32,1,128]{2,1,0:T(1,128)}), f32[32,1,128]{2,1,0:T(1,128)S(1)}, u32[]{:S(2)}, u32[]{:S(2)}) %all-to-all-start.6) | async-done | bytes 16416 | tf_op jit(solution)/shard_map/all_to_all | solution.py:14
  110.4 0.1 reduce_sum.49
  110.4 0.5 multiply_sqrt_fusion
  110.9 0.0 collective-permute-done.2
  110.9 1.8 %dynamic_update_slice.7 = f32[512,1024]{1,0:T(8,128)} dynamic-update-slice(f32[512,1024]{1,0:T(8,128)} %dynamic_update_slice.6, f32[512,128]{1,0:T(8,128)S(1)} %collective-permute-done.2, s32[]{:T(128)} %constant.28.clone.1, s32[]{:T(128)S(6)} %select_n.15) | dynamic-update-slice | bytes 524292 | tf_op jit(solution)/shard_map/dynamic_update_slice | solution.py:178
  (7 shorter events, 0.2 us)
Async XLA Ops:
  0.6 8.4 %copy-start = (f32[256,512]{1,0:T(8,128)S(1)}, f32[256,512]{1,0:T(8,128)}, u32[]{:S(2)}) copy-start(f32[256,512]{1,0:T(8,128)} %basis_ref.1) | copy-start | bytes 1572868
  3.3 19.1 %all-to-all-start = ((f32[8,224,128]{2,1,0:T(8,128)}), f32[8,224,128]{2,1,0:T(8,128)S(1)}, u32[]{:S(2)}, u32[]{:S(2)}) async-start(f32[8,224,128]{2,1,0:T(8,128)} %bitcast), calls=%async_computation | async-start | bytes 1835008 | tf_op jit(solution)/shard_map/all_to_all | solution.py:14
  9.0 13.4 %collective-permute-start = (f32[256,512]{1,0:T(8,128)S(1)}, f32[256,512]{1,0:T(8,128)S(1)}, u32[]{:S(2)}, u32[]{:S(2)}) collective-permute-start(f32[256,512]{1,0:T(8,128)S(1)} %copy-done), channel_id=1, source_target_pairs={{0,224},{32,0},{64,32},{96,64},{128,96},{160,128},{192,160},{224,1... | collective-permute-start | bytes 1572872 | tf_op jit(solution)/shard_map/ppermute | solution.py:36
  22.5 39.8 %copy-start.1 = (f32[256,128]{1,0:T(8,128)S(1)}, f32[256,128]{1,0:T(8,128)}, u32[]{:S(2)}) copy-start(f32[256,128]{1,0:T(8,128)} %vec_ref.1) | copy-start | bytes 393220
  73.7 11.7 %all-to-all-start.4 = ((f32[4,64,128]{2,1,0:T(8,128)}), f32[4,64,128]{2,1,0:T(8,128)S(1)}, u32[]{:S(2)}, u32[]{:S(2)}) async-start(f32[4,64,128]{2,1,0:T(8,128)} %broadcast_in_dim.17), calls=%async_computation.4 | async-start | bytes 262144 | tf_op jit(solution)/shard_map/all_to_all | solution.py:14
  77.0 18.5 %collective-permute-start.1 = (f32[1280,128]{1,0:T(8,128)S(1)}, f32[1280,128]{1,0:T(8,128)S(1)}, u32[]{:S(2)}, u32[]{:S(2)}) collective-permute-start(f32[1280,128]{1,0:T(8,128)S(1)} %slice.4), channel_id=1, source_target_pairs={{0,224},{32,0},{64,32},{96,64},{128,96},{160,128},{192,160},{224,1... | collective-permute-start | bytes 1966088 | tf_op jit(solution)/shard_map/ppermute | solution.py:36
  96.9 14.1 %collective-permute-start.2 = (f32[512,128]{1,0:T(8,128)S(1)}, f32[512,128]{1,0:T(8,128)S(1)}, u32[]{:S(2)}, u32[]{:S(2)}) collective-permute-start(f32[512,128]{1,0:T(8,128)S(1)} %get-tuple-element.26), channel_id=1, source_target_pairs={{0,32},{32,64},{64,96},{96,128},{128,160},{160,192},{192,224},{224... | collective-permute-start | bytes 786440 | tf_op jit(solution)/shard_map/ppermute | solution.py:36
  96.9 13.5 %all-to-all-start.6 = ((f32[32,1,128]{2,1,0:T(1,128)}), f32[32,1,128]{2,1,0:T(1,128)S(1)}, u32[]{:S(2)}, u32[]{:S(2)}) async-start(f32[32,1,128]{2,1,0:T(1,128)} %get-tuple-element.28), calls=%async_computation.6 | async-start | bytes 32768 | tf_op jit(solution)/shard_map/all_to_all | solution.py:14
